TPU v7x, 512 devices: a 8x2x16 block of a 8x8x16 slice. The times are simulated.
512 devices in a mesh: groups: 2 (over y), ctx: 32 (over z, core), tp: 8 (over x).
Axes of the slice: x: 8, y: 2, z: 16, core: 2. Of those that a mesh axis runs over, the one named last changes fastest.
The devices are a block of a 8x8x16 slice.
Arguments:
- q_nope: bfloat16 [4096, 16384], P(('groups', 'ctx'), 'tp'), parts along dimension 0, may hold values from -6 to 6
- q_rope: bfloat16 [4096, 8192], P(('groups', 'ctx'), 'tp'), parts along dimension 0, may hold values from -6 to 6
- c_kv: bfloat16 [4096, 512], P(('groups', 'ctx')), parts along dimension 0, may hold values from -6 to 46.4
- k_rope: bfloat16 [4096, 64], P(('groups', 'ctx')), parts along dimension 0, may hold values from -6 to 6
- positions: int32 [4096], P(('groups', 'ctx')), parts along dimension 0, may hold values from 0 to 2047, as said below
- w_uk: bfloat16 [128, 128, 512], P('tp', 'ctx'), may hold values from -0.5 to 0.5
- w_uv: bfloat16 [128, 512, 128], P('tp', 'ctx'), may hold values from -0.25 to 0.25
- w_out: bfloat16 [16384, 7168], P('tp', 'ctx'), may hold values from -0.125 to 0.125
Outputs:
- attn_proj: bfloat16 [4096, 7168], P(('groups', 'tp'), 'ctx'), parts along dimension 0
There are 2 independent parts, one for each index of `groups`. A program takes and returns all parts, laid end to end along the dimension named above; an argument that names none is the same for every part. Nothing has to cross between parts.
Inputs may be any that keep to these rules, and one draw needn't show every extreme that they name: The positions are the 2048 integers 0 to 2047, each once; every aligned block of 32 rows holds consecutive ascending positions.
All inputs are finite; a program needn't handle non-finite values.
Results may differ from a plain program's by a relative error of at most 0.015.
Values may be sent and summed in bfloat16 or wider, within the bound.
No kernel may reach another device: no remote copies, remote signals or barrier semaphores. Data moves between devices by JAX's collectives and lax.ppermute only.
A program may use at most 64 MiB of HBM per device.

v0:
```python
import jax
import jax.numpy as jnp
from jax import lax
from jax.sharding import PartitionSpec as P


def laid_out(blocks, dim):
    blocks = jnp.moveaxis(blocks, 0, dim)
    lengths = blocks.shape
    return blocks.reshape(*lengths[:dim], lengths[dim] * lengths[dim + 1], *lengths[dim + 2 :])


def gather_together(arrays, axis, dims):
    flat = jnp.concatenate([a.reshape(-1) for a in arrays])
    lines, at, gathered = (lax.all_gather(flat, axis), 0, [])
    for a, dim in zip(arrays, dims):
        blocks = lines[:, at : at + a.size].reshape(-1, *a.shape)
        gathered.append(laid_out(blocks, dim))
        at += a.size
    return tuple(gathered)


def in_blocks(x, dim, size):
    before, after = (x.shape[:dim], x.shape[dim + 1 :])
    return jnp.moveaxis(x.reshape(*before, size, -1, *after), dim, 0)


def sent_and_summed(x, axis, dim):
    blocks = in_blocks(x, dim, lax.axis_size(axis))
    arrived = lax.all_to_all(blocks, axis, split_axis=0, concat_axis=0, tiled=True)
    return arrived.astype(jnp.float32).sum(axis=0)


def rotate(values, position):
    half_dim = values.shape[-1] // 2
    freqs = 10000.0 ** (-jnp.arange(half_dim, dtype=jnp.float32) / half_dim)
    angles = position.astype(jnp.float32)[..., None] * freqs
    cosine = jnp.cos(angles)
    sine = jnp.sin(angles)
    first_half = values[..., :half_dim].astype(jnp.float32)
    second_half = values[..., half_dim:].astype(jnp.float32)
    return jnp.concatenate(
        [first_half * cosine - second_half * sine, second_half * cosine + first_half * sine],
        axis=-1,
    )


def on_device(q_nope, q_rope, c_kv, k_rope, positions, w_uk, w_uv, w_out):
    tok_count = q_nope.shape[0]
    head_count = w_uk.shape[0]
    latent = c_kv.shape[1]
    up_key, up_value = gather_together((w_uk, w_uv), "ctx", (1, 1))
    nope_dim = up_key.shape[1]
    rope_dim = k_rope.shape[1]
    softmax_scale = (nope_dim + rope_dim) ** (-0.5)
    q_parts = q_nope.reshape(tok_count, head_count, nope_dim)
    q_lat = jnp.einsum("thn,hnl->thl", q_parts, up_key, preferred_element_type=jnp.float32).astype(
        jnp.bfloat16
    )
    q_rot = rotate(q_rope.reshape(tok_count, head_count, rope_dim), positions[:, None]).astype(
        jnp.bfloat16
    )
    k_rot = rotate(k_rope, positions).astype(jnp.bfloat16)
    key_rows = jnp.concatenate([c_kv, k_rot], axis=1)
    queries = jnp.concatenate([q_lat, q_rot], axis=2).reshape(
        tok_count * head_count, latent + rope_dim
    )
    query_pos = jnp.repeat(positions, head_count)
    row_total = tok_count * head_count
    key_part = lax.all_gather(key_rows, "ctx", axis=0, tiled=True)
    key_pos = lax.all_gather(positions, "ctx", axis=0, tiled=True)
    run_max = jnp.full((row_total,), -1e30, jnp.float32)
    scores = (
        jnp.einsum("rk,sk->rs", queries, key_part, preferred_element_type=jnp.float32)
        * softmax_scale
    )
    visible = key_pos[None, :] <= query_pos[:, None]
    new_max = jnp.maximum(run_max, jnp.max(jnp.where(visible, scores, -1e30), axis=1))
    weights = jnp.where(visible, jnp.exp(scores - new_max[:, None]), 0.0)
    new_sum = jnp.sum(weights, axis=1)
    added = jnp.dot(
        weights.astype(jnp.bfloat16), key_part[:, :latent], preferred_element_type=jnp.float32
    )
    o_lat = (added / new_sum[:, None]).astype(jnp.bfloat16).reshape(tok_count, head_count, latent)
    head_out = jnp.einsum("thl,hlv->thv", o_lat, up_value, preferred_element_type=jnp.float32)
    rows_out = head_out.astype(jnp.bfloat16).reshape(tok_count, -1)
    partial_value = jnp.dot(
        lax.all_gather(rows_out, "ctx", axis=0, tiled=True),
        w_out,
        preferred_element_type=jnp.float32,
    )
    summed = sent_and_summed(partial_value.astype(jnp.bfloat16), "tp", 0)
    return summed.astype(jnp.bfloat16)


def solution(mesh):
    in_specs = (
        P(("groups", "ctx"), "tp"),
        P(("groups", "ctx"), "tp"),
        P(("groups", "ctx"), None),
        P(("groups", "ctx"), None),
        P(("groups", "ctx")),
        P("tp", "ctx", None),
        P("tp", "ctx", None),
        P("tp", "ctx"),
    )
    out_specs = P(("groups", "tp"), "ctx")
    return jax.shard_map(
        on_device, mesh=mesh, in_specs=in_specs, out_specs=out_specs, check_vma=False
    )
```

profile of v0, /device:TPU:65, one launch (start us, length us, event | category | flops | bytes accessed | tf_op | source)
XLA Modules:
  0.0 328.4 jit_solution(10513221402875094891)
XLA Ops:
  6.5 0.0 copy-start
  6.6 0.0 all-gather.9.cloned.1.call-start
  6.6 0.9 copy.33
  7.5 1.5 pad_maximum_fusion.1
  9.0 0.1 all-gather.9.cloned.1.call-update
  9.0 0.1 all-gather.5.cloned.1.call-start
  9.1 0.7 convert_element_type.45
  9.8 1.0 fusion.20
  10.8 1.6 pad_maximum_fusion.2
  12.3 0.1 all-gather.5.cloned.1.call-update
  12.4 0.1 all-gather.7.cloned.1.call-start
  12.5 1.3 dynamic-slice
  14.5 0.9 dynamic-update-slice
  15.4 57.5 %all-reduce = s32[2048]{0:T(1024)S(1)} all-reduce(s32[2048]{0:T(1024)S(1)} %dynamic-update-slice), channel_id=1, replica_groups=mesh['groups'=2,'ctx'=32,'tp'=8] {'ctx'}, use_global_device_ids=true, to_apply=%add | all-reduce | flops 2048 | bytes 16384
  72.9 0.7 broadcast_in_dim.11
  73.6 0.1 le.16
  73.7 1.1 reshape.118
  74.8 0.1 fusion.26
  75.0 0.2 fusion.14
  75.2 45.3 %all-gather.9.cloned.1.call-done = bf16[2097152]{0:T(1024)(128)(2,1)} async-done(((bf16[65536]{0:T(1024)(128)(2,1)}), bf16[2097152]{0:T(1024)(128)(2,1)}) %all-gather.9.cloned.1.call-update) | async-done | bytes 4194320 | tf_op jit(solution)/shard_map/all_gather | solution.py:15
  120.4 5.6 %reshape.123 = bf16[32,65536]{1,0:T(8,128)(2,1)} reshape(bf16[2097152]{0:T(1024)(128)(2,1)} %all-gather.9.cloned.1.call-done) | data formatting | bytes 8388608 | tf_op jit(solution)/shard_map/all_gather | solution.py:15
  126.0 4.4 %fusion.25 = (bf16[32,32768]{1,0:T(8,128)(2,1)}, bf16[4,8,256,128]{3,1,2,0:T(8,128)(2,1)}) fusion(bf16[32,65536]{1,0:T(8,128)(2,1)} %reshape.123), kind=kLoop, calls=%fused_computation.44 | loop fusion | bytes 8388608 | tf_op jit(solution)/shard_map/slice | solution.py:17
  130.4 3.3 %reshape.115 = bf16[32,16,4,512]{3,2,1,0:T(4,128)(2,1)S(1)} reshape(bf16[32,32768]{1,0:T(8,128)(2,1)} %get-tuple-element.5) | data formatting | bytes 4194304 | tf_op jit(solution)/shard_map/reshape | solution.py:17
  133.8 2.3 copy.20
  136.1 2.5 reshape.116
  138.6 1.4 fusion.6
  140.0 0.0 copy-start.1
  140.0 0.2 pad_maximum_fusion
  140.3 1.8 copy.24
  142.1 0.0 copy-done.1
  142.1 0.5 copy.34
  142.6 0.5 copy.19
  143.1 49.6 %all-gather.5.cloned.1.call-done = bf16[2048,576]{1,0:T(8,128)(2,1)} async-done(((bf16[64,576]{1,0:T(8,128)(2,1)}), bf16[2048,576]{1,0:T(8,128)(2,1)}) %all-gather.5.cloned.1.call-update) | async-done | bytes 2359312 | tf_op jit(solution)/shard_map/all_gather | solution.py:70
  192.8 5.9 %fusion = (f32[1024]{0:T(1024)S(1)}, f32[1024,2048]{1,0:T(8,128)S(1)}) fusion(s32[2048]{0:T(1024)S(1)} %all-reduce, s32[1024]{0:T(1024)S(1)} %le.16, bf16[1024,576]{1,0:T(8,128)(2,1)} %bitcast.43, bf16[2048,576]{1,0:T(8,128)(2,1)} %all-gather.5.cloned.1.call-done), kind=kOutput, calls=%fused_computation.2 | convolution fusion | flops 2424306688 | bytes 11943936 | tf_op jit(solution)/shard_map/rk,sk->rs/dot_general | solution.py:74
  198.7 0.0 copy-start.2
  198.7 2.8 fusion.1
  201.5 0.0 copy-done.2
  201.5 2.5 divide_convert_fusion
  204.0 1.4 fusion.7
  205.4 0.8 copy.48
  206.2 0.1 all-gather.7.cloned.1.call-update
  206.3 77.1 %all-gather.7.cloned.1.call-done = bf16[2048,2048]{1,0:T(8,128)(2,1)} async-done(((bf16[64,2048]{1,0:T(8,128)(2,1)}), bf16[2048,2048]{1,0:T(8,128)(2,1)}) %all-gather.7.cloned.1.call-update) | async-done | bytes 8388624 | tf_op jit(solution)/shard_map/all_gather | solution.py:88
  283.4 0.0 copy-done
  283.4 6.0 %convolution_convert_fusion = bf16[2048,224]{0,1:T(8,128)(2,1)S(1)} fusion(bf16[2048,2048]{1,0:T(8,128)(2,1)} %all-gather.7.cloned.1.call-done, bf16[2048,224]{0,1:T(8,128)(2,1)S(1)} %copy-done), kind=kOutput, calls=%fused_computation.6 | convolution fusion | flops 1879506944 | bytes 10223616 | tf_op jit(solution)/shard_map/dot_general | solution.py:87
  289.4 0.1 copy.47
  289.5 31.6 %all_to_all.5 = bf16[8,256,224]{1,2,0:T(8,128)(2,1)S(1)} all-to-all(bf16[8,256,224]{1,2,0:T(8,128)(2,1)S(1)} %bitcast.42), channel_id=1, replica_groups=mesh['groups'=2,'ctx'=32,'tp'=8] {'tp'}, dimensions={0} | all-to-all | bytes 1835008 | tf_op jit(solution)/shard_map/all_to_all | solution.py:30
  321.1 0.8 reduce_sum.22
  (3 shorter events, 0.0 us)
Async XLA Ops:
  6.5 276.9 %copy-start = (bf16[2048,224]{0,1:T(8,128)(2,1)S(1)}, bf16[2048,224]{0,1:T(8,128)(2,1)}, u32[]{:S(2)}) copy-start(bf16[2048,224]{0,1:T(8,128)(2,1)} %param.15) | copy-start | bytes 2752516
  6.6 113.9 %all-gather.9.cloned.1.call-start = ((), (), s32[]{:S(2)}) async-start(), calls=%async_computation.3 | async-start | bytes 4325376 | tf_op jit(solution)/shard_map/all_gather | solution.py:15
  9.0 183.7 %all-gather.5.cloned.1.call-start = ((), (), s32[]{:S(2)}) async-start(), calls=%async_computation.1 | async-start | bytes 2703360 | tf_op jit(solution)/shard_map/all_gather | solution.py:70
  12.4 271.0 %all-gather.7.cloned.1.call-start = ((), (), s32[]{:S(2)}) async-start(), calls=%async_computation.2 | async-start | bytes 8650752 | tf_op jit(solution)/shard_map/all_gather | solution.py:88
  140.0 2.1 copy-start.1
  198.7 2.8 copy-start.2
Sparse Core Ops, SparseCore 0:
  9.5 110.9 all-gather.8
  122.6 70.1 all-gather.4
  206.4 76.9 all-gather.6
where the time goes:
time: 329 us; the launch traced here: 328 us
  waiting for transfers between devices  172 us (52%)
  blocking collectives  89.1 us (27%)
  local copies, waits for them, and re-layouts  27.1 us (8%)
  matrix products  17.2 us (5%)
  between operations  14 us (4%)
  other arithmetic  8.72 us (3%)
    all_gather x1, waiting for transfers between devices, on_device(): lax.all_gather(rows_out, 'ctx', axis=0, tiled=True)  77.1 us
    unnamed x1, blocking collectives  57.5 us
    all_gather x1, waiting for transfers between devices, on_device(): key_part = lax.all_gather(key_rows, 'ctx', axis=0, tiled=True)  49.6 us
    all_gather x1, waiting for transfers between devices, gather_together(): lines, at, gathered = (lax.all_gather(flat, axis), 0, [])  45.3 us
    all_to_all x1, blocking collectives, sent_and_summed(): lax.all_to_all(blocks, axis, split_axis=0, concat_axis=0, tiled=True)  31.6 us
  transfers between devices with their start and end apart: 3, of which 3 were waited for; matrix products, arithmetic and copies ran while one was open for 9% of the time, Pallas kernels for 0%

commit v1 on v0

v1 whole, which is shorter than its diff:
```python
import functools

import jax
import jax.numpy as jnp
from jax import lax
from jax.experimental import pallas as pl
from jax.experimental.pallas import tpu as pltpu
from jax.sharding import PartitionSpec as P

LANES = 128
DIGIT = 32


def cos_sin(position, half_dim):
    freqs = 10000.0 ** (-jnp.arange(half_dim, dtype=jnp.float32) / half_dim)
    angles = position.astype(jnp.float32)[..., None] * freqs
    return jnp.cos(angles), jnp.sin(angles)


def rotate(values, cosine, sine):
    half_dim = values.shape[-1] // 2
    first_half = values[..., :half_dim].astype(jnp.float32)
    second_half = values[..., half_dim:].astype(jnp.float32)
    return jnp.concatenate(
        [first_half * cosine - second_half * sine, second_half * cosine + first_half * sine],
        axis=-1,
    )


def attend(ranks, toks, lat, tile, scale, qx_ref, qr_ref, qpos_ref, packed, out_ref, wk, keys, wv, q_all, sems):
    groups = qx_ref.shape[0]
    rope_lanes = qr_ref.shape[-1]
    per_group = qx_ref.shape[1]
    wide = lat // rope_lanes

    def copy(i, src, dst):
        c = pltpu.make_async_copy(src, dst, sems.at[i])
        c.start()
        return c

    rows_k, rows_v, rows_r = toks, toks + groups * tile, toks + 2 * groups * tile
    first = copy(0, packed.at[:, rows_k:rows_v, :], wk)
    key_copies = [copy(1, packed.at[:, 0:toks, :], keys.at[:, :, 0:lat])]
    part = toks // wide
    for j in range(wide):
        key_copies.append(
            copy(
                3 + j,
                packed.at[:, rows_r : rows_r + part, j * rope_lanes : (j + 1) * rope_lanes],
                keys.at[:, j * part : (j + 1) * part, lat : lat + rope_lanes],
            )
        )
    last = copy(2, packed.at[:, rows_v:rows_r, :], wv)
    first.wait()
    for g in range(groups):
        w = wk[:, g * tile : (g + 1) * tile, :].reshape(ranks * tile, lat)
        q_lat = jnp.dot(qx_ref[g], w, preferred_element_type=jnp.float32)
        q_all[g, :, 0:lat] = q_lat.astype(jnp.bfloat16)
        q_all[g, :, lat:] = qr_ref[g]
    for c in key_copies:
        c.wait()
    all_keys = keys[...].reshape(ranks * toks, lat + rope_lanes)
    lane = lax.broadcasted_iota(jnp.int32, (8, rope_lanes), 1)
    half = rope_lanes // 2
    pick = jnp.where(lane == half, float(DIGIT), jnp.where(lane == half + 1, 1.0, 0.0))
    key_pos = lax.dot_general(
        pick.astype(jnp.bfloat16),
        all_keys[:, lat:],
        (((1,), (1,)), ((), ())),
        preferred_element_type=jnp.float32,
    )[0:1]
    visible = key_pos <= qpos_ref[...]
    last.wait()
    factor = scale * 1.4426950408889634
    head_dim = lat // (per_group // toks)
    for g in range(groups):
        scores = lax.dot_general(
            q_all[g], all_keys, (((1,), (1,)), ((), ())), preferred_element_type=jnp.float32
        )
        scores = jnp.where(visible, scores, -1e30)
        top = jnp.max(scores, axis=1, keepdims=True)
        weights = jnp.exp2((scores - top) * factor)
        total = jnp.sum(weights, axis=1, keepdims=True)
        mixed = jnp.dot(
            weights.astype(jnp.bfloat16), all_keys[:, :lat], preferred_element_type=jnp.float32
        )
        o_lat = (mixed / total).astype(jnp.bfloat16)
        w = wv[:, g * tile : (g + 1) * tile, :].reshape(ranks * tile, lat)
        head_out = jnp.dot(o_lat, w, preferred_element_type=jnp.float32).astype(jnp.bfloat16)
        for h in range(per_group // toks):
            at = g * lat + h * head_dim
            out_ref[:, at : at + head_dim] = head_out[
                h * toks : (h + 1) * toks, h * head_dim : (h + 1) * head_dim
            ]


def on_device(q_nope, q_rope, c_kv, k_rope, positions, w_uk, w_uv, w_out):
    toks, lat = c_kv.shape
    heads, tile_rows, _ = w_uk.shape
    ranks = lax.axis_size("ctx")
    nope = tile_rows * ranks
    rope = k_rope.shape[1]
    v_dim = w_uv.shape[2]
    v_rows = w_uv.shape[1]
    scale = (nope + rope) ** (-0.5)
    group = lat // v_dim
    groups = heads // group
    tile = group * tile_rows
    assert tile == v_rows and group * nope == lat
    cosine, sine = cos_sin(positions, rope // 2)

    k_rot = rotate(k_rope, cosine, sine).astype(jnp.bfloat16)
    digits = jnp.stack([positions // DIGIT, positions % DIGIT], axis=1).astype(jnp.bfloat16)
    rot_part = jnp.concatenate(
        [k_rot, digits, jnp.zeros((toks, LANES - rope - 2), jnp.bfloat16)], axis=1
    )
    wide = lat // LANES
    rot_part = rot_part.reshape(wide, toks // wide, LANES).transpose(1, 0, 2).reshape(-1, lat)
    v_part = w_uv.reshape(groups, group, v_rows, v_dim).transpose(0, 2, 1, 3).reshape(-1, lat)
    own = jnp.concatenate([c_kv, w_uk.reshape(-1, lat), v_part, rot_part], axis=0)
    packed = lax.all_gather(own, "ctx", axis=0)

    row = lax.broadcasted_iota(jnp.int32, (lat, lat), 0)
    col = lax.broadcasted_iota(jnp.int32, (lat, lat), 1)
    target = (row % nope) // tile_rows * tile + (row // nope) * tile_rows + row % tile_rows
    order = (col == target).astype(jnp.bfloat16)
    q_groups = q_nope.reshape(toks, groups, lat).transpose(1, 0, 2)
    head_of = lax.broadcasted_iota(jnp.int32, (1, group, 1, lat), 3) // nope
    head = lax.broadcasted_iota(jnp.int32, (1, group, 1, lat), 1)
    q_masked = jnp.where(head_of == head, q_groups[:, None], jnp.bfloat16(0))
    qx = jnp.dot(
        q_masked.reshape(heads * toks, lat), order, preferred_element_type=jnp.float32
    ).astype(jnp.bfloat16)
    qx = qx.reshape(groups, group * toks, lat)
    q_rot = rotate(
        q_rope.reshape(toks, heads, rope), cosine[:, None], sine[:, None]
    ).astype(jnp.bfloat16)
    q_rot = jnp.pad(q_rot.transpose(1, 0, 2), ((0, 0), (0, 0), (0, LANES - rope)))
    q_rot = q_rot.reshape(groups, group * toks, LANES)
    q_pos = jnp.tile(positions.astype(jnp.float32), group)[:, None]

    vmem = pl.BlockSpec(memory_space=pltpu.VMEM)
    rows_out = pl.pallas_call(
        functools.partial(attend, ranks, toks, lat, tile, scale),
        out_shape=jax.ShapeDtypeStruct((toks, heads * v_dim), jnp.bfloat16),
        in_specs=[vmem, vmem, vmem, pl.BlockSpec(memory_space=pl.ANY)],
        out_specs=vmem,
        scratch_shapes=[
            pltpu.VMEM((ranks, groups * tile, lat), jnp.bfloat16),
            pltpu.VMEM((ranks, toks, lat + LANES), jnp.bfloat16),
            pltpu.VMEM((ranks, groups * tile, lat), jnp.bfloat16),
            pltpu.VMEM((groups, group * toks, lat + LANES), jnp.bfloat16),
            pltpu.SemaphoreType.DMA((3 + wide,)),
        ],
    )(qx, q_rot, q_pos, packed)

    partial_value = jnp.dot(
        lax.all_gather(rows_out, "ctx", axis=0, tiled=True),
        w_out,
        preferred_element_type=jnp.float32,
    ).astype(jnp.bfloat16)
    blocks = partial_value.reshape(lax.axis_size("tp"), -1, partial_value.shape[1])
    arrived = lax.all_to_all(blocks, "tp", split_axis=0, concat_axis=0, tiled=True)
    return arrived.astype(jnp.float32).sum(axis=0).astype(jnp.bfloat16)


def solution(mesh):
    in_specs = (
        P(("groups", "ctx"), "tp"),
        P(("groups", "ctx"), "tp"),
        P(("groups", "ctx"), None),
        P(("groups", "ctx"), None),
        P(("groups", "ctx")),
        P("tp", "ctx", None),
        P("tp", "ctx", None),
        P("tp", "ctx"),
    )
    out_specs = P(("groups", "tp"), "ctx")
    return jax.shard_map(
        on_device, mesh=mesh, in_specs=in_specs, out_specs=out_specs, check_vma=False
    )
```

time: 329 us -> 263 us (0.80)
  blocking collectives: 89.1 us -> 31.6 us
  local copies, waits for them, and re-layouts: 27.1 us -> 6.47 us
  Pallas kernels: 0 us -> 13.3 us
  waiting for transfers between devices: 172 us -> 185 us
  matrix products: 17.2 us -> 8.12 us
  other arithmetic: 8.72 us -> 4.56 us
    unnamed x1 -> x0, blocking collectives: 57.5 us -> none
    pallas_call x0 -> x1, Pallas kernels: none -> 13.3 us  [on_device(): pl.pallas_call(functools.partial(attend, ranks, toks, lat, tile, scale),...]
    all_gather x2 -> x1, waiting for transfers between devices: 94.9 us -> 107 us  [on_device(): packed = lax.all_gather(own, 'ctx', axis=0)]
    dot_general x4 -> x1, matrix products: 11.2 us -> 2.1 us  [on_device(): jnp.dot(q_masked.reshape(heads * toks, lat), order, preferred_element_typ...]
    all_gather x1 -> x0, local copies, waits for them, and re-layouts: 5.56 us -> none  [gather_together(): lines, at, gathered = (lax.all_gather(flat, axis), 0, [])]
    reshape x5 -> x4, local copies, waits for them, and re-layouts: 7.85 us -> 3.18 us  [the longest x1 1.13 us: on_device(): q_groups = q_nope.reshape(toks, groups, lat).transpose(1, 0, 2)]
    slice x1 -> x0, local copies, waits for them, and re-layouts: 4.42 us -> none  [gather_together(): blocks = lines[:, at:at + a.size].reshape(-1, *a.shape)]
    unnamed x11 -> x4, local copies, waits for them, and re-layouts: 3.64 us -> 0.02 us
  transfers between devices with their start and end apart: 3 -> 2, of which waited for: 3 -> 2; matrix products, arithmetic and copies ran while one was open for 9% -> 3% of each run, Pallas kernels for 0% -> 0%
where the time goes in v1:
time: 263 us
  waiting for transfers between devices  185 us (70%)
  blocking collectives  31.6 us (12%)
  between operations  13.6 us (5%)
  Pallas kernels  13.3 us (5%)
  matrix products  8.12 us (3%)
  local copies, waits for them, and re-layouts  6.47 us (2%)
  other arithmetic  4.56 us (2%)
    all_gather x1, waiting for transfers between devices, on_device(): packed = lax.all_gather(own, 'ctx', axis=0)  107 us
    all_gather x1, waiting for transfers between devices, on_device(): lax.all_gather(rows_out, 'ctx', axis=0, tiled=True)  77.4 us
    all_to_all x1, blocking collectives, on_device(): lax.all_to_all(blocks, 'tp', split_axis=0, concat_axis=0, tiled=True)  31.6 us
    pallas_call x1, Pallas kernels, on_device(): pl.pallas_call(functools.partial(attend, ranks, toks, lat, tile, scale),...  13.3 us
    dot_general x1, matrix products, on_device(): jnp.dot(lax.all_gather(rows_out, 'ctx', axis=0, tiled=True), w_out, prefe...  6.02 us
  transfers between devices with their start and end apart: 2, of which 2 were waited for; matrix products, arithmetic and copies ran while one was open for 3% of the time, Pallas kernels for 0%

profile of v1, /device:TPU:65, one launch (start us, length us, event | category | flops | bytes accessed | tf_op | source)
XLA Modules:
  0.0 262.6 jit_solution(11802056276642506272)
XLA Ops:
  6.5 0.0 copy-start
  6.6 0.0 all-gather.6.cloned.1.call-start
  6.6 0.8 fusion.46
  7.3 1.0 fusion.35
  8.4 0.1 stack.7
  8.4 0.1 copy.32
  8.6 0.1 stack.8
  8.7 0.1 copy.33
  8.8 0.2 concatenate.24
  9.0 0.9 copy.29
  9.9 0.9 reshape.153
  10.7 1.6 pad_maximum_fusion
  12.3 0.1 all-gather.6.cloned.1.call-update
  12.4 0.1 all-gather.4.cloned.1.call-start
  12.4 1.1 reshape.151
  13.6 0.1 fusion.55
  13.7 0.2 fusion.13
  13.9 0.2 maximum_bitcast_fusion
  14.1 0.8 pad.4
  14.9 1.1 reshape.149
  16.1 0.8 broadcast_in_dim_tile.4.qpos_ref
  16.9 0.1 broadcast_select_fusion
  17.0 2.1 convolution_convert_fusion.1
  19.1 107.5 %all-gather.6.cloned.1.call-done = bf16[6656,512]{1,0:T(8,128)(2,1)} async-done(((bf16[208,512]{1,0:T(8,128)(2,1)}), bf16[6656,512]{1,0:T(8,128)(2,1)}) %all-gather.6.cloned.1.call-update) | async-done | bytes 6815760 | tf_op jit(solution)/shard_map/all_gather | solution.py:121
  126.6 13.3 %shard_map.82 = bf16[64,2048]{1,0:T(8,128)(2,1)} custom-call(bf16[4,256,512]{2,1,0:T(8,128)(2,1)} %bitcast.34, bf16[4,256,128]{2,1,0:T(8,128)(2,1)} %bitcast.31, f32[256,1]{1,0:T(8,128)} %broadcast_in_dim_tile.4.qpos_ref, bf16[32,208,512]{2,1,0:T(8,128)(2,1)} %bitcast.29), custom_call_target="tpu_custom_call" | custom-call | tf_op jit(solution)/shard_map/pallas_call | solution.py:143
  139.9 0.1 all-gather.4.cloned.1.call-update
  139.9 77.4 %all-gather.4.cloned.1.call-done = bf16[2048,2048]{1,0:T(8,128)(2,1)} async-done(((bf16[64,2048]{1,0:T(8,128)(2,1)}), bf16[2048,2048]{1,0:T(8,128)(2,1)}) %all-gather.4.cloned.1.call-update) | async-done | bytes 8388624 | tf_op jit(solution)/shard_map/all_gather | solution.py:158
  217.3 0.0 copy-done
  217.3 6.0 %convolution_convert_fusion = bf16[2048,224]{0,1:T(8,128)(2,1)S(1)} fusion(bf16[2048,2048]{1,0:T(8,128)(2,1)} %all-gather.4.cloned.1.call-done, bf16[2048,224]{0,1:T(8,128)(2,1)S(1)} %copy-done), kind=kOutput, calls=%fused_computation | convolution fusion | flops 1879506944 | bytes 10223616 | tf_op jit(solution)/shard_map/dot_general | solution.py:157
  223.3 0.1 copy.48
  223.4 31.6 %all_to_all.5 = bf16[8,256,224]{1,2,0:T(8,128)(2,1)S(1)} all-to-all(bf16[8,256,224]{1,2,0:T(8,128)(2,1)S(1)} %bitcast.30), channel_id=1, replica_groups=mesh['groups'=2,'ctx'=32,'tp'=8] {'tp'}, dimensions={0} | all-to-all | bytes 1835008 | tf_op jit(solution)/shard_map/all_to_all | solution.py:163
  255.0 0.8 reduce_sum.12
  (14 shorter events, 0.1 us)
Async XLA Ops:
  6.5 210.8 %copy-start = (bf16[2048,224]{0,1:T(8,128)(2,1)S(1)}, bf16[2048,224]{0,1:T(8,128)(2,1)}, u32[]{:S(2)}) copy-start(bf16[2048,224]{0,1:T(8,128)(2,1)} %param.15) | copy-start | bytes 2752516
  6.6 120.0 %all-gather.6.cloned.1.call-start = ((), (), s32[]{:S(2)}) async-start(), calls=%async_computation.2 | async-start | bytes 7028736 | tf_op jit(solution)/shard_map/all_gather | solution.py:121
  12.4 204.9 %all-gather.4.cloned.1.call-start = ((), (), s32[]{:S(2)}) async-start(), calls=%async_computation.1 | async-start | bytes 8650752 | tf_op jit(solution)/shard_map/all_gather | solution.py:158
Sparse Core Ops, SparseCore 0:
  12.5 114.0 all-gather.5
  140.1 77.1 all-gather.3

commit v2 on v1

v2 whole, which is shorter than its diff:
```python
import functools

import jax
import jax.numpy as jnp
from jax import lax
from jax.experimental import pallas as pl
from jax.experimental.pallas import tpu as pltpu
from jax.sharding import PartitionSpec as P

LANES = 128
DIGIT = 32
CORES = 2


def cos_sin(position, half_dim):
    freqs = 10000.0 ** (-jnp.arange(half_dim, dtype=jnp.float32) / half_dim)
    angles = position.astype(jnp.float32)[..., None] * freqs
    return jnp.cos(angles), jnp.sin(angles)


def rotate(values, cosine, sine):
    half_dim = values.shape[-1] // 2
    first_half = values[..., :half_dim].astype(jnp.float32)
    second_half = values[..., half_dim:].astype(jnp.float32)
    return jnp.concatenate(
        [first_half * cosine - second_half * sine, second_half * cosine + first_half * sine],
        axis=-1,
    )


def attend(chips, toks, lat, scale, block, core_ref, q_ref, wv_ref, packed, out_ref, keys, sems):
    wide = lat // LANES
    part = toks // wide
    copies = [pltpu.make_async_copy(packed.at[:, :, 0:toks, :], keys.at[:, :, :, 0:lat], sems.at[0])]
    for j in range(wide):
        copies.append(
            pltpu.make_async_copy(
                packed.at[:, :, toks : toks + part, j * LANES : (j + 1) * LANES],
                keys.at[:, :, j * part : (j + 1) * part, lat : lat + LANES],
                sems.at[1 + j],
            )
        )
    for c in copies:
        c.start()
    for c in copies:
        c.wait()
    all_keys = keys[...].reshape(chips * CORES * toks, lat + LANES)
    half = LANES // 2
    lane = lax.broadcasted_iota(jnp.int32, (LANES, LANES), 1)
    pick = jnp.where(lane == half, float(DIGIT), jnp.where(lane == half + 1, 1.0, 0.0))
    pick = pick.astype(jnp.bfloat16)
    nt = (((1,), (1,)), ((), ()))
    key_pos = lax.dot_general(pick[0:8], all_keys[:, lat:], nt, preferred_element_type=jnp.float32)[0:1]
    own = keys[:, pl.ds(core_ref[0], 1), :, lat : lat + LANES].reshape(chips * toks, LANES)
    q_pos = lax.dot_general(own, pick, nt, preferred_element_type=jnp.float32)[:, 0:1]
    factor = scale * 1.4426950408889634
    for b in range(chips * toks // block):
        rows = slice(b * block, (b + 1) * block)
        scores = lax.dot_general(q_ref[rows, :], all_keys, nt, preferred_element_type=jnp.float32)
        scores = jnp.where(key_pos <= q_pos[rows], scores, -1e30)
        top = jnp.max(scores, axis=1, keepdims=True)
        weights = jnp.exp2((scores - top) * factor)
        total = jnp.sum(weights, axis=1, keepdims=True)
        mixed = jnp.dot(
            weights.astype(jnp.bfloat16), all_keys[:, :lat], preferred_element_type=jnp.float32
        )
        o_lat = (mixed / total).astype(jnp.bfloat16)
        out_ref[rows, :] = jnp.dot(
            o_lat, wv_ref[...], preferred_element_type=jnp.float32
        ).astype(jnp.bfloat16)


def project(chips, planes, toks, steps, gathered, weights, out_ref, heads_buf, w_buf, sems):
    each = chips // steps
    pairs = heads_buf.shape[2] // (CORES * toks)
    v_dim = heads_buf.shape[3]
    copies = []
    for s in range(steps):
        zs = slice(s * each, (s + 1) * each)
        group = [
            pltpu.make_async_copy(
                weights.at[:, :, s * each * v_dim : (s + 1) * each * v_dim], w_buf.at[s], sems.at[s, 0]
            )
        ]
        for pair in range(pairs):
            for k in range(CORES):
                at = (pair * CORES + k) * toks
                group.append(
                    pltpu.make_async_copy(
                        gathered.at[zs, k, :, pair * toks : (pair + 1) * toks, :],
                        heads_buf.at[zs, :, at : at + toks, :],
                        sems.at[s, 1 + pair * CORES + k],
                    )
                )
        copies.append(group)
    for group in copies:
        for c in group:
            c.start()
    total = None
    for s in range(steps):
        for c in copies[s]:
            c.wait()
        for i in range(each):
            z = s * each + i
            rows = jnp.concatenate([heads_buf[z, x] for x in range(planes)], axis=1)
            w = jnp.concatenate(
                [w_buf[s, x, :, i * v_dim : (i + 1) * v_dim] for x in range(planes)], axis=1
            )
            added = lax.dot_general(
                w, rows, (((1,), (1,)), ((), ())), preferred_element_type=jnp.float32
            )
            total = added if total is None else total + added
    out_ref[...] = total.astype(jnp.bfloat16)


def on_device(q_nope, q_rope, c_kv, k_rope, positions, w_uk, w_uv, w_out):
    toks, lat = c_kv.shape
    heads, tile_rows, _ = w_uk.shape
    ranks = lax.axis_size("ctx")
    planes = lax.axis_size("tp")
    chips = ranks // CORES
    assert heads == chips
    nope = tile_rows * ranks
    rope = k_rope.shape[1]
    v_rows, v_dim = w_uv.shape[1:]
    scale = (nope + rope) ** (-0.5)
    same_core = [[z * CORES + k for z in range(chips)] for k in range(CORES)]
    one_chip = [[z * CORES + k for k in range(CORES)] for z in range(chips)]
    cosine, sine = cos_sin(positions, rope // 2)

    k_rot = rotate(k_rope, cosine, sine).astype(jnp.bfloat16)
    digits = jnp.stack([positions // DIGIT, positions % DIGIT], axis=1).astype(jnp.bfloat16)
    rot_part = jnp.concatenate(
        [k_rot, digits, jnp.zeros((toks, LANES - rope - 2), jnp.bfloat16)], axis=1
    )
    wide = lat // LANES
    rot_part = rot_part.reshape(wide, toks // wide, LANES).transpose(1, 0, 2).reshape(-1, lat)
    packed = lax.all_gather(jnp.concatenate([c_kv, rot_part], axis=0), "ctx", axis=0)
    packed = packed.reshape(chips, CORES, toks + toks // wide, lat)

    q_parts = q_nope.reshape(toks, heads, nope).transpose(1, 0, 2)
    q_rot = rotate(q_rope.reshape(toks, heads, rope), cosine[:, None], sine[:, None])
    q_rot = q_rot.astype(jnp.bfloat16).transpose(1, 0, 2)
    q_rot = jnp.concatenate([q_rot[:, : toks // 2], q_rot[:, toks // 2 :]], axis=2)
    k_rows = tile_rows * wide
    sent = jnp.concatenate([q_parts, q_rot, w_uk.reshape(heads, k_rows, LANES), w_uv], axis=1)
    came = lax.all_to_all(
        sent, "ctx", split_axis=0, concat_axis=0, tiled=True, axis_index_groups=same_core
    )
    cut = toks + toks // 2
    q_parts = came[:, :toks].reshape(chips * toks, nope)
    q_rot = came[:, toks:cut]
    q_rot = jnp.concatenate([q_rot[:, :, :rope], q_rot[:, :, rope:]], axis=1).reshape(-1, rope)
    both = lax.all_to_all(
        jnp.broadcast_to(came[None, :, cut:], (CORES, chips, k_rows + v_rows, LANES)),
        "ctx",
        split_axis=0,
        concat_axis=0,
        tiled=True,
        axis_index_groups=one_chip,
    ).transpose(1, 0, 2, 3)
    up_key = both[:, :, :k_rows].reshape(nope, lat)
    up_value = both[:, :, k_rows:].reshape(lat, v_dim)
    q_lat = jnp.dot(q_parts, up_key, preferred_element_type=jnp.float32).astype(jnp.bfloat16)
    queries = jnp.concatenate(
        [q_lat, q_rot, jnp.zeros((chips * toks, LANES - rope), jnp.bfloat16)], axis=1
    )

    plane = lax.axis_index("tp")
    own_w = w_out.T
    right = [(i, (i + 1) % planes) for i in range(planes)]
    left = [(i, (i - 1) % planes) for i in range(planes)]
    all_w = jnp.zeros((planes, *own_w.shape), jnp.bfloat16)

    def placed(stack, block, shift):
        return lax.dynamic_update_slice(stack, block[None], ((plane + shift) % planes, 0, 0))

    def spread(stack, lower, upper, first, until):
        for s in range(first, until):
            lower = lax.ppermute(lower, "tp", right)
            stack = placed(stack, lower, planes - s)
            if 2 * s < planes:
                upper = lax.ppermute(upper, "tp", left)
                stack = placed(stack, upper, s)
        return stack, lower, upper

    all_w = placed(all_w, own_w, 0)
    early = planes // 4
    all_w, lower, upper = spread(all_w, own_w, own_w, 1, 1 + early)

    vmem = pl.BlockSpec(memory_space=pltpu.VMEM)
    smem = pl.BlockSpec(memory_space=pltpu.SMEM)
    hbm = pl.BlockSpec(memory_space=pl.ANY)
    core = (lax.axis_index("ctx") % CORES).astype(jnp.int32).reshape(1)
    block = min(256, chips * toks)
    head_out = pl.pallas_call(
        functools.partial(attend, chips, toks, lat, scale, block),
        out_shape=jax.ShapeDtypeStruct((chips * toks, v_dim), jnp.bfloat16),
        in_specs=[smem, vmem, vmem, hbm],
        out_specs=vmem,
        scratch_shapes=[
            pltpu.VMEM((chips, CORES, toks, lat + LANES), jnp.bfloat16),
            pltpu.SemaphoreType.DMA((1 + wide,)),
        ],
    )(core, queries, up_value, packed)

    head_out, all_w, lower, upper = lax.optimization_barrier((head_out, all_w, lower, upper))
    by_plane = lax.all_to_all(
        head_out.reshape(planes, -1, v_dim), "tp", split_axis=0, concat_axis=0, tiled=True
    )
    gathered = lax.all_gather(by_plane.reshape(-1, v_dim), "ctx", axis=0)
    gathered = gathered.reshape(chips, CORES, planes, -1, v_dim)
    all_w, _, _ = spread(all_w, lower, upper, 1 + early, planes // 2 + 1)

    out_toks = gathered.shape[3] * CORES
    columns = w_out.shape[1]
    steps = 4
    out = pl.pallas_call(
        functools.partial(project, chips, planes, toks, steps),
        out_shape=jax.ShapeDtypeStruct((columns, out_toks), jnp.bfloat16),
        in_specs=[hbm, hbm],
        out_specs=vmem,
        scratch_shapes=[
            pltpu.VMEM((chips, planes, out_toks, v_dim), jnp.bfloat16),
            pltpu.VMEM((steps, planes, columns, chips // steps * v_dim), jnp.bfloat16),
            pltpu.SemaphoreType.DMA((steps, 1 + out_toks // toks)),
        ],
    )(gathered, all_w)
    return out.T


def solution(mesh):
    in_specs = (
        P(("groups", "ctx"), "tp"),
        P(("groups", "ctx"), "tp"),
        P(("groups", "ctx"), None),
        P(("groups", "ctx"), None),
        P(("groups", "ctx")),
        P("tp", "ctx", None),
        P("tp", "ctx", None),
        P("tp", "ctx"),
    )
    out_specs = P(("groups", "tp"), "ctx")
    return jax.shard_map(
        on_device, mesh=mesh, in_specs=in_specs, out_specs=out_specs, check_vma=False
    )
```

time: 263 us -> 250 us (0.951)
  waiting for transfers between devices: 185 us -> 99.3 us
  starting transfers between devices: 0.07 us -> 66.8 us
  local copies, waits for them, and re-layouts: 6.47 us -> 17.4 us
  matrix products: 8.12 us -> 0.42 us
  blocking collectives: 31.6 us -> 24.5 us
  Pallas kernels: 13.3 us -> 19.8 us
    all_gather x2, waiting for transfers between devices: 185 us -> 48.4 us  [the longest x1 24.7 us: on_device(): gathered = lax.all_gather(by_plane.reshape(-1, v_dim), 'ctx', axis=0)]
    ppermute x0 -> x7, waiting for transfers between devices: none -> 50.8 us  [the longest x4 50.8 us: spread(): lower = lax.ppermute(lower, 'tp', right)]
    all_to_all x0 -> x1, starting transfers between devices: none -> 43.4 us  [on_device(): lax.all_to_all(sent, 'ctx', split_axis=0, concat_axis=0, tiled=True, axis...]
    ppermute x0 -> x7, starting transfers between devices: none -> 23.3 us  [the longest x3 13.4 us: spread(): upper = lax.ppermute(upper, 'tp', left)]
    dynamic_update_slice x0 -> x8, local copies, waits for them, and re-layouts: none -> 9.37 us  [placed(): lax.dynamic_update_slice(stack, block[None], ((plane + shift) % planes, 0...]
    dot_general x2 -> x1, matrix products: 8.12 us -> 0.42 us  [on_device(): jnp.dot(q_parts, up_key, preferred_element_type=jnp.float32)]
    all_to_all x1 -> x2, blocking collectives: 31.6 us -> 24.5 us  [the longest x1 18.4 us: on_device(): lax.all_to_all(head_out.reshape(planes, -1, v_dim), 'tp', split_axis=0, c...]
    pallas_call x1 -> x2, Pallas kernels: 13.3 us -> 19.8 us  [the longest x1 12.1 us: on_device(): pl.pallas_call(functools.partial(attend, chips, toks, lat, scale, block),...]
  transfers between devices with their start and end apart: 2 -> 10, of which waited for: 2 -> 5; matrix products, arithmetic and copies ran while one was open for 3% -> 8% of each run, Pallas kernels for 0% -> 0%
where the time goes in v2:
time: 250 us; the launch traced here: 249 us
  waiting for transfers between devices  99.3 us (40%)
  starting transfers between devices  66.8 us (27%)
  blocking collectives  24.5 us (10%)
  Pallas kernels  19.8 us (8%)
  local copies, waits for them, and re-layouts  17.4 us (7%)
  between operations  13.8 us (6%)
  other arithmetic  6.84 us (3%)
    ppermute x4, waiting for transfers between devices, spread(): lower = lax.ppermute(lower, 'tp', right)  50.8 us
    all_to_all x1, starting transfers between devices, on_device(): lax.all_to_all(sent, 'ctx', split_axis=0, concat_axis=0, tiled=True, axis...  43.4 us
    all_gather x1, waiting for transfers between devices, on_device(): gathered = lax.all_gather(by_plane.reshape(-1, v_dim), 'ctx', axis=0)  24.7 us
    all_gather x1, waiting for transfers between devices, on_device(): lax.all_gather(jnp.concatenate([c_kv, rot_part], axis=0), 'ctx', axis=0)  23.6 us
    all_to_all x1, blocking collectives, on_device(): lax.all_to_all(head_out.reshape(planes, -1, v_dim), 'tp', split_axis=0, c...  18.4 us
    ppermute x3, starting transfers between devices, spread(): upper = lax.ppermute(upper, 'tp', left)  13.4 us
    pallas_call x1, Pallas kernels, on_device(): pl.pallas_call(functools.partial(attend, chips, toks, lat, scale, block),...  12.1 us
    ppermute x4, starting transfers between devices, spread(): lower = lax.ppermute(lower, 'tp', right)  9.94 us
  transfers between devices with their start and end apart: 10, of which 5 were waited for; matrix products, arithmetic and copies ran while one was open for 8% of the time, Pallas kernels for 0%

profile of v2, /device:TPU:65, one launch (start us, length us, event | category | flops | bytes accessed | tf_op | source)
XLA Modules:
  0.0 248.8 jit_solution(13864549172091859306)
XLA Ops:
  6.6 0.7 fusion.8
  7.3 1.0 fusion.7
  8.3 0.1 stack.7
  8.4 0.1 copy.34
  8.5 0.1 stack.8
  8.6 0.1 copy.35
  8.8 0.2 concatenate.40
  9.0 1.6 pad_maximum_fusion.2
  10.6 4.1 %collective-permute-start = (bf16[224,2048]{1,0:T(8,128)(2,1)}, bf16[224,2048]{1,0:T(8,128)(2,1)S(1)}, u32[]{:S(2)}, u32[]{:S(2)}) collective-permute-start(bf16[224,2048]{1,0:T(8,128)(2,1)} %bitcast.55), channel_id=1, source_target_pairs={{0,1},{1,2},{2,3},{3,4},{4,5},{5,6},{6,7},{7,0},{8,9},{9,10},{10,1... | collective-permute-start | bytes 2752520 | tf_op jit(solution)/shard_map/ppermute | solution.py:180
  14.7 4.1 %collective-permute-start.1 = (bf16[224,2048]{1,0:T(8,128)(2,1)}, bf16[224,2048]{1,0:T(8,128)(2,1)S(1)}, u32[]{:S(2)}, u32[]{:S(2)}) collective-permute-start(bf16[224,2048]{1,0:T(8,128)(2,1)} %bitcast.56), channel_id=1, source_target_pairs={{0,7},{1,0},{2,1},{3,2},{4,3},{5,4},{6,5},{7,6},{8,15},{9,8},{10,9... | collective-permute-start | bytes 2752520 | tf_op jit(solution)/shard_map/ppermute | solution.py:183
  18.9 1.1 reshape.104
  20.0 0.1 fusion.13
  20.1 0.2 fusion.1
  20.3 0.2 maximum_bitcast_fusion
  20.5 0.9 reshape.105
  21.5 1.8 pad_maximum_fusion
  23.2 43.4 %all-to-all-start = ((bf16[16,128,128]{2,1,0:T(8,128)(2,1)}), bf16[16,128,128]{2,1,0:T(8,128)(2,1)S(1)}, u32[]{:S(2)}, u32[]{:S(2)}) async-start(bf16[16,128,128]{2,1,0:T(8,128)(2,1)} %pad_maximum_fusion), calls=%async_computation | async-start | bytes 1048576 | tf_op jit(solution)/shard_map/all_to_all | solution.py:147
  66.6 0.1 all-gather.4.cloned.1.call-start
  66.8 0.1 pad.4.clone
  66.9 3.9 %broadcast_in_dim.46 = bf16[8,224,2048]{2,1,0:T(8,128)(2,1)} broadcast(bf16[]{:T(256)} %constant.94.clone.1), dimensions={} | broadcast | bytes 7340034 | tf_op jit(solution)/shard_map/broadcast_in_dim | solution.py:173
  70.8 1.1 bitcast_dynamic-update-slice_fusion
  71.8 1.9 collective-permute-start.2
  73.8 4.6 %collective-permute-start.3 = (bf16[224,2048]{1,0:T(8,128)(2,1)S(1)}, bf16[224,2048]{1,0:T(8,128)(2,1)S(1)}, u32[]{:S(2)}, u32[]{:S(2)}) collective-permute-start(bf16[224,2048]{1,0:T(8,128)(2,1)S(1)} %collective-permute-done.1), channel_id=1, source_target_pairs={{0,7},{1,0},{2,1},{3,2},{4,3},{5,4},{6,5},{7,6},{8,15},{9,8},{10,9... | collective-permute-start | bytes 2752520 | tf_op jit(solution)/shard_map/ppermute | solution.py:183
  78.4 1.0 bitcast_dynamic-update-slice_fusion.7
  79.4 1.0 bitcast_dynamic-update-slice_fusion.6
  80.4 15.3 %collective-permute-done.2 = bf16[224,2048]{1,0:T(8,128)(2,1)S(1)} collective-permute-done((bf16[224,2048]{1,0:T(8,128)(2,1)S(1)}, bf16[224,2048]{1,0:T(8,128)(2,1)S(1)}, u32[]{:S(2)}, u32[]{:S(2)}) %collective-permute-start.2) | collective-permute-done | bytes 917536 | tf_op jit(solution)/shard_map/ppermute | solution.py:180
  95.7 1.1 bitcast_dynamic-update-slice_fusion.5
  96.8 0.2 copy-done.2
  97.0 1.0 bitcast_dynamic-update-slice_fusion.4
  98.1 6.1 %all_to_all.15 = bf16[2,16,32,128]{3,2,1,0:T(8,128)(2,1)S(1)} all-to-all(bf16[2,16,32,128]{3,2,1,0:T(8,128)(2,1)S(1)} %broadcast_in_dim.43), channel_id=1, replica_groups={{0,8},{16,24},{32,40},{48,56},{64,72},{80,88},{96,104},{112,120},{128,1..., dimensions={0} | all-to-all | bytes 524288 | tf_op jit(solution)/shard_map/all_to_all | solution.py:154
  104.2 0.1 reshape.107
  104.3 0.7 copy.31
  105.0 0.1 fusion.10
  105.2 0.4 convolution_convert_fusion
  105.6 1.4 maximum_maximum_fusion.q_ref
  107.0 23.6 %all-gather.6.cloned.1.call-done = bf16[2560,512]{1,0:T(8,128)(2,1)} async-done(((bf16[80,512]{1,0:T(8,128)(2,1)}), bf16[2560,512]{1,0:T(8,128)(2,1)}) %all-gather.6.cloned.1.call-update) | async-done | bytes 2621456 | tf_op jit(solution)/shard_map/all_gather | solution.py:138
  130.6 12.1 %shard_map.82 = bf16[1024,128]{1,0:T(8,128)(2,1)} custom-call(s32[1]{0:T(128)} %bitcast.core_ref, bf16[1024,640]{1,0:T(8,128)(2,1)} %maximum_maximum_fusion.q_ref, bf16[512,128]{1,0:T(8,128)(2,1)} %bitcast.57, bf16[16,2,80,512]{3,2,1,0:T(8,128)(2,1)} %bitcast.49), custom_call_target="tpu_custom_call" | custom-call | tf_op jit(solution)/shard_map/pallas_call | solution.py:196
  142.7 18.4 %all_to_all.16 = bf16[8,128,128]{2,1,0:T(8,128)(2,1)} all-to-all(bf16[8,128,128]{2,1,0:T(8,128)(2,1)} %bitcast.51), channel_id=1, replica_groups=mesh['groups'=2,'ctx'=32,'tp'=8] {'tp'}, dimensions={0} | all-to-all | bytes 524288 | tf_op jit(solution)/shard_map/all_to_all | solution.py:208
  161.1 2.0 collective-permute-start.4
  163.1 4.6 %collective-permute-start.5 = (bf16[224,2048]{1,0:T(8,128)(2,1)S(1)}, bf16[224,2048]{1,0:T(8,128)(2,1)}, u32[]{:S(2)}, u32[]{:S(2)}) collective-permute-start(bf16[224,2048]{1,0:T(8,128)(2,1)S(1)} %collective-permute-done.3), channel_id=1, source_target_pairs={{0,7},{1,0},{2,1},{3,2},{4,3},{5,4},{6,5},{7,6},{8,15},{9,8},{10,9... | collective-permute-start | bytes 2752520 | tf_op jit(solution)/shard_map/ppermute | solution.py:183
  167.8 17.4 %collective-permute-done.4 = bf16[224,2048]{1,0:T(8,128)(2,1)S(1)} collective-permute-done((bf16[224,2048]{1,0:T(8,128)(2,1)S(1)}, bf16[224,2048]{1,0:T(8,128)(2,1)S(1)}, u32[]{:S(2)}, u32[]{:S(2)}) %collective-permute-start.4) | collective-permute-done | bytes 917536 | tf_op jit(solution)/shard_map/ppermute | solution.py:180
  185.2 1.9 collective-permute-start.6
  187.1 1.0 bitcast_dynamic-update-slice_fusion.3
  188.1 2.2 bitcast_dynamic-update-slice_fusion.2
  190.3 18.1 %collective-permute-done.6 = bf16[224,2048]{1,0:T(8,128)(2,1)S(1)} collective-permute-done((bf16[224,2048]{1,0:T(8,128)(2,1)S(1)}, bf16[224,2048]{1,0:T(8,128)(2,1)S(1)}, u32[]{:S(2)}, u32[]{:S(2)}) %collective-permute-start.6) | collective-permute-done | bytes 917536 | tf_op jit(solution)/shard_map/ppermute | solution.py:180
  208.4 1.0 bitcast_dynamic-update-slice_fusion.1.weights
  209.4 24.7 %all-gather.4.cloned.1.call-done = bf16[32,1024,128]{2,1,0:T(8,128)(2,1)} async-done(((bf16[1,1024,128]{2,1,0:T(8,128)(2,1)}), bf16[32,1024,128]{2,1,0:T(8,128)(2,1)}) %all-gather.4.cloned.1.call-update) | async-done | bytes 8388624 | tf_op jit(solution)/shard_map/all_gather | solution.py:211
  234.2 7.7 %shard_map.83 = bf16[224,256]{1,0:T(8,128)(2,1)} custom-call(bf16[16,2,8,128,128]{4,3,2,1,0:T(8,128)(2,1)} %bitcast.48, bf16[8,224,2048]{2,1,0:T(8,128)(2,1)} %bitcast_dynamic-update-slice_fusion.1.weights), custom_call_target="tpu_custom_call" | custom-call | tf_op jit(solution)/shard_map/pallas_call | solution.py:218
  (29 shorter events, 0.4 us)
Async XLA Ops:
  6.5 14.9 %copy-start = (bf16[64,2048]{1,0:T(8,128)(2,1)S(1)}, bf16[64,2048]{1,0:T(8,128)(2,1)}, u32[]{:S(2)}) copy-start(bf16[64,2048]{1,0:T(8,128)(2,1)} %param.8) | copy-start | bytes 786436
  6.6 124.1 %all-gather.6.cloned.1.call-start = ((), (), s32[]{:S(2)}) async-start(), calls=%async_computation.4 | async-start | bytes 2703360 | tf_op jit(solution)/shard_map/all_gather | solution.py:138
  8.8 62.0 %copy-start.1 = (bf16[2048,224]{0,1:T(8,128)(2,1)S(1)}, bf16[2048,224]{0,1:T(8,128)(2,1)}, u32[]{:S(2)}) copy-start(bf16[2048,224]{0,1:T(8,128)(2,1)} %param.15) | copy-start | bytes 2752516
  10.6 61.2 %collective-permute-start = (bf16[224,2048]{1,0:T(8,128)(2,1)}, bf16[224,2048]{1,0:T(8,128)(2,1)S(1)}, u32[]{:S(2)}, u32[]{:S(2)}) collective-permute-start(bf16[224,2048]{1,0:T(8,128)(2,1)} %bitcast.55), channel_id=1, source_target_pairs={{0,1},{1,2},{2,3},{3,4},{4,5},{5,6},{6,7},{7,0},{8,9},{9,10},{10,1... | collective-permute-start | bytes 2752520 | tf_op jit(solution)/shard_map/ppermute | solution.py:180
  14.7 59.1 %collective-permute-start.1 = (bf16[224,2048]{1,0:T(8,128)(2,1)}, bf16[224,2048]{1,0:T(8,128)(2,1)S(1)}, u32[]{:S(2)}, u32[]{:S(2)}) collective-permute-start(bf16[224,2048]{1,0:T(8,128)(2,1)} %bitcast.56), channel_id=1, source_target_pairs={{0,7},{1,0},{2,1},{3,2},{4,3},{5,4},{6,5},{7,6},{8,15},{9,8},{10,9... | collective-permute-start | bytes 2752520 | tf_op jit(solution)/shard_map/ppermute | solution.py:183
  23.2 74.8 %all-to-all-start = ((bf16[16,128,128]{2,1,0:T(8,128)(2,1)}), bf16[16,128,128]{2,1,0:T(8,128)(2,1)S(1)}, u32[]{:S(2)}, u32[]{:S(2)}) async-start(bf16[16,128,128]{2,1,0:T(8,128)(2,1)} %pad_maximum_fusion), calls=%async_computation | async-start | bytes 1048576 | tf_op jit(solution)/shard_map/all_to_all | solution.py:147
  66.6 167.5 %all-gather.4.cloned.1.call-start = ((), (), s32[]{:S(2)}) async-start(), calls=%async_computation.3 | async-start | bytes 8650752 | tf_op jit(solution)/shard_map/all_gather | solution.py:211
  71.8 23.9 %collective-permute-start.2 = (bf16[224,2048]{1,0:T(8,128)(2,1)S(1)}, bf16[224,2048]{1,0:T(8,128)(2,1)S(1)}, u32[]{:S(2)}, u32[]{:S(2)}) collective-permute-start(bf16[224,2048]{1,0:T(8,128)(2,1)S(1)} %collective-permute-done), channel_id=1, source_target_pairs={{0,1},{1,2},{2,3},{3,4},{4,5},{5,6},{6,7},{7,0},{8,9},{9,10},{10,1... | collective-permute-start | bytes 2752520 | tf_op jit(solution)/shard_map/ppermute | solution.py:180
  73.8 23.0 %collective-permute-start.3 = (bf16[224,2048]{1,0:T(8,128)(2,1)S(1)}, bf16[224,2048]{1,0:T(8,128)(2,1)S(1)}, u32[]{:S(2)}, u32[]{:S(2)}) collective-permute-start(bf16[224,2048]{1,0:T(8,128)(2,1)S(1)} %collective-permute-done.1), channel_id=1, source_target_pairs={{0,7},{1,0},{2,1},{3,2},{4,3},{5,4},{6,5},{7,6},{8,15},{9,8},{10,9... | collective-permute-start | bytes 2752520 | tf_op jit(solution)/shard_map/ppermute | solution.py:183
  95.7 1.3 copy-start.2
  98.0 63.1 %copy-start.3 = (bf16[224,2048]{1,0:T(8,128)(2,1)S(1)}, bf16[224,2048]{1,0:T(8,128)(2,1)}, u32[]{:S(2)}) copy-start(bf16[224,2048]{1,0:T(8,128)(2,1)} %copy-done.2) | copy-start | bytes 2752516
  161.1 24.0 %collective-permute-start.4 = (bf16[224,2048]{1,0:T(8,128)(2,1)S(1)}, bf16[224,2048]{1,0:T(8,128)(2,1)S(1)}, u32[]{:S(2)}, u32[]{:S(2)}) collective-permute-start(bf16[224,2048]{1,0:T(8,128)(2,1)S(1)} %copy-done.3), channel_id=1, source_target_pairs={{0,1},{1,2},{2,3},{3,4},{4,5},{5,6},{6,7},{7,0},{8,9},{9,10},{10,1... | collective-permute-start | bytes 2752520 | tf_op jit(solution)/shard_map/ppermute | solution.py:180
  163.1 25.0 %collective-permute-start.5 = (bf16[224,2048]{1,0:T(8,128)(2,1)S(1)}, bf16[224,2048]{1,0:T(8,128)(2,1)}, u32[]{:S(2)}, u32[]{:S(2)}) collective-permute-start(bf16[224,2048]{1,0:T(8,128)(2,1)S(1)} %collective-permute-done.3), channel_id=1, source_target_pairs={{0,7},{1,0},{2,1},{3,2},{4,3},{5,4},{6,5},{7,6},{8,15},{9,8},{10,9... | collective-permute-start | bytes 2752520 | tf_op jit(solution)/shard_map/ppermute | solution.py:183
  185.2 23.2 %collective-permute-start.6 = (bf16[224,2048]{1,0:T(8,128)(2,1)S(1)}, bf16[224,2048]{1,0:T(8,128)(2,1)S(1)}, u32[]{:S(2)}, u32[]{:S(2)}) collective-permute-start(bf16[224,2048]{1,0:T(8,128)(2,1)S(1)} %collective-permute-done.4), channel_id=1, source_target_pairs={{0,1},{1,2},{2,3},{3,4},{4,5},{5,6},{6,7},{7,0},{8,9},{9,10},{10,1... | collective-permute-start | bytes 2752520 | tf_op jit(solution)/shard_map/ppermute | solution.py:180
Sparse Core Ops, SparseCore 0:
  10.7 119.8 all-gather.5
  161.3 72.8 all-gather.3

commit v3 on v2

--- a/solution.py
+++ b/solution.py
@@ -6,6 +6,7 @@
 from jax.experimental import pallas as pl
 from jax.experimental.pallas import tpu as pltpu
 from jax.sharding import PartitionSpec as P
+
 
 LANES = 128
 DIGIT = 32
@@ -28,31 +29,20 @@
     )
 
 
-def attend(chips, toks, lat, scale, block, core_ref, q_ref, wv_ref, packed, out_ref, keys, sems):
-    wide = lat // LANES
-    part = toks // wide
-    copies = [pltpu.make_async_copy(packed.at[:, :, 0:toks, :], keys.at[:, :, :, 0:lat], sems.at[0])]
-    for j in range(wide):
-        copies.append(
-            pltpu.make_async_copy(
-                packed.at[:, :, toks : toks + part, j * LANES : (j + 1) * LANES],
-                keys.at[:, :, j * part : (j + 1) * part, lat : lat + LANES],
-                sems.at[1 + j],
-            )
-        )
-    for c in copies:
-        c.start()
-    for c in copies:
-        c.wait()
-    all_keys = keys[...].reshape(chips * CORES * toks, lat + LANES)
+def attend(chips, planes, toks, lat, scale, block, q_ref, wv_ref, own_ref, other_ref, out_ref, pos_buf):
+    share = toks // planes
     half = LANES // 2
     lane = lax.broadcasted_iota(jnp.int32, (LANES, LANES), 1)
     pick = jnp.where(lane == half, float(DIGIT), jnp.where(lane == half + 1, 1.0, 0.0))
     pick = pick.astype(jnp.bfloat16)
     nt = (((1,), (1,)), ((), ()))
+    all_keys = jnp.concatenate([own_ref[...], other_ref[...]], axis=0)
     key_pos = lax.dot_general(pick[0:8], all_keys[:, lat:], nt, preferred_element_type=jnp.float32)[0:1]
-    own = keys[:, pl.ds(core_ref[0], 1), :, lat : lat + LANES].reshape(chips * toks, LANES)
-    q_pos = lax.dot_general(own, pick, nt, preferred_element_type=jnp.float32)[:, 0:1]
+    own_pos = lax.dot_general(own_ref[:, lat:], pick, nt, preferred_element_type=jnp.float32)
+    own_pos = own_pos.reshape(planes, chips, share, LANES)
+    for x in range(planes):
+        pos_buf[:, x] = own_pos[x]
+    q_pos = pos_buf[...].reshape(chips * toks, LANES)[:, 0:1]
     factor = scale * 1.4426950408889634
     for b in range(chips * toks // block):
         rows = slice(b * block, (b + 1) * block)
@@ -126,23 +116,32 @@
     scale = (nope + rope) ** (-0.5)
     same_core = [[z * CORES + k for z in range(chips)] for k in range(CORES)]
     one_chip = [[z * CORES + k for k in range(CORES)] for z in range(chips)]
+
+    plane = lax.axis_index("tp")
+    share = toks // planes
+
+    def cut_share(a):
+        return lax.dynamic_slice_in_dim(a, plane * share, share, 0)
+
+    own_pos = cut_share(positions)
+    k_rot = rotate(cut_share(k_rope), *cos_sin(own_pos, rope // 2)).astype(jnp.bfloat16)
+    digits = jnp.stack([own_pos // DIGIT, own_pos % DIGIT], axis=1).astype(jnp.bfloat16)
+    zeros = jnp.zeros((share, LANES - rope - 2), jnp.bfloat16)
+    own_keys = jnp.concatenate([cut_share(c_kv), k_rot, digits, zeros], axis=1)
+    own_keys = jnp.broadcast_to(own_keys, (chips, *own_keys.shape))
+    own_keys = lax.all_to_all(
+        own_keys, "ctx", split_axis=0, concat_axis=0, tiled=True, axis_index_groups=same_core
+    )
+    own_keys = lax.all_gather(own_keys.reshape(chips * share, -1), "tp", axis=0, tiled=True)
+    swap = [(r, r // CORES * CORES + (r + 1) % CORES) for r in range(ranks)]
+    other_keys = lax.ppermute(own_keys, "ctx", swap)
+
     cosine, sine = cos_sin(positions, rope // 2)
-
-    k_rot = rotate(k_rope, cosine, sine).astype(jnp.bfloat16)
-    digits = jnp.stack([positions // DIGIT, positions % DIGIT], axis=1).astype(jnp.bfloat16)
-    rot_part = jnp.concatenate(
-        [k_rot, digits, jnp.zeros((toks, LANES - rope - 2), jnp.bfloat16)], axis=1
-    )
-    wide = lat // LANES
-    rot_part = rot_part.reshape(wide, toks // wide, LANES).transpose(1, 0, 2).reshape(-1, lat)
-    packed = lax.all_gather(jnp.concatenate([c_kv, rot_part], axis=0), "ctx", axis=0)
-    packed = packed.reshape(chips, CORES, toks + toks // wide, lat)
-
     q_parts = q_nope.reshape(toks, heads, nope).transpose(1, 0, 2)
     q_rot = rotate(q_rope.reshape(toks, heads, rope), cosine[:, None], sine[:, None])
     q_rot = q_rot.astype(jnp.bfloat16).transpose(1, 0, 2)
     q_rot = jnp.concatenate([q_rot[:, : toks // 2], q_rot[:, toks // 2 :]], axis=2)
-    k_rows = tile_rows * wide
+    k_rows = tile_rows * lat // LANES
     sent = jnp.concatenate([q_parts, q_rot, w_uk.reshape(heads, k_rows, LANES), w_uv], axis=1)
     came = lax.all_to_all(
         sent, "ctx", split_axis=0, concat_axis=0, tiled=True, axis_index_groups=same_core
@@ -166,7 +165,6 @@
         [q_lat, q_rot, jnp.zeros((chips * toks, LANES - rope), jnp.bfloat16)], axis=1
     )
 
-    plane = lax.axis_index("tp")
     own_w = w_out.T
     right = [(i, (i + 1) % planes) for i in range(planes)]
     left = [(i, (i - 1) % planes) for i in range(planes)]
@@ -175,34 +173,20 @@
     def placed(stack, block, shift):
         return lax.dynamic_update_slice(stack, block[None], ((plane + shift) % planes, 0, 0))
 
-    def spread(stack, lower, upper, first, until):
-        for s in range(first, until):
-            lower = lax.ppermute(lower, "tp", right)
-            stack = placed(stack, lower, planes - s)
-            if 2 * s < planes:
-                upper = lax.ppermute(upper, "tp", left)
-                stack = placed(stack, upper, s)
-        return stack, lower, upper
-
-    all_w = placed(all_w, own_w, 0)
-    early = planes // 4
-    all_w, lower, upper = spread(all_w, own_w, own_w, 1, 1 + early)
+    lower = lax.ppermute(own_w, "tp", right)
+    all_w = placed(placed(all_w, own_w, 0), lower, planes - 1)
+    upper = own_w
 
     vmem = pl.BlockSpec(memory_space=pltpu.VMEM)
-    smem = pl.BlockSpec(memory_space=pltpu.SMEM)
     hbm = pl.BlockSpec(memory_space=pl.ANY)
-    core = (lax.axis_index("ctx") % CORES).astype(jnp.int32).reshape(1)
     block = min(256, chips * toks)
     head_out = pl.pallas_call(
-        functools.partial(attend, chips, toks, lat, scale, block),
+        functools.partial(attend, chips, planes, toks, lat, scale, block),
         out_shape=jax.ShapeDtypeStruct((chips * toks, v_dim), jnp.bfloat16),
-        in_specs=[smem, vmem, vmem, hbm],
+        in_specs=[vmem, vmem, vmem, vmem],
         out_specs=vmem,
-        scratch_shapes=[
-            pltpu.VMEM((chips, CORES, toks, lat + LANES), jnp.bfloat16),
-            pltpu.SemaphoreType.DMA((1 + wide,)),
-        ],
-    )(core, queries, up_value, packed)
+        scratch_shapes=[pltpu.VMEM((chips, planes, share, LANES), jnp.float32)],
+    )(queries, up_value, own_keys, other_keys)
 
     head_out, all_w, lower, upper = lax.optimization_barrier((head_out, all_w, lower, upper))
     by_plane = lax.all_to_all(
@@ -210,7 +194,10 @@
     )
     gathered = lax.all_gather(by_plane.reshape(-1, v_dim), "ctx", axis=0)
     gathered = gathered.reshape(chips, CORES, planes, -1, v_dim)
-    all_w, _, _ = spread(all_w, lower, upper, 1 + early, planes // 2 + 1)
+    for s in range(1, planes // 2):
+        lower = lax.ppermute(lower, "tp", right)
+        upper = lax.ppermute(upper, "tp", left)
+        all_w = placed(placed(all_w, lower, planes - 1 - s), upper, s)
 
     out_toks = gathered.shape[3] * CORES
     columns = w_out.shape[1]
@@ -241,6 +228,5 @@
         P("tp", "ctx"),
     )
     out_specs = P(("groups", "tp"), "ctx")
-    return jax.shard_map(
-        on_device, mesh=mesh, in_specs=in_specs, out_specs=out_specs, check_vma=False
-    )
+
+    return jax.shard_map(on_device, mesh=mesh, in_specs=in_specs, out_specs=out_specs, check_vma=False)

time: 250 us -> 251 us (level)
  starting transfers between devices: 66.8 us -> 80.8 us
  waiting for transfers between devices: 99.3 us -> 87.4 us
  local copies, waits for them, and re-layouts: 17.4 us -> 20.6 us
  blocking collectives: 24.5 us -> 21.6 us
    all_to_all x0 -> x1, starting transfers between devices: none -> 44.2 us  [on_device(): lax.all_to_all(own_keys, 'ctx', split_axis=0, concat_axis=0, tiled=True,...]
    all_to_all x1, starting transfers between devices: 43.4 us -> 7.81 us  [on_device(): lax.all_to_all(sent, 'ctx', split_axis=0, concat_axis=0, tiled=True, axis...]
    all_gather x1, waiting for transfers between devices: 24.7 us -> 8.69 us  [on_device(): gathered = lax.all_gather(by_plane.reshape(-1, v_dim), 'ctx', axis=0)]
    all_to_all x0 -> x1, waiting for transfers between devices: none -> 9.75 us  [on_device(): lax.all_to_all(own_keys, 'ctx', split_axis=0, concat_axis=0, tiled=True,...]
    ppermute x7 -> x8, waiting for transfers between devices: 50.8 us -> 44.3 us  [the longest x3 44.3 us: on_device(): lower = lax.ppermute(lower, 'tp', right)]
    ppermute x7 -> x8, starting transfers between devices: 23.3 us -> 28.7 us  [the longest x3 13.8 us: on_device(): upper = lax.ppermute(upper, 'tp', left)]
  transfers between devices with their start and end apart: 10 -> 12, of which waited for: 5 -> 6; matrix products, arithmetic and copies ran while one was open for 8% -> 9% of each run, Pallas kernels for 0% -> 0%
where the time goes in v3:
time: 251 us; the launch traced here: 250 us
  waiting for transfers between devices  87.4 us (35%)
  starting transfers between devices  80.8 us (32%)
  blocking collectives  21.6 us (9%)
  local copies, waits for them, and re-layouts  20.6 us (8%)
  Pallas kernels  19 us (8%)
  between operations  13.8 us (5%)
  other arithmetic  6.08 us (2%)
    ppermute x3, waiting for transfers between devices, on_device(): lower = lax.ppermute(lower, 'tp', right)  44.3 us
    all_to_all x1, starting transfers between devices, on_device(): lax.all_to_all(own_keys, 'ctx', split_axis=0, concat_axis=0, tiled=True,...  44.2 us
    all_gather x1, waiting for transfers between devices, on_device(): lax.all_gather(own_keys.reshape(chips * share, -1), 'tp', axis=0, tiled=T...  24.6 us
    all_to_all x1, blocking collectives, on_device(): lax.all_to_all(head_out.reshape(planes, -1, v_dim), 'tp', split_axis=0, c...  17.3 us
    ppermute x3, starting transfers between devices, on_device(): upper = lax.ppermute(upper, 'tp', left)  13.8 us
    pallas_call x1, Pallas kernels, on_device(): pl.pallas_call(functools.partial(attend, chips, planes, toks, lat, scale,...  11.2 us
    all_to_all x1, waiting for transfers between devices, on_device(): lax.all_to_all(own_keys, 'ctx', split_axis=0, concat_axis=0, tiled=True,...  9.75 us
    dynamic_update_slice x8, local copies, waits for them, and re-layouts, placed(): lax.dynamic_update_slice(stack, block[None], ((plane + shift) % planes, 0...  9.34 us
  transfers between devices with their start and end apart: 12, of which 6 were waited for; matrix products, arithmetic and copies ran while one was open for 9% of the time, Pallas kernels for 0%

profile of v3, /device:TPU:65, one launch (start us, length us, event | category | flops | bytes accessed | tf_op | source)
XLA Modules:
  0.0 249.7 jit_solution(16452280904971717163)
XLA Ops:
  6.6 0.8 fusion.13
  7.4 0.7 convert_bitcast_fusion
  8.1 0.7 constant_dynamic-slice_fusion
  9.0 0.7 constant_dynamic-slice_fusion.1
  9.9 0.7 broadcast_in_dim.51
  10.6 44.2 %all-to-all-start.2 = ((bf16[16,8,640]{2,1,0:T(8,128)(2,1)}), bf16[16,8,640]{2,1,0:T(8,128)(2,1)S(1)}, u32[]{:S(2)}, u32[]{:S(2)}) async-start(bf16[16,8,640]{2,1,0:T(8,128)(2,1)} %broadcast_in_dim.51), calls=%async_computation.2 | async-start | bytes 327680 | tf_op jit(solution)/shard_map/all_to_all | solution.py:132
  54.9 0.7 convert_element_type.25
  55.6 1.1 reshape.84
  56.7 0.2 multiply_cosine_fusion
  56.9 0.1 fusion.17
  57.0 9.7 %all-to-all-done.2 = bf16[16,8,640]{2,1,0:T(8,128)(2,1)S(1)} async-done(((bf16[16,8,640]{2,1,0:T(8,128)(2,1)}), bf16[16,8,640]{2,1,0:T(8,128)(2,1)S(1)}, u32[]{:S(2)}, u32[]{:S(2)}) %all-to-all-start.2) | async-done | bytes 163872 | tf_op jit(solution)/shard_map/all_to_all | solution.py:132
  66.8 0.7 copy-done.3
  67.5 0.2 fusion.1
  67.7 0.9 reshape.85
  68.6 0.2 maximum_bitcast_fusion
  68.9 1.8 pad_maximum_fusion
  70.6 7.8 %all-to-all-start = ((bf16[16,128,128]{2,1,0:T(8,128)(2,1)}), bf16[16,128,128]{2,1,0:T(8,128)(2,1)S(1)}, u32[]{:S(2)}, u32[]{:S(2)}) async-start(bf16[16,128,128]{2,1,0:T(8,128)(2,1)} %pad_maximum_fusion), calls=%async_computation | async-start | bytes 1048576 | tf_op jit(solution)/shard_map/all_to_all | solution.py:146
  78.5 3.5 %collective-permute-start.1 = (bf16[224,2048]{1,0:T(8,128)(2,1)S(1)}, bf16[224,2048]{1,0:T(8,128)(2,1)}, u32[]{:S(2)}, u32[]{:S(2)}) collective-permute-start(bf16[224,2048]{1,0:T(8,128)(2,1)S(1)} %bitcast.50), channel_id=1, source_target_pairs={{0,1},{1,2},{2,3},{3,4},{4,5},{5,6},{6,7},{7,0},{8,9},{9,10},{10,1... | collective-permute-start | bytes 2752520 | tf_op jit(solution)/shard_map/ppermute | solution.py:176
  82.2 3.9 %broadcast_in_dim.52 = bf16[8,224,2048]{2,1,0:T(8,128)(2,1)} broadcast(bf16[]{:T(256)} %constant.80.clone.1), dimensions={} | broadcast | bytes 7340034 | tf_op jit(solution)/shard_map/broadcast_in_dim | solution.py:171
  86.1 1.1 bitcast_dynamic-update-slice_fusion
  87.2 24.6 %all-gather.3.cloned.1.call-done.own_ref = bf16[1024,640]{1,0:T(8,128)(2,1)} async-done(((bf16[128,640]{1,0:T(8,128)(2,1)}), bf16[1024,640]{1,0:T(8,128)(2,1)}) %all-gather.3.cloned.1.call-update) | async-done | bytes 1310736 | tf_op jit(solution)/shard_map/all_gather | solution.py:135
  111.7 5.5 %collective-permute-start = (bf16[1024,640]{1,0:T(8,128)(2,1)}, bf16[1024,640]{1,0:T(8,128)(2,1)S(1)}, u32[]{:S(2)}, u32[]{:S(2)}) collective-permute-start(bf16[1024,640]{1,0:T(8,128)(2,1)} %all-gather.3.cloned.1.call-done.own_ref), channel_id=1, source_target_pairs={{0,8},{8,0},{16,24},{24,16},{32,40},{40,32},{48,56},{56,48},{64,72... | collective-permute-start | bytes 3932168 | tf_op jit(solution)/shard_map/ppermute | solution.py:137
  117.2 2.2 bitcast_dynamic-update-slice_fusion.7
  119.5 4.3 %all_to_all.20 = bf16[2,16,32,128]{3,2,1,0:T(8,128)(2,1)S(1)} all-to-all(bf16[2,16,32,128]{3,2,1,0:T(8,128)(2,1)S(1)} %broadcast_in_dim.48), channel_id=1, replica_groups={{0,8},{16,24},{32,40},{48,56},{64,72},{80,88},{96,104},{112,120},{128,1..., dimensions={0} | all-to-all | bytes 524288 | tf_op jit(solution)/shard_map/all_to_all | solution.py:153
  124.0 0.7 copy.27
  124.7 0.1 fusion.14
  124.9 0.4 convolution_convert_fusion
  125.3 1.4 maximum_maximum_fusion.q_ref
  126.7 1.1 copy-done.1
  127.7 11.2 %shard_map.82 = bf16[1024,128]{1,0:T(8,128)(2,1)} custom-call(bf16[1024,640]{1,0:T(8,128)(2,1)} %maximum_maximum_fusion.q_ref, bf16[512,128]{1,0:T(8,128)(2,1)} %bitcast.53, bf16[1024,640]{1,0:T(8,128)(2,1)} %all-gather.3.cloned.1.call-done.own_ref, bf16[1024,640]{1,0:T(8,128)(2,1)} %copy-done.1), custom_call_target="tpu_custom_call" | custom-call | tf_op jit(solution)/shard_map/pallas_call | solution.py:183
  139.0 17.3 %all_to_all.21 = bf16[8,128,128]{2,1,0:T(8,128)(2,1)} all-to-all(bf16[8,128,128]{2,1,0:T(8,128)(2,1)} %bitcast.46), channel_id=1, replica_groups=mesh['groups'=2,'ctx'=32,'tp'=8] {'tp'}, dimensions={0} | all-to-all | bytes 524288 | tf_op jit(solution)/shard_map/all_to_all | solution.py:192
  156.3 2.0 collective-permute-start.2
  158.3 4.6 %collective-permute-start.3 = (bf16[224,2048]{1,0:T(8,128)(2,1)S(1)}, bf16[224,2048]{1,0:T(8,128)(2,1)S(1)}, u32[]{:S(2)}, u32[]{:S(2)}) collective-permute-start(bf16[224,2048]{1,0:T(8,128)(2,1)S(1)} %bitcast.51), channel_id=1, source_target_pairs={{0,7},{1,0},{2,1},{3,2},{4,3},{5,4},{6,5},{7,6},{8,15},{9,8},{10,9... | collective-permute-start | bytes 2752520 | tf_op jit(solution)/shard_map/ppermute | solution.py:199
  162.9 17.0 %collective-permute-done.2 = bf16[224,2048]{1,0:T(8,128)(2,1)S(1)} collective-permute-done((bf16[224,2048]{1,0:T(8,128)(2,1)}, bf16[224,2048]{1,0:T(8,128)(2,1)S(1)}, u32[]{:S(2)}, u32[]{:S(2)}) %collective-permute-start.2) | collective-permute-done | bytes 917536 | tf_op jit(solution)/shard_map/ppermute | solution.py:198
  180.0 1.9 collective-permute-start.4
  181.9 4.6 %collective-permute-start.5 = (bf16[224,2048]{1,0:T(8,128)(2,1)S(1)}, bf16[224,2048]{1,0:T(8,128)(2,1)S(1)}, u32[]{:S(2)}, u32[]{:S(2)}) collective-permute-start(bf16[224,2048]{1,0:T(8,128)(2,1)S(1)} %collective-permute-done.3), channel_id=1, source_target_pairs={{0,7},{1,0},{2,1},{3,2},{4,3},{5,4},{6,5},{7,6},{8,15},{9,8},{10,9... | collective-permute-start | bytes 2752520 | tf_op jit(solution)/shard_map/ppermute | solution.py:199
  186.5 1.0 bitcast_dynamic-update-slice_fusion.6
  187.5 1.0 bitcast_dynamic-update-slice_fusion.5
  188.5 14.0 %collective-permute-done.4 = bf16[224,2048]{1,0:T(8,128)(2,1)S(1)} collective-permute-done((bf16[224,2048]{1,0:T(8,128)(2,1)S(1)}, bf16[224,2048]{1,0:T(8,128)(2,1)S(1)}, u32[]{:S(2)}, u32[]{:S(2)}) %collective-permute-start.4) | collective-permute-done | bytes 917536 | tf_op jit(solution)/shard_map/ppermute | solution.py:198
  202.6 1.9 collective-permute-start.6
  204.5 4.6 %collective-permute-start.7 = (bf16[224,2048]{1,0:T(8,128)(2,1)S(1)}, bf16[224,2048]{1,0:T(8,128)(2,1)S(1)}, u32[]{:S(2)}, u32[]{:S(2)}) collective-permute-start(bf16[224,2048]{1,0:T(8,128)(2,1)S(1)} %collective-permute-done.5), channel_id=1, source_target_pairs={{0,7},{1,0},{2,1},{3,2},{4,3},{5,4},{6,5},{7,6},{8,15},{9,8},{10,9... | collective-permute-start | bytes 2752520 | tf_op jit(solution)/shard_map/ppermute | solution.py:199
  209.1 1.0 bitcast_dynamic-update-slice_fusion.4
  210.1 1.0 bitcast_dynamic-update-slice_fusion.3
  211.1 13.2 %collective-permute-done.6 = bf16[224,2048]{1,0:T(8,128)(2,1)S(1)} collective-permute-done((bf16[224,2048]{1,0:T(8,128)(2,1)S(1)}, bf16[224,2048]{1,0:T(8,128)(2,1)S(1)}, u32[]{:S(2)}, u32[]{:S(2)}) %collective-permute-start.6) | collective-permute-done | bytes 917536 | tf_op jit(solution)/shard_map/ppermute | solution.py:198
  224.3 1.1 bitcast_dynamic-update-slice_fusion.2
  225.4 1.0 bitcast_dynamic-update-slice_fusion.1.weights
  226.4 8.7 %all-gather.5.cloned.1.call-done = bf16[32,1024,128]{2,1,0:T(8,128)(2,1)} async-done(((bf16[1,1024,128]{2,1,0:T(8,128)(2,1)}), bf16[32,1024,128]{2,1,0:T(8,128)(2,1)}) %all-gather.5.cloned.1.call-update) | async-done | bytes 8388624 | tf_op jit(solution)/shard_map/all_gather | solution.py:195
  235.1 7.7 %shard_map.83 = bf16[224,256]{1,0:T(8,128)(2,1)} custom-call(bf16[16,2,8,128,128]{4,3,2,1,0:T(8,128)(2,1)} %bitcast.44, bf16[8,224,2048]{2,1,0:T(8,128)(2,1)} %bitcast_dynamic-update-slice_fusion.1.weights), custom_call_target="tpu_custom_call" | custom-call | tf_op jit(solution)/shard_map/pallas_call | solution.py:205
  (33 shorter events, 1.1 us)
Async XLA Ops:
  6.5 62.2 %copy-start = (bf16[64,2048]{1,0:T(8,128)(2,1)S(1)}, bf16[64,2048]{1,0:T(8,128)(2,1)}, u32[]{:S(2)}) copy-start(bf16[64,2048]{1,0:T(8,128)(2,1)} %param.8) | copy-start | bytes 786436
  6.6 72.0 %copy-start.2 = (bf16[2048,224]{0,1:T(8,128)(2,1)S(1)}, bf16[2048,224]{0,1:T(8,128)(2,1)}, u32[]{:S(2)}) copy-start(bf16[2048,224]{0,1:T(8,128)(2,1)} %param.15) | copy-start | bytes 2752516
  10.6 56.2 %all-to-all-start.2 = ((bf16[16,8,640]{2,1,0:T(8,128)(2,1)}), bf16[16,8,640]{2,1,0:T(8,128)(2,1)S(1)}, u32[]{:S(2)}, u32[]{:S(2)}) async-start(bf16[16,8,640]{2,1,0:T(8,128)(2,1)} %broadcast_in_dim.51), calls=%async_computation.2 | async-start | bytes 327680 | tf_op jit(solution)/shard_map/all_to_all | solution.py:132
  54.8 56.9 %all-gather.3.cloned.1.call-start = ((), (), s32[]{:S(2)}) async-start(), calls=%async_computation.4 | async-start | bytes 1474560 | tf_op jit(solution)/shard_map/all_gather | solution.py:135
  66.8 0.7 copy-start.3
  70.6 48.8 %all-to-all-start = ((bf16[16,128,128]{2,1,0:T(8,128)(2,1)}), bf16[16,128,128]{2,1,0:T(8,128)(2,1)S(1)}, u32[]{:S(2)}, u32[]{:S(2)}) async-start(bf16[16,128,128]{2,1,0:T(8,128)(2,1)} %pad_maximum_fusion), calls=%async_computation | async-start | bytes 1048576 | tf_op jit(solution)/shard_map/all_to_all | solution.py:146
  78.4 156.6 %all-gather.5.cloned.1.call-start = ((), (), s32[]{:S(2)}) async-start(), calls=%async_computation.5 | async-start | bytes 8650752 | tf_op jit(solution)/shard_map/all_gather | solution.py:195
  78.5 38.7 %collective-permute-start.1 = (bf16[224,2048]{1,0:T(8,128)(2,1)S(1)}, bf16[224,2048]{1,0:T(8,128)(2,1)}, u32[]{:S(2)}, u32[]{:S(2)}) collective-permute-start(bf16[224,2048]{1,0:T(8,128)(2,1)S(1)} %bitcast.50), channel_id=1, source_target_pairs={{0,1},{1,2},{2,3},{3,4},{4,5},{5,6},{6,7},{7,0},{8,9},{9,10},{10,1... | collective-permute-start | bytes 2752520 | tf_op jit(solution)/shard_map/ppermute | solution.py:176
  111.7 14.9 %collective-permute-start = (bf16[1024,640]{1,0:T(8,128)(2,1)}, bf16[1024,640]{1,0:T(8,128)(2,1)S(1)}, u32[]{:S(2)}, u32[]{:S(2)}) collective-permute-start(bf16[1024,640]{1,0:T(8,128)(2,1)} %all-gather.3.cloned.1.call-done.own_ref), channel_id=1, source_target_pairs={{0,8},{8,0},{16,24},{24,16},{32,40},{40,32},{48,56},{56,48},{64,72... | collective-permute-start | bytes 3932168 | tf_op jit(solution)/shard_map/ppermute | solution.py:137
  126.6 1.1 copy-start.1
  156.3 23.7 %collective-permute-start.2 = (bf16[224,2048]{1,0:T(8,128)(2,1)}, bf16[224,2048]{1,0:T(8,128)(2,1)S(1)}, u32[]{:S(2)}, u32[]{:S(2)}) collective-permute-start(bf16[224,2048]{1,0:T(8,128)(2,1)} %collective-permute-done.1), channel_id=1, source_target_pairs={{0,1},{1,2},{2,3},{3,4},{4,5},{5,6},{6,7},{7,0},{8,9},{9,10},{10,1... | collective-permute-start | bytes 2752520 | tf_op jit(solution)/shard_map/ppermute | solution.py:198
  158.3 23.7 %collective-permute-start.3 = (bf16[224,2048]{1,0:T(8,128)(2,1)S(1)}, bf16[224,2048]{1,0:T(8,128)(2,1)S(1)}, u32[]{:S(2)}, u32[]{:S(2)}) collective-permute-start(bf16[224,2048]{1,0:T(8,128)(2,1)S(1)} %bitcast.51), channel_id=1, source_target_pairs={{0,7},{1,0},{2,1},{3,2},{4,3},{5,4},{6,5},{7,6},{8,15},{9,8},{10,9... | collective-permute-start | bytes 2752520 | tf_op jit(solution)/shard_map/ppermute | solution.py:199
  180.0 22.6 %collective-permute-start.4 = (bf16[224,2048]{1,0:T(8,128)(2,1)S(1)}, bf16[224,2048]{1,0:T(8,128)(2,1)S(1)}, u32[]{:S(2)}, u32[]{:S(2)}) collective-permute-start(bf16[224,2048]{1,0:T(8,128)(2,1)S(1)} %collective-permute-done.2), channel_id=1, source_target_pairs={{0,1},{1,2},{2,3},{3,4},{4,5},{5,6},{6,7},{7,0},{8,9},{9,10},{10,1... | collective-permute-start | bytes 2752520 | tf_op jit(solution)/shard_map/ppermute | solution.py:198
  181.9 22.6 %collective-permute-start.5 = (bf16[224,2048]{1,0:T(8,128)(2,1)S(1)}, bf16[224,2048]{1,0:T(8,128)(2,1)S(1)}, u32[]{:S(2)}, u32[]{:S(2)}) collective-permute-start(bf16[224,2048]{1,0:T(8,128)(2,1)S(1)} %collective-permute-done.3), channel_id=1, source_target_pairs={{0,7},{1,0},{2,1},{3,2},{4,3},{5,4},{6,5},{7,6},{8,15},{9,8},{10,9... | collective-permute-start | bytes 2752520 | tf_op jit(solution)/shard_map/ppermute | solution.py:199
  202.6 21.7 %collective-permute-start.6 = (bf16[224,2048]{1,0:T(8,128)(2,1)S(1)}, bf16[224,2048]{1,0:T(8,128)(2,1)S(1)}, u32[]{:S(2)}, u32[]{:S(2)}) collective-permute-start(bf16[224,2048]{1,0:T(8,128)(2,1)S(1)} %collective-permute-done.4), channel_id=1, source_target_pairs={{0,1},{1,2},{2,3},{3,4},{4,5},{5,6},{6,7},{7,0},{8,9},{9,10},{10,1... | collective-permute-start | bytes 2752520 | tf_op jit(solution)/shard_map/ppermute | solution.py:198
  204.5 20.9 %collective-permute-start.7 = (bf16[224,2048]{1,0:T(8,128)(2,1)S(1)}, bf16[224,2048]{1,0:T(8,128)(2,1)S(1)}, u32[]{:S(2)}, u32[]{:S(2)}) collective-permute-start(bf16[224,2048]{1,0:T(8,128)(2,1)S(1)} %collective-permute-done.5), channel_id=1, source_target_pairs={{0,7},{1,0},{2,1},{3,2},{4,3},{5,4},{6,5},{7,6},{8,15},{9,8},{10,9... | collective-permute-start | bytes 2752520 | tf_op jit(solution)/shard_map/ppermute | solution.py:199
Sparse Core Ops, SparseCore 0:
  67.6 44.0 all-gather.2
  156.4 78.6 all-gather.4

commit v4 on v3

--- a/solution.py
+++ b/solution.py
@@ -150,14 +150,11 @@
     q_parts = came[:, :toks].reshape(chips * toks, nope)
     q_rot = came[:, toks:cut]
     q_rot = jnp.concatenate([q_rot[:, :, :rope], q_rot[:, :, rope:]], axis=1).reshape(-1, rope)
+    both = jnp.broadcast_to(came[None, :, cut:], (CORES, chips, k_rows + v_rows, LANES))
     both = lax.all_to_all(
-        jnp.broadcast_to(came[None, :, cut:], (CORES, chips, k_rows + v_rows, LANES)),
-        "ctx",
-        split_axis=0,
-        concat_axis=0,
-        tiled=True,
-        axis_index_groups=one_chip,
-    ).transpose(1, 0, 2, 3)
+        both, "ctx", split_axis=0, concat_axis=0, tiled=True, axis_index_groups=one_chip
+    )
+    both = both.transpose(1, 0, 2, 3)
     up_key = both[:, :, :k_rows].reshape(nope, lat)
     up_value = both[:, :, k_rows:].reshape(lat, v_dim)
     q_lat = jnp.dot(q_parts, up_key, preferred_element_type=jnp.float32).astype(jnp.bfloat16)
@@ -188,7 +185,6 @@
         scratch_shapes=[pltpu.VMEM((chips, planes, share, LANES), jnp.float32)],
     )(queries, up_value, own_keys, other_keys)
 
-    head_out, all_w, lower, upper = lax.optimization_barrier((head_out, all_w, lower, upper))
     by_plane = lax.all_to_all(
         head_out.reshape(planes, -1, v_dim), "tp", split_axis=0, concat_axis=0, tiled=True
     )
@@ -201,7 +197,7 @@
 
     out_toks = gathered.shape[3] * CORES
     columns = w_out.shape[1]
-    steps = 4
+    steps = 8
     out = pl.pallas_call(
         functools.partial(project, chips, planes, toks, steps),
         out_shape=jax.ShapeDtypeStruct((columns, out_toks), jnp.bfloat16),

time: 251 us -> 257 us (1.024)
  waiting for transfers between devices: 87.4 us -> 95.5 us
    ppermute x1, waiting for transfers between devices: 0.01 us -> 16.8 us  [on_device(): lower = lax.ppermute(own_w, 'tp', right)]
    all_gather x1, waiting for transfers between devices: 8.69 us -> 0.01 us  [on_device(): gathered = lax.all_gather(by_plane.reshape(-1, v_dim), 'ctx', axis=0)]
    all_gather x1, waiting for transfers between devices: 24.6 us -> 29.8 us  [on_device(): lax.all_gather(own_keys.reshape(chips * share, -1), 'tp', axis=0, tiled=T...]
    ppermute x3, waiting for transfers between devices: 44.3 us -> 40.3 us  [on_device(): lower = lax.ppermute(lower, 'tp', right)]
  transfers between devices with their start and end apart: 12 -> 12, of which waited for: 6 -> 6; matrix products, arithmetic and copies ran while one was open for 9% -> 8% of each run, Pallas kernels for 0% -> 0%
where the time goes in v4:
time: 257 us; the launch traced here: 254 us
  waiting for transfers between devices  95.5 us (37%)
  starting transfers between devices  80.6 us (31%)
  local copies, waits for them, and re-layouts  19.6 us (8%)
  blocking collectives  19.1 us (7%)
  Pallas kernels  18.8 us (7%)
  between operations  13.8 us (5%)
  other arithmetic  6.03 us (2%)
    all_to_all x1, starting transfers between devices, on_device(): lax.all_to_all(own_keys, 'ctx', split_axis=0, concat_axis=0, tiled=True,...  44.2 us
    ppermute x3, waiting for transfers between devices, on_device(): lower = lax.ppermute(lower, 'tp', right)  40.3 us
    all_gather x1, waiting for transfers between devices, on_device(): lax.all_gather(own_keys.reshape(chips * share, -1), 'tp', axis=0, tiled=T...  29.8 us
    ppermute x1, waiting for transfers between devices, on_device(): lower = lax.ppermute(own_w, 'tp', right)  16.8 us
    all_to_all x1, blocking collectives, on_device(): lax.all_to_all(head_out.reshape(planes, -1, v_dim), 'tp', split_axis=0, c...  15.4 us
    ppermute x3, starting transfers between devices, on_device(): upper = lax.ppermute(upper, 'tp', left)  13.8 us
    pallas_call x1, Pallas kernels, on_device(): pl.pallas_call(functools.partial(attend, chips, planes, toks, lat, scale,...  11.2 us
    all_to_all x1, waiting for transfers between devices, on_device(): lax.all_to_all(own_keys, 'ctx', split_axis=0, concat_axis=0, tiled=True,...  8.5 us
  transfers between devices with their start and end apart: 12, of which 6 were waited for; matrix products, arithmetic and copies ran while one was open for 8% of the time, Pallas kernels for 0%

profile of v4, /device:TPU:65, one launch (start us, length us, event | category | flops | bytes accessed | tf_op | source)
XLA Modules:
  0.0 253.7 jit_solution(17971976385823045848)
XLA Ops:
  6.6 0.8 fusion.13
  7.3 0.7 convert_bitcast_fusion
  8.1 0.7 constant_dynamic-slice_fusion
  9.0 0.7 constant_dynamic-slice_fusion.1
  9.9 0.7 broadcast_in_dim.51
  10.6 44.2 %all-to-all-start.2 = ((bf16[16,8,640]{2,1,0:T(8,128)(2,1)}), bf16[16,8,640]{2,1,0:T(8,128)(2,1)S(1)}, u32[]{:S(2)}, u32[]{:S(2)}) async-start(bf16[16,8,640]{2,1,0:T(8,128)(2,1)} %broadcast_in_dim.51), calls=%async_computation.2 | async-start | bytes 327680 | tf_op jit(solution)/shard_map/all_to_all | solution.py:132
  54.9 0.7 convert_element_type.25
  55.5 0.2 multiply_cosine_fusion
  55.7 1.1 reshape.84
  56.8 0.9 reshape.85
  57.7 0.1 fusion.17
  57.9 0.2 fusion.1
  58.1 0.2 maximum_bitcast_fusion
  58.2 8.5 %all-to-all-done.2 = bf16[16,8,640]{2,1,0:T(8,128)(2,1)S(1)} async-done(((bf16[16,8,640]{2,1,0:T(8,128)(2,1)}), bf16[16,8,640]{2,1,0:T(8,128)(2,1)S(1)}, u32[]{:S(2)}, u32[]{:S(2)}) %all-to-all-start.2) | async-done | bytes 163872 | tf_op jit(solution)/shard_map/all_to_all | solution.py:132
  66.7 0.7 copy-done.3
  67.6 1.8 pad_maximum_fusion
  69.3 7.9 %all-to-all-start = ((bf16[16,128,128]{2,1,0:T(8,128)(2,1)}), bf16[16,128,128]{2,1,0:T(8,128)(2,1)S(1)}, u32[]{:S(2)}, u32[]{:S(2)}) async-start(bf16[16,128,128]{2,1,0:T(8,128)(2,1)} %pad_maximum_fusion), calls=%async_computation | async-start | bytes 1048576 | tf_op jit(solution)/shard_map/all_to_all | solution.py:146
  77.3 29.8 %all-gather.3.cloned.1.call-done.own_ref = bf16[1024,640]{1,0:T(8,128)(2,1)} async-done(((bf16[128,640]{1,0:T(8,128)(2,1)}), bf16[1024,640]{1,0:T(8,128)(2,1)}) %all-gather.3.cloned.1.call-update) | async-done | bytes 1310736 | tf_op jit(solution)/shard_map/all_gather | solution.py:135
  107.1 6.5 %collective-permute-start = (bf16[1024,640]{1,0:T(8,128)(2,1)}, bf16[1024,640]{1,0:T(8,128)(2,1)S(1)}, u32[]{:S(2)}, u32[]{:S(2)}) collective-permute-start(bf16[1024,640]{1,0:T(8,128)(2,1)} %all-gather.3.cloned.1.call-done.own_ref), channel_id=1, source_target_pairs={{0,8},{8,0},{16,24},{24,16},{32,40},{40,32},{48,56},{56,48},{64,72... | collective-permute-start | bytes 3932168 | tf_op jit(solution)/shard_map/ppermute | solution.py:137
  113.8 3.6 %all_to_all.20 = bf16[2,16,32,128]{3,2,1,0:T(8,128)(2,1)S(1)} all-to-all(bf16[2,16,32,128]{3,2,1,0:T(8,128)(2,1)S(1)} %broadcast_in_dim.48), channel_id=1, replica_groups={{0,8},{16,24},{32,40},{48,56},{64,72},{80,88},{96,104},{112,120},{128,1..., dimensions={0} | all-to-all | bytes 524288 | tf_op jit(solution)/shard_map/all_to_all | solution.py:154
  117.6 0.7 copy.27
  118.2 0.1 fusion.14
  118.4 0.4 convolution_convert_fusion
  118.9 1.4 maximum_maximum_fusion.q_ref
  120.2 1.1 copy-done.1
  121.3 11.2 %shard_map.82 = bf16[1024,128]{1,0:T(8,128)(2,1)} custom-call(bf16[1024,640]{1,0:T(8,128)(2,1)} %maximum_maximum_fusion.q_ref, bf16[512,128]{1,0:T(8,128)(2,1)} %bitcast.53, bf16[1024,640]{1,0:T(8,128)(2,1)} %all-gather.3.cloned.1.call-done.own_ref, bf16[1024,640]{1,0:T(8,128)(2,1)} %copy-done.1), custom_call_target="tpu_custom_call" | custom-call | tf_op jit(solution)/shard_map/pallas_call | solution.py:180
  132.5 15.4 %all_to_all.21 = bf16[8,128,128]{2,1,0:T(8,128)(2,1)} all-to-all(bf16[8,128,128]{2,1,0:T(8,128)(2,1)} %bitcast.46), channel_id=1, replica_groups=mesh['groups'=2,'ctx'=32,'tp'=8] {'tp'}, dimensions={0} | all-to-all | bytes 524288 | tf_op jit(solution)/shard_map/all_to_all | solution.py:188
  148.1 2.0 collective-permute-start.1
  150.0 4.6 %collective-permute-start.3 = (bf16[224,2048]{1,0:T(8,128)(2,1)S(1)}, bf16[224,2048]{1,0:T(8,128)(2,1)S(1)}, u32[]{:S(2)}, u32[]{:S(2)}) collective-permute-start(bf16[224,2048]{1,0:T(8,128)(2,1)S(1)} %bitcast.51), channel_id=1, source_target_pairs={{0,7},{1,0},{2,1},{3,2},{4,3},{5,4},{6,5},{7,6},{8,15},{9,8},{10,9... | collective-permute-start | bytes 2752520 | tf_op jit(solution)/shard_map/ppermute | solution.py:195
  154.7 16.8 %collective-permute-done.1 = bf16[224,2048]{1,0:T(8,128)(2,1)S(1)} collective-permute-done((bf16[224,2048]{1,0:T(8,128)(2,1)S(1)}, bf16[224,2048]{1,0:T(8,128)(2,1)S(1)}, u32[]{:S(2)}, u32[]{:S(2)}) %collective-permute-start.1) | collective-permute-done | bytes 917536 | tf_op jit(solution)/shard_map/ppermute | solution.py:173
  171.5 2.1 collective-permute-start.2
  173.6 4.6 %collective-permute-start.5 = (bf16[224,2048]{1,0:T(8,128)(2,1)S(1)}, bf16[224,2048]{1,0:T(8,128)(2,1)S(1)}, u32[]{:S(2)}, u32[]{:S(2)}) collective-permute-start(bf16[224,2048]{1,0:T(8,128)(2,1)S(1)} %collective-permute-done.3), channel_id=1, source_target_pairs={{0,7},{1,0},{2,1},{3,2},{4,3},{5,4},{6,5},{7,6},{8,15},{9,8},{10,9... | collective-permute-start | bytes 2752520 | tf_op jit(solution)/shard_map/ppermute | solution.py:195
  178.2 3.9 %broadcast_in_dim.52 = bf16[8,224,2048]{2,1,0:T(8,128)(2,1)} broadcast(bf16[]{:T(256)} %constant.80.clone.1), dimensions={} | broadcast | bytes 7340034 | tf_op jit(solution)/shard_map/broadcast_in_dim | solution.py:168
  182.1 1.1 bitcast_dynamic-update-slice_fusion
  183.2 1.0 bitcast_dynamic-update-slice_fusion.7
  184.2 9.9 %collective-permute-done.2 = bf16[224,2048]{1,0:T(8,128)(2,1)S(1)} collective-permute-done((bf16[224,2048]{1,0:T(8,128)(2,1)S(1)}, bf16[224,2048]{1,0:T(8,128)(2,1)S(1)}, u32[]{:S(2)}, u32[]{:S(2)}) %collective-permute-start.2) | collective-permute-done | bytes 917536 | tf_op jit(solution)/shard_map/ppermute | solution.py:194
  194.2 1.9 collective-permute-start.4
  196.1 4.6 %collective-permute-start.7 = (bf16[224,2048]{1,0:T(8,128)(2,1)S(1)}, bf16[224,2048]{1,0:T(8,128)(2,1)S(1)}, u32[]{:S(2)}, u32[]{:S(2)}) collective-permute-start(bf16[224,2048]{1,0:T(8,128)(2,1)S(1)} %collective-permute-done.5), channel_id=1, source_target_pairs={{0,7},{1,0},{2,1},{3,2},{4,3},{5,4},{6,5},{7,6},{8,15},{9,8},{10,9... | collective-permute-start | bytes 2752520 | tf_op jit(solution)/shard_map/ppermute | solution.py:195
  200.7 1.0 bitcast_dynamic-update-slice_fusion.6
  201.8 1.0 bitcast_dynamic-update-slice_fusion.5
  202.7 13.3 %collective-permute-done.4 = bf16[224,2048]{1,0:T(8,128)(2,1)S(1)} collective-permute-done((bf16[224,2048]{1,0:T(8,128)(2,1)S(1)}, bf16[224,2048]{1,0:T(8,128)(2,1)S(1)}, u32[]{:S(2)}, u32[]{:S(2)}) %collective-permute-start.4) | collective-permute-done | bytes 917536 | tf_op jit(solution)/shard_map/ppermute | solution.py:194
  216.1 1.9 collective-permute-start.6
  218.0 1.0 bitcast_dynamic-update-slice_fusion.4
  219.1 1.0 bitcast_dynamic-update-slice_fusion.3
  220.1 17.0 %collective-permute-done.6 = bf16[224,2048]{1,0:T(8,128)(2,1)S(1)} collective-permute-done((bf16[224,2048]{1,0:T(8,128)(2,1)S(1)}, bf16[224,2048]{1,0:T(8,128)(2,1)S(1)}, u32[]{:S(2)}, u32[]{:S(2)}) %collective-permute-start.6) | collective-permute-done | bytes 917536 | tf_op jit(solution)/shard_map/ppermute | solution.py:194
  237.1 1.1 bitcast_dynamic-update-slice_fusion.2
  238.2 1.0 bitcast_dynamic-update-slice_fusion.1.weights
  239.3 7.5 %shard_map.83 = bf16[224,256]{1,0:T(8,128)(2,1)} custom-call(bf16[16,2,8,128,128]{4,3,2,1,0:T(8,128)(2,1)} %bitcast.44, bf16[8,224,2048]{2,1,0:T(8,128)(2,1)} %bitcast_dynamic-update-slice_fusion.1.weights), custom_call_target="tpu_custom_call" | custom-call | tf_op jit(solution)/shard_map/pallas_call | solution.py:201
  (33 shorter events, 1.1 us)
Async XLA Ops:
  6.5 60.9 %copy-start = (bf16[64,2048]{1,0:T(8,128)(2,1)S(1)}, bf16[64,2048]{1,0:T(8,128)(2,1)}, u32[]{:S(2)}) copy-start(bf16[64,2048]{1,0:T(8,128)(2,1)} %param.8) | copy-start | bytes 786436
  10.6 56.2 %all-to-all-start.2 = ((bf16[16,8,640]{2,1,0:T(8,128)(2,1)}), bf16[16,8,640]{2,1,0:T(8,128)(2,1)S(1)}, u32[]{:S(2)}, u32[]{:S(2)}) async-start(bf16[16,8,640]{2,1,0:T(8,128)(2,1)} %broadcast_in_dim.51), calls=%async_computation.2 | async-start | bytes 327680 | tf_op jit(solution)/shard_map/all_to_all | solution.py:132
  54.8 52.3 %all-gather.3.cloned.1.call-start = ((), (), s32[]{:S(2)}) async-start(), calls=%async_computation.4 | async-start | bytes 1474560 | tf_op jit(solution)/shard_map/all_gather | solution.py:135
  66.7 0.7 copy-start.3
  69.3 78.7 %copy-start.2 = (bf16[2048,224]{0,1:T(8,128)(2,1)S(1)}, bf16[2048,224]{0,1:T(8,128)(2,1)}, u32[]{:S(2)}) copy-start(bf16[2048,224]{0,1:T(8,128)(2,1)} %param.15) | copy-start | bytes 2752516
  69.3 44.4 %all-to-all-start = ((bf16[16,128,128]{2,1,0:T(8,128)(2,1)}), bf16[16,128,128]{2,1,0:T(8,128)(2,1)S(1)}, u32[]{:S(2)}, u32[]{:S(2)}) async-start(bf16[16,128,128]{2,1,0:T(8,128)(2,1)} %pad_maximum_fusion), calls=%async_computation | async-start | bytes 1048576 | tf_op jit(solution)/shard_map/all_to_all | solution.py:146
  77.3 162.0 %all-gather.5.cloned.1.call-start = ((), (), s32[]{:S(2)}) async-start(), calls=%async_computation.5 | async-start | bytes 8650752 | tf_op jit(solution)/shard_map/all_gather | solution.py:191
  107.1 13.1 %collective-permute-start = (bf16[1024,640]{1,0:T(8,128)(2,1)}, bf16[1024,640]{1,0:T(8,128)(2,1)S(1)}, u32[]{:S(2)}, u32[]{:S(2)}) collective-permute-start(bf16[1024,640]{1,0:T(8,128)(2,1)} %all-gather.3.cloned.1.call-done.own_ref), channel_id=1, source_target_pairs={{0,8},{8,0},{16,24},{24,16},{32,40},{40,32},{48,56},{56,48},{64,72... | collective-permute-start | bytes 3932168 | tf_op jit(solution)/shard_map/ppermute | solution.py:137
  120.2 1.1 copy-start.1
  148.1 23.4 %collective-permute-start.1 = (bf16[224,2048]{1,0:T(8,128)(2,1)S(1)}, bf16[224,2048]{1,0:T(8,128)(2,1)S(1)}, u32[]{:S(2)}, u32[]{:S(2)}) collective-permute-start(bf16[224,2048]{1,0:T(8,128)(2,1)S(1)} %bitcast.50), channel_id=1, source_target_pairs={{0,1},{1,2},{2,3},{3,4},{4,5},{5,6},{6,7},{7,0},{8,9},{9,10},{10,1... | collective-permute-start | bytes 2752520 | tf_op jit(solution)/shard_map/ppermute | solution.py:173
  150.0 23.6 %collective-permute-start.3 = (bf16[224,2048]{1,0:T(8,128)(2,1)S(1)}, bf16[224,2048]{1,0:T(8,128)(2,1)S(1)}, u32[]{:S(2)}, u32[]{:S(2)}) collective-permute-start(bf16[224,2048]{1,0:T(8,128)(2,1)S(1)} %bitcast.51), channel_id=1, source_target_pairs={{0,7},{1,0},{2,1},{3,2},{4,3},{5,4},{6,5},{7,6},{8,15},{9,8},{10,9... | collective-permute-start | bytes 2752520 | tf_op jit(solution)/shard_map/ppermute | solution.py:195
  171.5 22.7 %collective-permute-start.2 = (bf16[224,2048]{1,0:T(8,128)(2,1)S(1)}, bf16[224,2048]{1,0:T(8,128)(2,1)S(1)}, u32[]{:S(2)}, u32[]{:S(2)}) collective-permute-start(bf16[224,2048]{1,0:T(8,128)(2,1)S(1)} %collective-permute-done.1), channel_id=1, source_target_pairs={{0,1},{1,2},{2,3},{3,4},{4,5},{5,6},{6,7},{7,0},{8,9},{9,10},{10,1... | collective-permute-start | bytes 2752520 | tf_op jit(solution)/shard_map/ppermute | solution.py:194
  173.6 22.5 %collective-permute-start.5 = (bf16[224,2048]{1,0:T(8,128)(2,1)S(1)}, bf16[224,2048]{1,0:T(8,128)(2,1)S(1)}, u32[]{:S(2)}, u32[]{:S(2)}) collective-permute-start(bf16[224,2048]{1,0:T(8,128)(2,1)S(1)} %collective-permute-done.3), channel_id=1, source_target_pairs={{0,7},{1,0},{2,1},{3,2},{4,3},{5,4},{6,5},{7,6},{8,15},{9,8},{10,9... | collective-permute-start | bytes 2752520 | tf_op jit(solution)/shard_map/ppermute | solution.py:195
  194.2 21.9 %collective-permute-start.4 = (bf16[224,2048]{1,0:T(8,128)(2,1)S(1)}, bf16[224,2048]{1,0:T(8,128)(2,1)S(1)}, u32[]{:S(2)}, u32[]{:S(2)}) collective-permute-start(bf16[224,2048]{1,0:T(8,128)(2,1)S(1)} %collective-permute-done.2), channel_id=1, source_target_pairs={{0,1},{1,2},{2,3},{3,4},{4,5},{5,6},{6,7},{7,0},{8,9},{9,10},{10,1... | collective-permute-start | bytes 2752520 | tf_op jit(solution)/shard_map/ppermute | solution.py:194
  196.1 42.1 %collective-permute-start.7 = (bf16[224,2048]{1,0:T(8,128)(2,1)S(1)}, bf16[224,2048]{1,0:T(8,128)(2,1)S(1)}, u32[]{:S(2)}, u32[]{:S(2)}) collective-permute-start(bf16[224,2048]{1,0:T(8,128)(2,1)S(1)} %collective-permute-done.5), channel_id=1, source_target_pairs={{0,7},{1,0},{2,1},{3,2},{4,3},{5,4},{6,5},{7,6},{8,15},{9,8},{10,9... | collective-permute-start | bytes 2752520 | tf_op jit(solution)/shard_map/ppermute | solution.py:195
  216.1 21.1 %collective-permute-start.6 = (bf16[224,2048]{1,0:T(8,128)(2,1)S(1)}, bf16[224,2048]{1,0:T(8,128)(2,1)S(1)}, u32[]{:S(2)}, u32[]{:S(2)}) collective-permute-start(bf16[224,2048]{1,0:T(8,128)(2,1)S(1)} %collective-permute-done.4), channel_id=1, source_target_pairs={{0,1},{1,2},{2,3},{3,4},{4,5},{5,6},{6,7},{7,0},{8,9},{9,10},{10,1... | collective-permute-start | bytes 2752520 | tf_op jit(solution)/shard_map/ppermute | solution.py:194
Sparse Core Ops, SparseCore 0:
  67.6 39.4 all-gather.2
  148.2 78.8 all-gather.4

commit v5 on v4

--- a/solution.py
+++ b/solution.py
@@ -44,17 +44,23 @@
         pos_buf[:, x] = own_pos[x]
     q_pos = pos_buf[...].reshape(chips * toks, LANES)[:, 0:1]
     factor = scale * 1.4426950408889634
-    for b in range(chips * toks // block):
-        rows = slice(b * block, (b + 1) * block)
-        scores = lax.dot_general(q_ref[rows, :], all_keys, nt, preferred_element_type=jnp.float32)
-        scores = jnp.where(key_pos <= q_pos[rows], scores, -1e30)
+    blocks = [slice(at, at + block) for at in range(0, chips * toks, block)]
+
+    def score(rows):
+        return lax.dot_general(q_ref[rows, :], all_keys, nt, preferred_element_type=jnp.float32)
+
+    following = score(blocks[0])
+    for b, rows in enumerate(blocks):
+        scores = jnp.where(key_pos <= q_pos[rows], following, -1e30)
+        if b + 1 < len(blocks):
+            following = score(blocks[b + 1])
         top = jnp.max(scores, axis=1, keepdims=True)
         weights = jnp.exp2((scores - top) * factor)
         total = jnp.sum(weights, axis=1, keepdims=True)
         mixed = jnp.dot(
             weights.astype(jnp.bfloat16), all_keys[:, :lat], preferred_element_type=jnp.float32
         )
-        o_lat = (mixed / total).astype(jnp.bfloat16)
+        o_lat = (mixed * (1.0 / total)).astype(jnp.bfloat16)
         out_ref[rows, :] = jnp.dot(
             o_lat, wv_ref[...], preferred_element_type=jnp.float32
         ).astype(jnp.bfloat16)
@@ -183,6 +189,7 @@
         in_specs=[vmem, vmem, vmem, vmem],
         out_specs=vmem,
         scratch_shapes=[pltpu.VMEM((chips, planes, share, LANES), jnp.float32)],
+        compiler_params=pltpu.CompilerParams(vmem_limit_bytes=20 * 2**20),
     )(queries, up_value, own_keys, other_keys)
 
     by_plane = lax.all_to_all(

time: 257 us -> 253 us (0.984)
  Pallas kernels: 18.8 us -> 14.6 us
    pallas_call x1, Pallas kernels: 11.2 us -> 7.04 us  [on_device(): pl.pallas_call(functools.partial(attend, chips, planes, toks, lat, scale,...]
  transfers between devices with their start and end apart: 12 -> 12, of which waited for: 6 -> 6; matrix products, arithmetic and copies ran while one was open for 8% -> 9% of each run, Pallas kernels for 0% -> 0%
where the time goes in v5:
time: 253 us; the launch traced here: 250 us
  waiting for transfers between devices  94.4 us (37%)
  starting transfers between devices  80.5 us (32%)
  local copies, waits for them, and re-layouts  21.2 us (8%)
  blocking collectives  19.1 us (8%)
  Pallas kernels  14.6 us (6%)
  between operations  13.8 us (5%)
  other arithmetic  4.97 us (2%)
    all_to_all x1, starting transfers between devices, on_device(): lax.all_to_all(own_keys, 'ctx', split_axis=0, concat_axis=0, tiled=True,...  44.2 us
    ppermute x3, waiting for transfers between devices, on_device(): lower = lax.ppermute(lower, 'tp', right)  38.7 us
    all_gather x1, waiting for transfers between devices, on_device(): lax.all_gather(own_keys.reshape(chips * share, -1), 'tp', axis=0, tiled=T...  30 us
    ppermute x1, waiting for transfers between devices, on_device(): lower = lax.ppermute(own_w, 'tp', right)  17 us
    all_to_all x1, blocking collectives, on_device(): lax.all_to_all(head_out.reshape(planes, -1, v_dim), 'tp', split_axis=0, c...  15.4 us
    ppermute x3, starting transfers between devices, on_device(): upper = lax.ppermute(upper, 'tp', left)  14 us
    dynamic_update_slice x8, local copies, waits for them, and re-layouts, placed(): lax.dynamic_update_slice(stack, block[None], ((plane + shift) % planes, 0...  9.51 us
    all_to_all x1, waiting for transfers between devices, on_device(): lax.all_to_all(own_keys, 'ctx', split_axis=0, concat_axis=0, tiled=True,...  8.5 us
  transfers between devices with their start and end apart: 12, of which 6 were waited for; matrix products, arithmetic and copies ran while one was open for 9% of the time, Pallas kernels for 0%

profile of v5, /device:TPU:65, one launch (start us, length us, event | category | flops | bytes accessed | tf_op | source)
XLA Modules:
  0.0 249.8 jit_solution(3045934060985106899)
XLA Ops:
  6.6 0.8 fusion.13
  7.3 0.7 convert_bitcast_fusion
  8.1 0.7 constant_dynamic-slice_fusion
  9.0 0.7 constant_dynamic-slice_fusion.1
  9.9 0.7 broadcast_in_dim.51
  10.6 44.2 %all-to-all-start.2 = ((bf16[16,8,640]{2,1,0:T(8,128)(2,1)}), bf16[16,8,640]{2,1,0:T(8,128)(2,1)S(1)}, u32[]{:S(2)}, u32[]{:S(2)}) async-start(bf16[16,8,640]{2,1,0:T(8,128)(2,1)} %broadcast_in_dim.51), calls=%async_computation.2 | async-start | bytes 327680 | tf_op jit(solution)/shard_map/all_to_all | solution.py:138
  54.9 0.7 convert_element_type.25
  55.5 0.2 multiply_cosine_fusion
  55.7 1.1 reshape.84
  56.8 0.9 reshape.85
  57.7 0.1 fusion.17
  57.9 0.2 fusion.1
  58.1 0.2 maximum_bitcast_fusion
  58.2 8.5 %all-to-all-done.2 = bf16[16,8,640]{2,1,0:T(8,128)(2,1)S(1)} async-done(((bf16[16,8,640]{2,1,0:T(8,128)(2,1)}), bf16[16,8,640]{2,1,0:T(8,128)(2,1)S(1)}, u32[]{:S(2)}, u32[]{:S(2)}) %all-to-all-start.2) | async-done | bytes 163872 | tf_op jit(solution)/shard_map/all_to_all | solution.py:138
  66.7 0.7 copy-done.2
  67.5 1.8 pad_maximum_fusion
  69.3 7.8 %all-to-all-start = ((bf16[16,128,128]{2,1,0:T(8,128)(2,1)}), bf16[16,128,128]{2,1,0:T(8,128)(2,1)S(1)}, u32[]{:S(2)}, u32[]{:S(2)}) async-start(bf16[16,128,128]{2,1,0:T(8,128)(2,1)} %pad_maximum_fusion), calls=%async_computation | async-start | bytes 1048576 | tf_op jit(solution)/shard_map/all_to_all | solution.py:152
  77.2 30.0 %all-gather.3.cloned.1.call-done.own_ref = bf16[1024,640]{1,0:T(8,128)(2,1)} async-done(((bf16[128,640]{1,0:T(8,128)(2,1)}), bf16[1024,640]{1,0:T(8,128)(2,1)}) %all-gather.3.cloned.1.call-update) | async-done | bytes 1310736 | tf_op jit(solution)/shard_map/all_gather | solution.py:141
  107.2 6.5 %collective-permute-start = (bf16[1024,640]{1,0:T(8,128)(2,1)}, bf16[1024,640]{1,0:T(8,128)(2,1)S(1)}, u32[]{:S(2)}, u32[]{:S(2)}) collective-permute-start(bf16[1024,640]{1,0:T(8,128)(2,1)} %all-gather.3.cloned.1.call-done.own_ref), channel_id=1, source_target_pairs={{0,8},{8,0},{16,24},{24,16},{32,40},{40,32},{48,56},{56,48},{64,72... | collective-permute-start | bytes 3932168 | tf_op jit(solution)/shard_map/ppermute | solution.py:143
  113.9 3.6 %all_to_all.20 = bf16[2,16,32,128]{3,2,1,0:T(8,128)(2,1)S(1)} all-to-all(bf16[2,16,32,128]{3,2,1,0:T(8,128)(2,1)S(1)} %broadcast_in_dim.48), channel_id=1, replica_groups={{0,8},{16,24},{32,40},{48,56},{64,72},{80,88},{96,104},{112,120},{128,1..., dimensions={0} | all-to-all | bytes 524288 | tf_op jit(solution)/shard_map/all_to_all | solution.py:160
  117.5 0.7 fusion.15
  118.2 0.7 reshape.87
  118.9 0.9 copy.27
  120.1 1.3 convolution_convert_fusion
  121.4 0.3 maximum_maximum_fusion.q_ref
  121.7 7.0 %shard_map.82 = bf16[1024,128]{1,0:T(8,128)(2,1)S(1)} custom-call(bf16[1024,640]{1,0:T(8,128)(2,1)S(1)} %maximum_maximum_fusion.q_ref, bf16[512,128]{1,0:T(8,128)(2,1)S(1)} %bitcast.45, bf16[1024,640]{1,0:T(8,128)(2,1)S(1)} %copy-done.1, bf16[1024,640]{1,0:T(8,128)(2,1)S(1)} %collective-permute-done.other_ref), custom_call_target="tpu_custom_call" | custom-call | tf_op jit(solution)/shard_map/pallas_call | solution.py:186
  128.8 15.4 %all_to_all.21 = bf16[8,128,128]{2,1,0:T(8,128)(2,1)} all-to-all(bf16[8,128,128]{2,1,0:T(8,128)(2,1)S(1)} %bitcast.44), channel_id=1, replica_groups=mesh['groups'=2,'ctx'=32,'tp'=8] {'tp'}, dimensions={0} | all-to-all | bytes 524288 | tf_op jit(solution)/shard_map/all_to_all | solution.py:195
  144.3 2.0 collective-permute-start.1
  146.2 4.6 %collective-permute-start.3 = (bf16[224,2048]{1,0:T(8,128)(2,1)}, bf16[224,2048]{1,0:T(8,128)(2,1)S(1)}, u32[]{:S(2)}, u32[]{:S(2)}) collective-permute-start(bf16[224,2048]{1,0:T(8,128)(2,1)} %bitcast.52), channel_id=1, source_target_pairs={{0,7},{1,0},{2,1},{3,2},{4,3},{5,4},{6,5},{7,6},{8,15},{9,8},{10,9... | collective-permute-start | bytes 2752520 | tf_op jit(solution)/shard_map/ppermute | solution.py:202
  151.0 17.0 %collective-permute-done.1 = bf16[224,2048]{1,0:T(8,128)(2,1)S(1)} collective-permute-done((bf16[224,2048]{1,0:T(8,128)(2,1)}, bf16[224,2048]{1,0:T(8,128)(2,1)S(1)}, u32[]{:S(2)}, u32[]{:S(2)}) %collective-permute-start.1) | collective-permute-done | bytes 917536 | tf_op jit(solution)/shard_map/ppermute | solution.py:179
  168.0 1.9 collective-permute-start.2
  169.9 4.8 %collective-permute-start.5 = (bf16[224,2048]{1,0:T(8,128)(2,1)S(1)}, bf16[224,2048]{1,0:T(8,128)(2,1)S(1)}, u32[]{:S(2)}, u32[]{:S(2)}) collective-permute-start(bf16[224,2048]{1,0:T(8,128)(2,1)S(1)} %collective-permute-done.3), channel_id=1, source_target_pairs={{0,7},{1,0},{2,1},{3,2},{4,3},{5,4},{6,5},{7,6},{8,15},{9,8},{10,9... | collective-permute-start | bytes 2752520 | tf_op jit(solution)/shard_map/ppermute | solution.py:202
  174.7 3.9 %broadcast_in_dim.52 = bf16[8,224,2048]{2,1,0:T(8,128)(2,1)} broadcast(bf16[]{:T(256)} %constant.80.clone.1), dimensions={} | broadcast | bytes 7340034 | tf_op jit(solution)/shard_map/broadcast_in_dim | solution.py:174
  178.6 2.3 bitcast_dynamic-update-slice_fusion
  180.9 1.0 bitcast_dynamic-update-slice_fusion.7
  181.9 8.7 %collective-permute-done.2 = bf16[224,2048]{1,0:T(8,128)(2,1)S(1)} collective-permute-done((bf16[224,2048]{1,0:T(8,128)(2,1)S(1)}, bf16[224,2048]{1,0:T(8,128)(2,1)S(1)}, u32[]{:S(2)}, u32[]{:S(2)}) %collective-permute-start.2) | collective-permute-done | bytes 917536 | tf_op jit(solution)/shard_map/ppermute | solution.py:201
  190.6 1.9 collective-permute-start.4
  192.5 4.6 %collective-permute-start.7 = (bf16[224,2048]{1,0:T(8,128)(2,1)S(1)}, bf16[224,2048]{1,0:T(8,128)(2,1)S(1)}, u32[]{:S(2)}, u32[]{:S(2)}) collective-permute-start(bf16[224,2048]{1,0:T(8,128)(2,1)S(1)} %collective-permute-done.5), channel_id=1, source_target_pairs={{0,7},{1,0},{2,1},{3,2},{4,3},{5,4},{6,5},{7,6},{8,15},{9,8},{10,9... | collective-permute-start | bytes 2752520 | tf_op jit(solution)/shard_map/ppermute | solution.py:202
  197.2 1.0 bitcast_dynamic-update-slice_fusion.6
  198.2 1.0 bitcast_dynamic-update-slice_fusion.5
  199.2 13.2 %collective-permute-done.4 = bf16[224,2048]{1,0:T(8,128)(2,1)S(1)} collective-permute-done((bf16[224,2048]{1,0:T(8,128)(2,1)S(1)}, bf16[224,2048]{1,0:T(8,128)(2,1)S(1)}, u32[]{:S(2)}, u32[]{:S(2)}) %collective-permute-start.4) | collective-permute-done | bytes 917536 | tf_op jit(solution)/shard_map/ppermute | solution.py:201
  212.4 1.9 collective-permute-start.6
  214.3 1.0 bitcast_dynamic-update-slice_fusion.4
  215.3 1.0 bitcast_dynamic-update-slice_fusion.3
  216.4 16.9 %collective-permute-done.6 = bf16[224,2048]{1,0:T(8,128)(2,1)S(1)} collective-permute-done((bf16[224,2048]{1,0:T(8,128)(2,1)S(1)}, bf16[224,2048]{1,0:T(8,128)(2,1)S(1)}, u32[]{:S(2)}, u32[]{:S(2)}) %collective-permute-start.6) | collective-permute-done | bytes 917536 | tf_op jit(solution)/shard_map/ppermute | solution.py:201
  233.3 1.1 bitcast_dynamic-update-slice_fusion.2
  234.4 1.0 bitcast_dynamic-update-slice_fusion.1.weights
  235.4 7.5 %shard_map.83 = bf16[224,256]{1,0:T(8,128)(2,1)} custom-call(bf16[16,2,8,128,128]{4,3,2,1,0:T(8,128)(2,1)} %bitcast.46, bf16[8,224,2048]{2,1,0:T(8,128)(2,1)} %bitcast_dynamic-update-slice_fusion.1.weights), custom_call_target="tpu_custom_call" | custom-call | tf_op jit(solution)/shard_map/pallas_call | solution.py:208
  (31 shorter events, 1.1 us)
Async XLA Ops:
  6.5 60.9 %copy-start = (bf16[64,2048]{1,0:T(8,128)(2,1)S(1)}, bf16[64,2048]{1,0:T(8,128)(2,1)}, u32[]{:S(2)}) copy-start(bf16[64,2048]{1,0:T(8,128)(2,1)} %param.8) | copy-start | bytes 786436
  10.6 56.2 %all-to-all-start.2 = ((bf16[16,8,640]{2,1,0:T(8,128)(2,1)}), bf16[16,8,640]{2,1,0:T(8,128)(2,1)S(1)}, u32[]{:S(2)}, u32[]{:S(2)}) async-start(bf16[16,8,640]{2,1,0:T(8,128)(2,1)} %broadcast_in_dim.51), calls=%async_computation.2 | async-start | bytes 327680 | tf_op jit(solution)/shard_map/all_to_all | solution.py:138
  54.8 52.4 %all-gather.3.cloned.1.call-start = ((), (), s32[]{:S(2)}) async-start(), calls=%async_computation.4 | async-start | bytes 1474560 | tf_op jit(solution)/shard_map/all_gather | solution.py:141
  66.7 0.7 copy-start.2
  69.3 44.5 %all-to-all-start = ((bf16[16,128,128]{2,1,0:T(8,128)(2,1)}), bf16[16,128,128]{2,1,0:T(8,128)(2,1)S(1)}, u32[]{:S(2)}, u32[]{:S(2)}) async-start(bf16[16,128,128]{2,1,0:T(8,128)(2,1)} %pad_maximum_fusion), calls=%async_computation | async-start | bytes 1048576 | tf_op jit(solution)/shard_map/all_to_all | solution.py:152
  77.1 158.3 %all-gather.5.cloned.1.call-start = ((), (), s32[]{:S(2)}) async-start(), calls=%async_computation.5 | async-start | bytes 8650752 | tf_op jit(solution)/shard_map/all_gather | solution.py:198
  107.2 14.5 %copy-start.1 = (bf16[1024,640]{1,0:T(8,128)(2,1)S(1)}, bf16[1024,640]{1,0:T(8,128)(2,1)}, u32[]{:S(2)}) copy-start(bf16[1024,640]{1,0:T(8,128)(2,1)} %all-gather.3.cloned.1.call-done.own_ref) | copy-start | bytes 3932164
  107.2 14.5 %collective-permute-start = (bf16[1024,640]{1,0:T(8,128)(2,1)}, bf16[1024,640]{1,0:T(8,128)(2,1)S(1)}, u32[]{:S(2)}, u32[]{:S(2)}) collective-permute-start(bf16[1024,640]{1,0:T(8,128)(2,1)} %all-gather.3.cloned.1.call-done.own_ref), channel_id=1, source_target_pairs={{0,8},{8,0},{16,24},{24,16},{32,40},{40,32},{48,56},{56,48},{64,72... | collective-permute-start | bytes 3932168 | tf_op jit(solution)/shard_map/ppermute | solution.py:143
  144.3 23.7 %collective-permute-start.1 = (bf16[224,2048]{1,0:T(8,128)(2,1)}, bf16[224,2048]{1,0:T(8,128)(2,1)S(1)}, u32[]{:S(2)}, u32[]{:S(2)}) collective-permute-start(bf16[224,2048]{1,0:T(8,128)(2,1)} %bitcast.51), channel_id=1, source_target_pairs={{0,1},{1,2},{2,3},{3,4},{4,5},{5,6},{6,7},{7,0},{8,9},{9,10},{10,1... | collective-permute-start | bytes 2752520 | tf_op jit(solution)/shard_map/ppermute | solution.py:179
  146.2 23.7 %collective-permute-start.3 = (bf16[224,2048]{1,0:T(8,128)(2,1)}, bf16[224,2048]{1,0:T(8,128)(2,1)S(1)}, u32[]{:S(2)}, u32[]{:S(2)}) collective-permute-start(bf16[224,2048]{1,0:T(8,128)(2,1)} %bitcast.52), channel_id=1, source_target_pairs={{0,7},{1,0},{2,1},{3,2},{4,3},{5,4},{6,5},{7,6},{8,15},{9,8},{10,9... | collective-permute-start | bytes 2752520 | tf_op jit(solution)/shard_map/ppermute | solution.py:202
  168.0 22.6 %collective-permute-start.2 = (bf16[224,2048]{1,0:T(8,128)(2,1)S(1)}, bf16[224,2048]{1,0:T(8,128)(2,1)S(1)}, u32[]{:S(2)}, u32[]{:S(2)}) collective-permute-start(bf16[224,2048]{1,0:T(8,128)(2,1)S(1)} %collective-permute-done.1), channel_id=1, source_target_pairs={{0,1},{1,2},{2,3},{3,4},{4,5},{5,6},{6,7},{7,0},{8,9},{9,10},{10,1... | collective-permute-start | bytes 2752520 | tf_op jit(solution)/shard_map/ppermute | solution.py:201
  169.9 22.6 %collective-permute-start.5 = (bf16[224,2048]{1,0:T(8,128)(2,1)S(1)}, bf16[224,2048]{1,0:T(8,128)(2,1)S(1)}, u32[]{:S(2)}, u32[]{:S(2)}) collective-permute-start(bf16[224,2048]{1,0:T(8,128)(2,1)S(1)} %collective-permute-done.3), channel_id=1, source_target_pairs={{0,7},{1,0},{2,1},{3,2},{4,3},{5,4},{6,5},{7,6},{8,15},{9,8},{10,9... | collective-permute-start | bytes 2752520 | tf_op jit(solution)/shard_map/ppermute | solution.py:202
  190.6 21.8 %collective-permute-start.4 = (bf16[224,2048]{1,0:T(8,128)(2,1)S(1)}, bf16[224,2048]{1,0:T(8,128)(2,1)S(1)}, u32[]{:S(2)}, u32[]{:S(2)}) collective-permute-start(bf16[224,2048]{1,0:T(8,128)(2,1)S(1)} %collective-permute-done.2), channel_id=1, source_target_pairs={{0,1},{1,2},{2,3},{3,4},{4,5},{5,6},{6,7},{7,0},{8,9},{9,10},{10,1... | collective-permute-start | bytes 2752520 | tf_op jit(solution)/shard_map/ppermute | solution.py:201
  192.5 41.8 %collective-permute-start.7 = (bf16[224,2048]{1,0:T(8,128)(2,1)S(1)}, bf16[224,2048]{1,0:T(8,128)(2,1)S(1)}, u32[]{:S(2)}, u32[]{:S(2)}) collective-permute-start(bf16[224,2048]{1,0:T(8,128)(2,1)S(1)} %collective-permute-done.5), channel_id=1, source_target_pairs={{0,7},{1,0},{2,1},{3,2},{4,3},{5,4},{6,5},{7,6},{8,15},{9,8},{10,9... | collective-permute-start | bytes 2752520 | tf_op jit(solution)/shard_map/ppermute | solution.py:202
  212.4 20.9 %collective-permute-start.6 = (bf16[224,2048]{1,0:T(8,128)(2,1)S(1)}, bf16[224,2048]{1,0:T(8,128)(2,1)S(1)}, u32[]{:S(2)}, u32[]{:S(2)}) collective-permute-start(bf16[224,2048]{1,0:T(8,128)(2,1)S(1)} %collective-permute-done.4), channel_id=1, source_target_pairs={{0,1},{1,2},{2,3},{3,4},{4,5},{5,6},{6,7},{7,0},{8,9},{9,10},{10,1... | collective-permute-start | bytes 2752520 | tf_op jit(solution)/shard_map/ppermute | solution.py:201
Sparse Core Ops, SparseCore 0:
  67.6 39.6 all-gather.2
  144.4 78.6 all-gather.4

commit v6 on v5

--- a/solution.py
+++ b/solution.py
@@ -118,10 +118,9 @@
     assert heads == chips
     nope = tile_rows * ranks
     rope = k_rope.shape[1]
-    v_rows, v_dim = w_uv.shape[1:]
+    _, v_dim = w_uv.shape[1:]
     scale = (nope + rope) ** (-0.5)
     same_core = [[z * CORES + k for z in range(chips)] for k in range(CORES)]
-    one_chip = [[z * CORES + k for k in range(CORES)] for z in range(chips)]
 
     plane = lax.axis_index("tp")
     share = toks // planes
@@ -156,11 +155,12 @@
     q_parts = came[:, :toks].reshape(chips * toks, nope)
     q_rot = came[:, toks:cut]
     q_rot = jnp.concatenate([q_rot[:, :, :rope], q_rot[:, :, rope:]], axis=1).reshape(-1, rope)
-    both = jnp.broadcast_to(came[None, :, cut:], (CORES, chips, k_rows + v_rows, LANES))
-    both = lax.all_to_all(
-        both, "ctx", split_axis=0, concat_axis=0, tiled=True, axis_index_groups=one_chip
-    )
-    both = both.transpose(1, 0, 2, 3)
+    own_up = came[:, cut:]
+    other_up = lax.ppermute(own_up, "ctx", swap)
+    is_first = lax.axis_index("ctx") % CORES == 0
+    both = jnp.stack(
+        [jnp.where(is_first, own_up, other_up), jnp.where(is_first, other_up, own_up)], axis=1
+    )
     up_key = both[:, :, :k_rows].reshape(nope, lat)
     up_value = both[:, :, k_rows:].reshape(lat, v_dim)
     q_lat = jnp.dot(q_parts, up_key, preferred_element_type=jnp.float32).astype(jnp.bfloat16)
@@ -173,12 +173,12 @@
     left = [(i, (i - 1) % planes) for i in range(planes)]
     all_w = jnp.zeros((planes, *own_w.shape), jnp.bfloat16)
 
-    def placed(stack, block, shift):
-        return lax.dynamic_update_slice(stack, block[None], ((plane + shift) % planes, 0, 0))
-
-    lower = lax.ppermute(own_w, "tp", right)
-    all_w = placed(placed(all_w, own_w, 0), lower, planes - 1)
-    upper = own_w
+    part_columns = own_w.shape[0] // 2
+    halves = [own_w[:part_columns], own_w[part_columns:]]
+
+    def placed(stack, block, shift, half):
+        at = ((plane + shift) % planes, half * part_columns, 0)
+        return lax.dynamic_update_slice(stack, block[None], at)
 
     vmem = pl.BlockSpec(memory_space=pltpu.VMEM)
     hbm = pl.BlockSpec(memory_space=pl.ANY)
@@ -197,10 +197,15 @@
     )
     gathered = lax.all_gather(by_plane.reshape(-1, v_dim), "ctx", axis=0)
     gathered = gathered.reshape(chips, CORES, planes, -1, v_dim)
-    for s in range(1, planes // 2):
-        lower = lax.ppermute(lower, "tp", right)
-        upper = lax.ppermute(upper, "tp", left)
-        all_w = placed(placed(all_w, lower, planes - 1 - s), upper, s)
+    for half in range(2):
+        all_w = placed(all_w, halves[half], 0, half)
+    upward, downward = list(halves), list(halves)
+    for s in range(1, planes // 2 + 1):
+        for i in range(2):
+            for half, moving, to, shift in ((i, upward, right, -s), (1 - i, downward, left, s)):
+                if i == 0 or 2 * s < planes:
+                    moving[half] = lax.ppermute(moving[half], "tp", to)
+                    all_w = placed(all_w, moving[half], planes + shift, half)
 
     out_toks = gathered.shape[3] * CORES
     columns = w_out.shape[1]

time: 253 us -> 241 us (0.953)
  waiting for transfers between devices: 94.4 us -> 54 us
  starting transfers between devices: 80.5 us -> 106 us
  local copies, waits for them, and re-layouts: 21.2 us -> 26.4 us
  blocking collectives: 19.1 us -> 15 us
    ppermute x7 -> x15, waiting for transfers between devices: 55.8 us -> 15.5 us  [the longest x14 15.5 us: on_device(): moving[half] = lax.ppermute(moving[half], 'tp', to)]
    ppermute x7 -> x15, starting transfers between devices: 21.8 us -> 46.8 us  [the longest x14 44.8 us: on_device(): moving[half] = lax.ppermute(moving[half], 'tp', to)]
    dynamic_update_slice x8 -> x16, local copies, waits for them, and re-layouts: 9.51 us -> 15.1 us  [placed(): return lax.dynamic_update_slice(stack, block[None], at)]
    all_to_all x1 -> x0, blocking collectives: 3.62 us -> none  [on_device(): lax.all_to_all(both, 'ctx', split_axis=0, concat_axis=0, tiled=True, axis...]
  transfers between devices with their start and end apart: 12 -> 20, of which waited for: 6 -> 5; matrix products, arithmetic and copies ran while one was open for 9% -> 13% of each run, Pallas kernels for 0% -> 0%
where the time goes in v6:
time: 241 us; the launch traced here: 238 us
  starting transfers between devices  106 us (44%)
  waiting for transfers between devices  54 us (22%)
  local copies, waits for them, and re-layouts  26.4 us (11%)
  blocking collectives  15 us (6%)
  Pallas kernels  14.6 us (6%)
  between operations  14 us (6%)
  other arithmetic  6.69 us (3%)
    ppermute x14, starting transfers between devices, on_device(): moving[half] = lax.ppermute(moving[half], 'tp', to)  44.8 us
    all_to_all x1, starting transfers between devices, on_device(): lax.all_to_all(own_keys, 'ctx', split_axis=0, concat_axis=0, tiled=True,...  44.2 us
    all_gather x1, waiting for transfers between devices, on_device(): lax.all_gather(own_keys.reshape(chips * share, -1), 'tp', axis=0, tiled=T...  29 us
    ppermute x14, waiting for transfers between devices, on_device(): moving[half] = lax.ppermute(moving[half], 'tp', to)  15.5 us
    dynamic_update_slice x16, local copies, waits for them, and re-layouts, placed(): return lax.dynamic_update_slice(stack, block[None], at)  15.1 us
    all_to_all x1, blocking collectives, on_device(): lax.all_to_all(head_out.reshape(planes, -1, v_dim), 'tp', split_axis=0, c...  15 us
    all_to_all x1, waiting for transfers between devices, on_device(): lax.all_to_all(own_keys, 'ctx', split_axis=0, concat_axis=0, tiled=True,...  9.38 us
    all_to_all x1, starting transfers between devices, on_device(): lax.all_to_all(sent, 'ctx', split_axis=0, concat_axis=0, tiled=True, axis...  7.81 us
  transfers between devices with their start and end apart: 20, of which 5 were waited for; matrix products, arithmetic and copies ran while one was open for 13% of the time, Pallas kernels for 0%

profile of v6, /device:TPU:65, one launch (start us, length us, event | category | flops | bytes accessed | tf_op | source)
XLA Modules:
  0.0 237.6 jit_solution(658977335802695421)
XLA Ops:
  10.5 44.2 %all-to-all-start.1 = ((bf16[16,8,640]{2,1,0:T(8,128)(2,1)}), bf16[16,8,640]{2,1,0:T(8,128)(2,1)S(1)}, u32[]{:S(2)}, u32[]{:S(2)}) async-start(bf16[16,8,640]{2,1,0:T(8,128)(2,1)} %broadcast_in_dim.68), calls=%async_computation.1 | async-start | bytes 327680 | tf_op jit(solution)/shard_map/all_to_all | solution.py:137
  55.7 1.1 reshape.83
  57.3 9.4 %all-to-all-done.1 = bf16[16,8,640]{2,1,0:T(8,128)(2,1)S(1)} async-done(((bf16[16,8,640]{2,1,0:T(8,128)(2,1)}), bf16[16,8,640]{2,1,0:T(8,128)(2,1)S(1)}, u32[]{:S(2)}, u32[]{:S(2)}) %all-to-all-start.1) | async-done | bytes 163872 | tf_op jit(solution)/shard_map/all_to_all | solution.py:137
  67.5 0.9 reshape.84
  68.4 1.8 pad_maximum_fusion
  70.2 7.8 %all-to-all-start = ((bf16[16,128,128]{2,1,0:T(8,128)(2,1)}), bf16[16,128,128]{2,1,0:T(8,128)(2,1)S(1)}, u32[]{:S(2)}, u32[]{:S(2)}) async-start(bf16[16,128,128]{2,1,0:T(8,128)(2,1)} %pad_maximum_fusion), calls=%async_computation | async-start | bytes 1048576 | tf_op jit(solution)/shard_map/all_to_all | solution.py:151
  78.1 29.0 %all-gather.3.cloned.1.call-done.own_ref = bf16[1024,640]{1,0:T(8,128)(2,1)} async-done(((bf16[128,640]{1,0:T(8,128)(2,1)}), bf16[1024,640]{1,0:T(8,128)(2,1)}) %all-gather.3.cloned.1.call-update) | async-done | bytes 1310736 | tf_op jit(solution)/shard_map/all_gather | solution.py:140
  107.1 6.7 %collective-permute-start.1 = (bf16[1024,640]{1,0:T(8,128)(2,1)}, bf16[1024,640]{1,0:T(8,128)(2,1)S(1)}, u32[]{:S(2)}, u32[]{:S(2)}) collective-permute-start(bf16[1024,640]{1,0:T(8,128)(2,1)} %all-gather.3.cloned.1.call-done.own_ref), channel_id=1, source_target_pairs={{0,8},{8,0},{16,24},{24,16},{32,40},{40,32},{48,56},{56,48},{64,72... | collective-permute-start | bytes 3932168 | tf_op jit(solution)/shard_map/ppermute | solution.py:142
  113.9 2.0 collective-permute-start
  117.6 1.4 convolution_convert_fusion
  119.0 1.3 maximum_maximum_fusion.q_ref
  120.3 7.0 %shard_map.82 = bf16[1024,128]{1,0:T(8,128)(2,1)S(1)} custom-call(bf16[1024,640]{1,0:T(8,128)(2,1)S(1)} %maximum_maximum_fusion.q_ref, bf16[512,128]{1,0:T(8,128)(2,1)S(1)} %bitcast.65, bf16[1024,640]{1,0:T(8,128)(2,1)S(1)} %copy-done.1, bf16[1024,640]{1,0:T(8,128)(2,1)S(1)} %collective-permute-done.1.other_ref), custom_call_target="tpu_custom_call" | custom-call | tf_op jit(solution)/shard_map/pallas_call | solution.py:186
  127.3 15.0 %all_to_all.15 = bf16[8,128,128]{2,1,0:T(8,128)(2,1)} all-to-all(bf16[8,128,128]{2,1,0:T(8,128)(2,1)S(1)} %bitcast.64), channel_id=1, replica_groups=mesh['groups'=2,'ctx'=32,'tp'=8] {'tp'}, dimensions={0} | all-to-all | bytes 524288 | tf_op jit(solution)/shard_map/all_to_all | solution.py:195
  142.4 1.2 fusion.15
  143.6 2.0 collective-permute-start.3
  145.6 3.4 %collective-permute-start.4 = (bf16[112,2048]{1,0:T(8,128)(2,1)S(1)}, bf16[112,2048]{1,0:T(8,128)(2,1)S(1)}, u32[]{:S(2)}, u32[]{:S(2)}) collective-permute-start(bf16[112,2048]{1,0:T(8,128)(2,1)S(1)} %get-tuple-element.7), channel_id=1, source_target_pairs={{0,1},{1,2},{2,3},{3,4},{4,5},{5,6},{6,7},{7,0},{8,9},{9,10},{10,1... | collective-permute-start | bytes 1376264 | tf_op jit(solution)/shard_map/ppermute | solution.py:207
  149.0 2.0 collective-permute-start.2
  150.9 4.8 %collective-permute-start.5 = (bf16[112,2048]{1,0:T(8,128)(2,1)S(1)}, bf16[112,2048]{1,0:T(8,128)(2,1)S(1)}, u32[]{:S(2)}, u32[]{:S(2)}) collective-permute-start(bf16[112,2048]{1,0:T(8,128)(2,1)S(1)} %get-tuple-element.8), channel_id=1, source_target_pairs={{0,7},{1,0},{2,1},{3,2},{4,3},{5,4},{6,5},{7,6},{8,15},{9,8},{10,9... | collective-permute-start | bytes 1376264 | tf_op jit(solution)/shard_map/ppermute | solution.py:207
  155.9 3.9 %broadcast_in_dim.69 = bf16[8,224,2048]{2,1,0:T(8,128)(2,1)} broadcast(bf16[]{:T(256)} %constant.116.clone.1), dimensions={} | broadcast | bytes 7340034 | tf_op jit(solution)/shard_map/broadcast_in_dim | solution.py:174
  159.7 1.9 bitcast_dynamic-update-slice_fusion.15
  161.6 0.8 bitcast_dynamic-update-slice_fusion.14
  162.4 6.3 %collective-permute-done.2 = bf16[112,2048]{1,0:T(8,128)(2,1)} collective-permute-done((bf16[112,2048]{1,0:T(8,128)(2,1)S(1)}, bf16[112,2048]{1,0:T(8,128)(2,1)}, u32[]{:S(2)}, u32[]{:S(2)}) %collective-permute-start.2) | collective-permute-done | bytes 458784 | tf_op jit(solution)/shard_map/ppermute | solution.py:207
  168.7 1.9 collective-permute-start.6
  170.6 4.6 %collective-permute-start.7 = (bf16[112,2048]{1,0:T(8,128)(2,1)S(1)}, bf16[112,2048]{1,0:T(8,128)(2,1)S(1)}, u32[]{:S(2)}, u32[]{:S(2)}) collective-permute-start(bf16[112,2048]{1,0:T(8,128)(2,1)S(1)} %collective-permute-done.3), channel_id=1, source_target_pairs={{0,7},{1,0},{2,1},{3,2},{4,3},{5,4},{6,5},{7,6},{8,15},{9,8},{10,9... | collective-permute-start | bytes 1376264 | tf_op jit(solution)/shard_map/ppermute | solution.py:207
  175.2 2.0 collective-permute-start.8
  177.2 4.6 %collective-permute-start.9 = (bf16[112,2048]{1,0:T(8,128)(2,1)S(1)}, bf16[112,2048]{1,0:T(8,128)(2,1)S(1)}, u32[]{:S(2)}, u32[]{:S(2)}) collective-permute-start(bf16[112,2048]{1,0:T(8,128)(2,1)S(1)} %collective-permute-done.5), channel_id=1, source_target_pairs={{0,7},{1,0},{2,1},{3,2},{4,3},{5,4},{6,5},{7,6},{8,15},{9,8},{10,9... | collective-permute-start | bytes 1376264 | tf_op jit(solution)/shard_map/ppermute | solution.py:207
  181.8 1.9 bitcast_dynamic-update-slice_fusion.13
  183.7 0.8 bitcast_dynamic-update-slice_fusion.12
  184.5 0.8 bitcast_dynamic-update-slice_fusion.11
  185.3 0.8 bitcast_dynamic-update-slice_fusion.10
  186.1 1.9 collective-permute-start.10
  188.1 4.6 %collective-permute-start.11 = (bf16[112,2048]{1,0:T(8,128)(2,1)S(1)}, bf16[112,2048]{1,0:T(8,128)(2,1)S(1)}, u32[]{:S(2)}, u32[]{:S(2)}) collective-permute-start(bf16[112,2048]{1,0:T(8,128)(2,1)S(1)} %collective-permute-done.7), channel_id=1, source_target_pairs={{0,7},{1,0},{2,1},{3,2},{4,3},{5,4},{6,5},{7,6},{8,15},{9,8},{10,9... | collective-permute-start | bytes 1376264 | tf_op jit(solution)/shard_map/ppermute | solution.py:207
  192.7 2.0 collective-permute-start.12
  194.7 4.6 %collective-permute-start.13 = (bf16[112,2048]{1,0:T(8,128)(2,1)S(1)}, bf16[112,2048]{1,0:T(8,128)(2,1)S(1)}, u32[]{:S(2)}, u32[]{:S(2)}) collective-permute-start(bf16[112,2048]{1,0:T(8,128)(2,1)S(1)} %collective-permute-done.9), channel_id=1, source_target_pairs={{0,7},{1,0},{2,1},{3,2},{4,3},{5,4},{6,5},{7,6},{8,15},{9,8},{10,9... | collective-permute-start | bytes 1376264 | tf_op jit(solution)/shard_map/ppermute | solution.py:207
  199.3 0.8 bitcast_dynamic-update-slice_fusion.9
  200.1 0.8 bitcast_dynamic-update-slice_fusion.8
  200.9 0.8 bitcast_dynamic-update-slice_fusion.7
  201.7 0.8 bitcast_dynamic-update-slice_fusion.6
  202.5 1.9 collective-permute-start.14
  204.5 4.6 %collective-permute-start.15 = (bf16[112,2048]{1,0:T(8,128)(2,1)S(1)}, bf16[112,2048]{1,0:T(8,128)(2,1)S(1)}, u32[]{:S(2)}, u32[]{:S(2)}) collective-permute-start(bf16[112,2048]{1,0:T(8,128)(2,1)S(1)} %collective-permute-done.11), channel_id=1, source_target_pairs={{0,7},{1,0},{2,1},{3,2},{4,3},{5,4},{6,5},{7,6},{8,15},{9,8},{10,9... | collective-permute-start | bytes 1376264 | tf_op jit(solution)/shard_map/ppermute | solution.py:207
  209.1 0.8 bitcast_dynamic-update-slice_fusion.5
  209.9 0.8 bitcast_dynamic-update-slice_fusion.4
  210.7 1.0 collective-permute-done.12
  212.5 0.8 bitcast_dynamic-update-slice_fusion.2
  213.3 8.1 %collective-permute-done.14 = bf16[112,2048]{1,0:T(8,128)(2,1)S(1)} collective-permute-done((bf16[112,2048]{1,0:T(8,128)(2,1)S(1)}, bf16[112,2048]{1,0:T(8,128)(2,1)S(1)}, u32[]{:S(2)}, u32[]{:S(2)}) %collective-permute-start.14) | collective-permute-done | bytes 458784 | tf_op jit(solution)/shard_map/ppermute | solution.py:207
  221.4 0.8 bitcast_dynamic-update-slice_fusion.1
  222.3 0.8 bitcast_dynamic-update-slice_fusion.weights
  223.1 7.5 %shard_map.83 = bf16[224,256]{1,0:T(8,128)(2,1)} custom-call(bf16[16,2,8,128,128]{4,3,2,1,0:T(8,128)(2,1)} %bitcast.66, bf16[8,224,2048]{2,1,0:T(8,128)(2,1)} %bitcast_dynamic-update-slice_fusion.weights), custom_call_target="tpu_custom_call" | custom-call | tf_op jit(solution)/shard_map/pallas_call | solution.py:213
  (55 shorter events, 9.0 us)
Async XLA Ops:
  6.5 61.8 %copy-start = (bf16[64,2048]{1,0:T(8,128)(2,1)S(1)}, bf16[64,2048]{1,0:T(8,128)(2,1)}, u32[]{:S(2)}) copy-start(bf16[64,2048]{1,0:T(8,128)(2,1)} %param.8) | copy-start | bytes 786436
  10.5 56.2 %all-to-all-start.1 = ((bf16[16,8,640]{2,1,0:T(8,128)(2,1)}), bf16[16,8,640]{2,1,0:T(8,128)(2,1)S(1)}, u32[]{:S(2)}, u32[]{:S(2)}) async-start(bf16[16,8,640]{2,1,0:T(8,128)(2,1)} %broadcast_in_dim.68), calls=%async_computation.1 | async-start | bytes 327680 | tf_op jit(solution)/shard_map/all_to_all | solution.py:137
  54.8 52.3 %all-gather.3.cloned.1.call-start = ((), (), s32[]{:S(2)}) async-start(), calls=%async_computation.3 | async-start | bytes 1474560 | tf_op jit(solution)/shard_map/all_gather | solution.py:140
  66.7 0.7 copy-start.3
  70.2 43.7 %all-to-all-start = ((bf16[16,128,128]{2,1,0:T(8,128)(2,1)}), bf16[16,128,128]{2,1,0:T(8,128)(2,1)S(1)}, u32[]{:S(2)}, u32[]{:S(2)}) async-start(bf16[16,128,128]{2,1,0:T(8,128)(2,1)} %pad_maximum_fusion), calls=%async_computation | async-start | bytes 1048576 | tf_op jit(solution)/shard_map/all_to_all | solution.py:151
  78.0 145.1 %all-gather.5.cloned.1.call-start = ((), (), s32[]{:S(2)}) async-start(), calls=%async_computation.4 | async-start | bytes 8650752 | tf_op jit(solution)/shard_map/all_gather | solution.py:198
  107.1 13.2 %copy-start.1 = (bf16[1024,640]{1,0:T(8,128)(2,1)S(1)}, bf16[1024,640]{1,0:T(8,128)(2,1)}, u32[]{:S(2)}) copy-start(bf16[1024,640]{1,0:T(8,128)(2,1)} %all-gather.3.cloned.1.call-done.own_ref) | copy-start | bytes 3932164
  107.1 13.1 %collective-permute-start.1 = (bf16[1024,640]{1,0:T(8,128)(2,1)}, bf16[1024,640]{1,0:T(8,128)(2,1)S(1)}, u32[]{:S(2)}, u32[]{:S(2)}) collective-permute-start(bf16[1024,640]{1,0:T(8,128)(2,1)} %all-gather.3.cloned.1.call-done.own_ref), channel_id=1, source_target_pairs={{0,8},{8,0},{16,24},{24,16},{32,40},{40,32},{48,56},{56,48},{64,72... | collective-permute-start | bytes 3932168 | tf_op jit(solution)/shard_map/ppermute | solution.py:142
  113.9 3.6 %collective-permute-start = (bf16[16,32,128]{2,1,0:T(8,128)(2,1)S(1)}, bf16[16,32,128]{2,1,0:T(8,128)(2,1)S(1)}, u32[]{:S(2)}, u32[]{:S(2)}) collective-permute-start(bf16[16,32,128]{2,1,0:T(8,128)(2,1)S(1)} %slice.64), channel_id=1, source_target_pairs={{0,8},{8,0},{16,24},{24,16},{32,40},{40,32},{48,56},{56,48},{64,72... | collective-permute-start | bytes 393224 | tf_op jit(solution)/shard_map/ppermute | solution.py:159
  127.3 34.3 %copy-start.2 = (bf16[2048,224]{0,1:T(8,128)(2,1)S(1)}, bf16[2048,224]{0,1:T(8,128)(2,1)}, u32[]{:S(2)}) copy-start(bf16[2048,224]{0,1:T(8,128)(2,1)} %param.15) | copy-start | bytes 2752516
  143.6 27.0 %collective-permute-start.3 = (bf16[112,2048]{1,0:T(8,128)(2,1)S(1)}, bf16[112,2048]{1,0:T(8,128)(2,1)S(1)}, u32[]{:S(2)}, u32[]{:S(2)}) collective-permute-start(bf16[112,2048]{1,0:T(8,128)(2,1)S(1)} %get-tuple-element.7), channel_id=1, source_target_pairs={{0,7},{1,0},{2,1},{3,2},{4,3},{5,4},{6,5},{7,6},{8,15},{9,8},{10,9... | collective-permute-start | bytes 1376264 | tf_op jit(solution)/shard_map/ppermute | solution.py:207
  145.6 29.6 %collective-permute-start.4 = (bf16[112,2048]{1,0:T(8,128)(2,1)S(1)}, bf16[112,2048]{1,0:T(8,128)(2,1)S(1)}, u32[]{:S(2)}, u32[]{:S(2)}) collective-permute-start(bf16[112,2048]{1,0:T(8,128)(2,1)S(1)} %get-tuple-element.7), channel_id=1, source_target_pairs={{0,1},{1,2},{2,3},{3,4},{4,5},{5,6},{6,7},{7,0},{8,9},{9,10},{10,1... | collective-permute-start | bytes 1376264 | tf_op jit(solution)/shard_map/ppermute | solution.py:207
  149.0 19.7 %collective-permute-start.2 = (bf16[112,2048]{1,0:T(8,128)(2,1)S(1)}, bf16[112,2048]{1,0:T(8,128)(2,1)}, u32[]{:S(2)}, u32[]{:S(2)}) collective-permute-start(bf16[112,2048]{1,0:T(8,128)(2,1)S(1)} %get-tuple-element.8), channel_id=1, source_target_pairs={{0,1},{1,2},{2,3},{3,4},{4,5},{5,6},{6,7},{7,0},{8,9},{9,10},{10,1... | collective-permute-start | bytes 1376264 | tf_op jit(solution)/shard_map/ppermute | solution.py:207
  150.9 26.3 %collective-permute-start.5 = (bf16[112,2048]{1,0:T(8,128)(2,1)S(1)}, bf16[112,2048]{1,0:T(8,128)(2,1)S(1)}, u32[]{:S(2)}, u32[]{:S(2)}) collective-permute-start(bf16[112,2048]{1,0:T(8,128)(2,1)S(1)} %get-tuple-element.8), channel_id=1, source_target_pairs={{0,7},{1,0},{2,1},{3,2},{4,3},{5,4},{6,5},{7,6},{8,15},{9,8},{10,9... | collective-permute-start | bytes 1376264 | tf_op jit(solution)/shard_map/ppermute | solution.py:207
  168.7 17.5 %collective-permute-start.6 = (bf16[112,2048]{1,0:T(8,128)(2,1)}, bf16[112,2048]{1,0:T(8,128)(2,1)S(1)}, u32[]{:S(2)}, u32[]{:S(2)}) collective-permute-start(bf16[112,2048]{1,0:T(8,128)(2,1)} %collective-permute-done.2), channel_id=1, source_target_pairs={{0,1},{1,2},{2,3},{3,4},{4,5},{5,6},{6,7},{7,0},{8,9},{9,10},{10,1... | collective-permute-start | bytes 1376264 | tf_op jit(solution)/shard_map/ppermute | solution.py:207
  170.6 17.4 %collective-permute-start.7 = (bf16[112,2048]{1,0:T(8,128)(2,1)S(1)}, bf16[112,2048]{1,0:T(8,128)(2,1)S(1)}, u32[]{:S(2)}, u32[]{:S(2)}) collective-permute-start(bf16[112,2048]{1,0:T(8,128)(2,1)S(1)} %collective-permute-done.3), channel_id=1, source_target_pairs={{0,7},{1,0},{2,1},{3,2},{4,3},{5,4},{6,5},{7,6},{8,15},{9,8},{10,9... | collective-permute-start | bytes 1376264 | tf_op jit(solution)/shard_map/ppermute | solution.py:207
  175.2 17.4 %collective-permute-start.8 = (bf16[112,2048]{1,0:T(8,128)(2,1)S(1)}, bf16[112,2048]{1,0:T(8,128)(2,1)S(1)}, u32[]{:S(2)}, u32[]{:S(2)}) collective-permute-start(bf16[112,2048]{1,0:T(8,128)(2,1)S(1)} %collective-permute-done.4), channel_id=1, source_target_pairs={{0,1},{1,2},{2,3},{3,4},{4,5},{5,6},{6,7},{7,0},{8,9},{9,10},{10,1... | collective-permute-start | bytes 1376264 | tf_op jit(solution)/shard_map/ppermute | solution.py:207
  177.2 17.4 %collective-permute-start.9 = (bf16[112,2048]{1,0:T(8,128)(2,1)S(1)}, bf16[112,2048]{1,0:T(8,128)(2,1)S(1)}, u32[]{:S(2)}, u32[]{:S(2)}) collective-permute-start(bf16[112,2048]{1,0:T(8,128)(2,1)S(1)} %collective-permute-done.5), channel_id=1, source_target_pairs={{0,7},{1,0},{2,1},{3,2},{4,3},{5,4},{6,5},{7,6},{8,15},{9,8},{10,9... | collective-permute-start | bytes 1376264 | tf_op jit(solution)/shard_map/ppermute | solution.py:207
  186.1 16.4 %collective-permute-start.10 = (bf16[112,2048]{1,0:T(8,128)(2,1)S(1)}, bf16[112,2048]{1,0:T(8,128)(2,1)S(1)}, u32[]{:S(2)}, u32[]{:S(2)}) collective-permute-start(bf16[112,2048]{1,0:T(8,128)(2,1)S(1)} %collective-permute-done.6), channel_id=1, source_target_pairs={{0,1},{1,2},{2,3},{3,4},{4,5},{5,6},{6,7},{7,0},{8,9},{9,10},{10,1... | collective-permute-start | bytes 1376264 | tf_op jit(solution)/shard_map/ppermute | solution.py:207
  188.1 16.4 %collective-permute-start.11 = (bf16[112,2048]{1,0:T(8,128)(2,1)S(1)}, bf16[112,2048]{1,0:T(8,128)(2,1)S(1)}, u32[]{:S(2)}, u32[]{:S(2)}) collective-permute-start(bf16[112,2048]{1,0:T(8,128)(2,1)S(1)} %collective-permute-done.7), channel_id=1, source_target_pairs={{0,7},{1,0},{2,1},{3,2},{4,3},{5,4},{6,5},{7,6},{8,15},{9,8},{10,9... | collective-permute-start | bytes 1376264 | tf_op jit(solution)/shard_map/ppermute | solution.py:207
  192.7 19.0 %collective-permute-start.12 = (bf16[112,2048]{1,0:T(8,128)(2,1)S(1)}, bf16[112,2048]{1,0:T(8,128)(2,1)S(1)}, u32[]{:S(2)}, u32[]{:S(2)}) collective-permute-start(bf16[112,2048]{1,0:T(8,128)(2,1)S(1)} %collective-permute-done.8), channel_id=1, source_target_pairs={{0,1},{1,2},{2,3},{3,4},{4,5},{5,6},{6,7},{7,0},{8,9},{9,10},{10,1... | collective-permute-start | bytes 1376264 | tf_op jit(solution)/shard_map/ppermute | solution.py:207
  194.7 17.8 %collective-permute-start.13 = (bf16[112,2048]{1,0:T(8,128)(2,1)S(1)}, bf16[112,2048]{1,0:T(8,128)(2,1)S(1)}, u32[]{:S(2)}, u32[]{:S(2)}) collective-permute-start(bf16[112,2048]{1,0:T(8,128)(2,1)S(1)} %collective-permute-done.9), channel_id=1, source_target_pairs={{0,7},{1,0},{2,1},{3,2},{4,3},{5,4},{6,5},{7,6},{8,15},{9,8},{10,9... | collective-permute-start | bytes 1376264 | tf_op jit(solution)/shard_map/ppermute | solution.py:207
  202.5 18.9 %collective-permute-start.14 = (bf16[112,2048]{1,0:T(8,128)(2,1)S(1)}, bf16[112,2048]{1,0:T(8,128)(2,1)S(1)}, u32[]{:S(2)}, u32[]{:S(2)}) collective-permute-start(bf16[112,2048]{1,0:T(8,128)(2,1)S(1)} %collective-permute-done.10), channel_id=1, source_target_pairs={{0,1},{1,2},{2,3},{3,4},{4,5},{5,6},{6,7},{7,0},{8,9},{9,10},{10,1... | collective-permute-start | bytes 1376264 | tf_op jit(solution)/shard_map/ppermute | solution.py:207
  204.5 17.8 %collective-permute-start.15 = (bf16[112,2048]{1,0:T(8,128)(2,1)S(1)}, bf16[112,2048]{1,0:T(8,128)(2,1)S(1)}, u32[]{:S(2)}, u32[]{:S(2)}) collective-permute-start(bf16[112,2048]{1,0:T(8,128)(2,1)S(1)} %collective-permute-done.11), channel_id=1, source_target_pairs={{0,7},{1,0},{2,1},{3,2},{4,3},{5,4},{6,5},{7,6},{8,15},{9,8},{10,9... | collective-permute-start | bytes 1376264 | tf_op jit(solution)/shard_map/ppermute | solution.py:207
Sparse Core Ops, SparseCore 0:
  67.6 39.4 all-gather.2
  142.5 79.1 all-gather.4

commit v7 on v5

--- a/solution.py
+++ b/solution.py
@@ -2,6 +2,7 @@
 
 import jax
 import jax.numpy as jnp
+import numpy as np
 from jax import lax
 from jax.experimental import pallas as pl
 from jax.experimental.pallas import tpu as pltpu
@@ -13,10 +14,8 @@
 CORES = 2
 
 
-def cos_sin(position, half_dim):
-    freqs = 10000.0 ** (-jnp.arange(half_dim, dtype=jnp.float32) / half_dim)
-    angles = position.astype(jnp.float32)[..., None] * freqs
-    return jnp.cos(angles), jnp.sin(angles)
+def frequencies(half_dim):
+    return np.power(10000.0, -np.arange(half_dim) / half_dim).astype(np.float32)
 
 
 def rotate(values, cosine, sine):
@@ -27,6 +26,19 @@
         [first_half * cosine - second_half * sine, second_half * cosine + first_half * sine],
         axis=-1,
     )
+
+
+def prepare(chips, share, plane_ref, positions_ref, freqs_ref, c_kv_ref, k_rope_ref, out_ref):
+    at = pl.multiple_of(plane_ref[0] * share, share)
+    position = positions_ref[at] + lax.broadcasted_iota(jnp.int32, (share, 1), 0)
+    angles = position.astype(jnp.float32) * freqs_ref[...]
+    rotated = rotate(k_rope_ref[pl.ds(at, share), :], jnp.cos(angles), jnp.sin(angles))
+    lane = lax.broadcasted_iota(jnp.int32, (share, LANES - rotated.shape[1]), 1)
+    digits = jnp.where(lane == 0, position // DIGIT, jnp.where(lane == 1, position % DIGIT, 0))
+    row = jnp.concatenate([rotated, digits.astype(jnp.float32)], axis=1).astype(jnp.bfloat16)
+    row = jnp.concatenate([c_kv_ref[pl.ds(at, share), :], row], axis=1)
+    for z in range(chips):
+        out_ref[z] = row
 
 
 def attend(chips, planes, toks, lat, scale, block, q_ref, wv_ref, own_ref, other_ref, out_ref, pos_buf):
@@ -126,15 +138,16 @@
     plane = lax.axis_index("tp")
     share = toks // planes
 
-    def cut_share(a):
-        return lax.dynamic_slice_in_dim(a, plane * share, share, 0)
-
-    own_pos = cut_share(positions)
-    k_rot = rotate(cut_share(k_rope), *cos_sin(own_pos, rope // 2)).astype(jnp.bfloat16)
-    digits = jnp.stack([own_pos // DIGIT, own_pos % DIGIT], axis=1).astype(jnp.bfloat16)
-    zeros = jnp.zeros((share, LANES - rope - 2), jnp.bfloat16)
-    own_keys = jnp.concatenate([cut_share(c_kv), k_rot, digits, zeros], axis=1)
-    own_keys = jnp.broadcast_to(own_keys, (chips, *own_keys.shape))
+    assert DIGIT % share == 0
+    vmem = pl.BlockSpec(memory_space=pltpu.VMEM)
+    smem = pl.BlockSpec(memory_space=pltpu.SMEM)
+    freqs = jnp.asarray(frequencies(rope // 2))[None]
+    own_keys = pl.pallas_call(
+        functools.partial(prepare, chips, share),
+        out_shape=jax.ShapeDtypeStruct((chips, share, lat + LANES), jnp.bfloat16),
+        in_specs=[smem, smem, vmem, vmem, vmem],
+        out_specs=vmem,
+    )(plane.astype(jnp.int32).reshape(1), positions, freqs, c_kv, k_rope)
     own_keys = lax.all_to_all(
         own_keys, "ctx", split_axis=0, concat_axis=0, tiled=True, axis_index_groups=same_core
     )
@@ -142,7 +155,8 @@
     swap = [(r, r // CORES * CORES + (r + 1) % CORES) for r in range(ranks)]
     other_keys = lax.ppermute(own_keys, "ctx", swap)
 
-    cosine, sine = cos_sin(positions, rope // 2)
+    angles = positions.astype(jnp.float32)[:, None] * freqs
+    cosine, sine = jnp.cos(angles), jnp.sin(angles)
     q_parts = q_nope.reshape(toks, heads, nope).transpose(1, 0, 2)
     q_rot = rotate(q_rope.reshape(toks, heads, rope), cosine[:, None], sine[:, None])
     q_rot = q_rot.astype(jnp.bfloat16).transpose(1, 0, 2)
@@ -180,7 +194,6 @@
     all_w = placed(placed(all_w, own_w, 0), lower, planes - 1)
     upper = own_w
 
-    vmem = pl.BlockSpec(memory_space=pltpu.VMEM)
     hbm = pl.BlockSpec(memory_space=pl.ANY)
     block = min(256, chips * toks)
     head_out = pl.pallas_call(

time: 253 us -> 251 us (level)
  transfers between devices with their start and end apart: 12 -> 12, of which waited for: 6 -> 6; matrix products, arithmetic and copies ran while one was open for 9% -> 10% of each run, Pallas kernels for 0% -> 0%
where the time goes in v7:
time: 251 us; the launch traced here: 248 us
  waiting for transfers between devices  93.7 us (37%)
  starting transfers between devices  80.5 us (32%)
  blocking collectives  19 us (8%)
  local copies, waits for them, and re-layouts  18.9 us (8%)
  Pallas kernels  16.3 us (6%)
  between operations  13.8 us (5%)
  other arithmetic  3.99 us (2%)
    all_to_all x1, starting transfers between devices, on_device(): lax.all_to_all(own_keys, 'ctx', split_axis=0, concat_axis=0, tiled=True,...  44.2 us
    ppermute x3, waiting for transfers between devices, on_device(): lower = lax.ppermute(lower, 'tp', right)  38.8 us
    all_gather x1, waiting for transfers between devices, on_device(): lax.all_gather(own_keys.reshape(chips * share, -1), 'tp', axis=0, tiled=T...  30 us
    ppermute x1, waiting for transfers between devices, on_device(): lower = lax.ppermute(own_w, 'tp', right)  17 us
    all_to_all x1, blocking collectives, on_device(): lax.all_to_all(head_out.reshape(planes, -1, v_dim), 'tp', split_axis=0, c...  15.4 us
    ppermute x3, starting transfers between devices, on_device(): upper = lax.ppermute(upper, 'tp', left)  14 us
    dynamic_update_slice x8, local copies, waits for them, and re-layouts, placed(): lax.dynamic_update_slice(stack, block[None], ((plane + shift) % planes, 0...  9.54 us
    all_to_all x1, waiting for transfers between devices, on_device(): lax.all_to_all(own_keys, 'ctx', split_axis=0, concat_axis=0, tiled=True,...  7.85 us
  transfers between devices with their start and end apart: 12, of which 6 were waited for; matrix products, arithmetic and copies ran while one was open for 10% of the time, Pallas kernels for 0%

profile of v7, /device:TPU:65, one launch (start us, length us, event | category | flops | bytes accessed | tf_op | source)
XLA Modules:
  0.0 247.6 jit_solution(17804300363902252209)
XLA Ops:
  6.6 1.8 shard_map.91
  8.3 44.2 %all-to-all-start.2 = ((bf16[16,8,640]{2,1,0:T(8,128)(2,1)}), bf16[16,8,640]{2,1,0:T(8,128)(2,1)S(1)}, u32[]{:S(2)}, u32[]{:S(2)}) async-start(bf16[16,8,640]{2,1,0:T(8,128)(2,1)} %shard_map.91), calls=%async_computation.2 | async-start | bytes 327680 | tf_op jit(solution)/shard_map/all_to_all | solution.py:151
  52.6 0.7 convert_element_type.14
  53.3 1.1 reshape.78
  54.4 0.9 reshape.79
  55.3 0.9 multiply_cosine_fusion
  56.1 0.1 fusion.7
  56.3 0.2 fusion.1
  56.5 0.2 maximum_bitcast_fusion
  56.6 7.8 %all-to-all-done.2 = bf16[16,8,640]{2,1,0:T(8,128)(2,1)S(1)} async-done(((bf16[16,8,640]{2,1,0:T(8,128)(2,1)}), bf16[16,8,640]{2,1,0:T(8,128)(2,1)S(1)}, u32[]{:S(2)}, u32[]{:S(2)}) %all-to-all-start.2) | async-done | bytes 163872 | tf_op jit(solution)/shard_map/all_to_all | solution.py:151
  64.5 0.7 copy-done.2
  65.3 1.8 pad_maximum_fusion
  67.1 7.8 %all-to-all-start = ((bf16[16,128,128]{2,1,0:T(8,128)(2,1)}), bf16[16,128,128]{2,1,0:T(8,128)(2,1)S(1)}, u32[]{:S(2)}, u32[]{:S(2)}) async-start(bf16[16,128,128]{2,1,0:T(8,128)(2,1)} %pad_maximum_fusion), calls=%async_computation | async-start | bytes 1048576 | tf_op jit(solution)/shard_map/all_to_all | solution.py:166
  74.9 0.1 all-gather.5.cloned.1.call-start
  75.0 30.0 %all-gather.3.cloned.1.call-done.own_ref = bf16[1024,640]{1,0:T(8,128)(2,1)} async-done(((bf16[128,640]{1,0:T(8,128)(2,1)}), bf16[1024,640]{1,0:T(8,128)(2,1)}) %all-gather.3.cloned.1.call-update) | async-done | bytes 1310736 | tf_op jit(solution)/shard_map/all_gather | solution.py:154
  105.0 6.5 %collective-permute-start = (bf16[1024,640]{1,0:T(8,128)(2,1)}, bf16[1024,640]{1,0:T(8,128)(2,1)S(1)}, u32[]{:S(2)}, u32[]{:S(2)}) collective-permute-start(bf16[1024,640]{1,0:T(8,128)(2,1)} %all-gather.3.cloned.1.call-done.own_ref), channel_id=1, source_target_pairs={{0,8},{8,0},{16,24},{24,16},{32,40},{40,32},{48,56},{56,48},{64,72... | collective-permute-start | bytes 3932168 | tf_op jit(solution)/shard_map/ppermute | solution.py:156
  111.5 0.1 pad.2.clone
  111.7 3.6 %all_to_all.20 = bf16[2,16,32,128]{3,2,1,0:T(8,128)(2,1)S(1)} all-to-all(bf16[2,16,32,128]{3,2,1,0:T(8,128)(2,1)S(1)} %broadcast_in_dim.42), channel_id=1, replica_groups={{0,8},{16,24},{32,40},{48,56},{64,72},{80,88},{96,104},{112,120},{128,1..., dimensions={0} | all-to-all | bytes 524288 | tf_op jit(solution)/shard_map/all_to_all | solution.py:174
  115.3 0.7 fusion.5
  116.0 0.7 reshape.81
  116.7 0.9 copy.24
  117.7 0.1 fusion.4
  117.8 0.1 pad_maximum_fusion.1
  117.8 1.3 convolution_convert_fusion
  119.2 0.3 maximum_maximum_fusion.q_ref
  119.5 7.0 %shard_map.92 = bf16[1024,128]{1,0:T(8,128)(2,1)S(1)} custom-call(bf16[1024,640]{1,0:T(8,128)(2,1)S(1)} %maximum_maximum_fusion.q_ref, bf16[512,128]{1,0:T(8,128)(2,1)S(1)} %bitcast.42, bf16[1024,640]{1,0:T(8,128)(2,1)S(1)} %copy-done.1, bf16[1024,640]{1,0:T(8,128)(2,1)S(1)} %collective-permute-done.other_ref), custom_call_target="tpu_custom_call" | custom-call | tf_op jit(solution)/shard_map/pallas_call | solution.py:199
  126.6 15.4 %all_to_all.21 = bf16[8,128,128]{2,1,0:T(8,128)(2,1)} all-to-all(bf16[8,128,128]{2,1,0:T(8,128)(2,1)S(1)} %bitcast.41), channel_id=1, replica_groups=mesh['groups'=2,'ctx'=32,'tp'=8] {'tp'}, dimensions={0} | all-to-all | bytes 524288 | tf_op jit(solution)/shard_map/all_to_all | solution.py:208
  142.0 2.0 collective-permute-start.1
  144.0 4.6 %collective-permute-start.3 = (bf16[224,2048]{1,0:T(8,128)(2,1)}, bf16[224,2048]{1,0:T(8,128)(2,1)S(1)}, u32[]{:S(2)}, u32[]{:S(2)}) collective-permute-start(bf16[224,2048]{1,0:T(8,128)(2,1)} %bitcast.49), channel_id=1, source_target_pairs={{0,7},{1,0},{2,1},{3,2},{4,3},{5,4},{6,5},{7,6},{8,15},{9,8},{10,9... | collective-permute-start | bytes 2752520 | tf_op jit(solution)/shard_map/ppermute | solution.py:215
  148.7 17.0 %collective-permute-done.1 = bf16[224,2048]{1,0:T(8,128)(2,1)S(1)} collective-permute-done((bf16[224,2048]{1,0:T(8,128)(2,1)}, bf16[224,2048]{1,0:T(8,128)(2,1)S(1)}, u32[]{:S(2)}, u32[]{:S(2)}) %collective-permute-start.1) | collective-permute-done | bytes 917536 | tf_op jit(solution)/shard_map/ppermute | solution.py:193
  165.7 1.9 collective-permute-start.2
  167.6 4.8 %collective-permute-start.5 = (bf16[224,2048]{1,0:T(8,128)(2,1)S(1)}, bf16[224,2048]{1,0:T(8,128)(2,1)S(1)}, u32[]{:S(2)}, u32[]{:S(2)}) collective-permute-start(bf16[224,2048]{1,0:T(8,128)(2,1)S(1)} %collective-permute-done.3), channel_id=1, source_target_pairs={{0,7},{1,0},{2,1},{3,2},{4,3},{5,4},{6,5},{7,6},{8,15},{9,8},{10,9... | collective-permute-start | bytes 2752520 | tf_op jit(solution)/shard_map/ppermute | solution.py:215
  172.4 3.9 %broadcast_in_dim.45 = bf16[8,224,2048]{2,1,0:T(8,128)(2,1)} broadcast(bf16[]{:T(256)} %constant.53.clone.1), dimensions={} | broadcast | bytes 7340034 | tf_op jit(solution)/shard_map/broadcast_in_dim | solution.py:188
  176.3 2.3 bitcast_dynamic-update-slice_fusion
  178.6 1.1 bitcast_dynamic-update-slice_fusion.7
  179.6 8.6 %collective-permute-done.2 = bf16[224,2048]{1,0:T(8,128)(2,1)S(1)} collective-permute-done((bf16[224,2048]{1,0:T(8,128)(2,1)S(1)}, bf16[224,2048]{1,0:T(8,128)(2,1)S(1)}, u32[]{:S(2)}, u32[]{:S(2)}) %collective-permute-start.2) | collective-permute-done | bytes 917536 | tf_op jit(solution)/shard_map/ppermute | solution.py:214
  188.2 1.9 collective-permute-start.4
  190.2 4.6 %collective-permute-start.7 = (bf16[224,2048]{1,0:T(8,128)(2,1)S(1)}, bf16[224,2048]{1,0:T(8,128)(2,1)S(1)}, u32[]{:S(2)}, u32[]{:S(2)}) collective-permute-start(bf16[224,2048]{1,0:T(8,128)(2,1)S(1)} %collective-permute-done.5), channel_id=1, source_target_pairs={{0,7},{1,0},{2,1},{3,2},{4,3},{5,4},{6,5},{7,6},{8,15},{9,8},{10,9... | collective-permute-start | bytes 2752520 | tf_op jit(solution)/shard_map/ppermute | solution.py:215
  194.8 1.0 bitcast_dynamic-update-slice_fusion.6
  195.8 1.0 bitcast_dynamic-update-slice_fusion.5
  196.9 13.2 %collective-permute-done.4 = bf16[224,2048]{1,0:T(8,128)(2,1)S(1)} collective-permute-done((bf16[224,2048]{1,0:T(8,128)(2,1)S(1)}, bf16[224,2048]{1,0:T(8,128)(2,1)S(1)}, u32[]{:S(2)}, u32[]{:S(2)}) %collective-permute-start.4) | collective-permute-done | bytes 917536 | tf_op jit(solution)/shard_map/ppermute | solution.py:214
  210.1 1.9 collective-permute-start.6
  212.0 1.0 bitcast_dynamic-update-slice_fusion.4
  213.0 1.0 bitcast_dynamic-update-slice_fusion.3
  214.0 17.0 %collective-permute-done.6 = bf16[224,2048]{1,0:T(8,128)(2,1)S(1)} collective-permute-done((bf16[224,2048]{1,0:T(8,128)(2,1)S(1)}, bf16[224,2048]{1,0:T(8,128)(2,1)S(1)}, u32[]{:S(2)}, u32[]{:S(2)}) %collective-permute-start.6) | collective-permute-done | bytes 917536 | tf_op jit(solution)/shard_map/ppermute | solution.py:214
  231.0 1.1 bitcast_dynamic-update-slice_fusion.2
  232.1 1.0 bitcast_dynamic-update-slice_fusion.1.weights
  233.1 7.5 %shard_map.93 = bf16[224,256]{1,0:T(8,128)(2,1)} custom-call(bf16[16,2,8,128,128]{4,3,2,1,0:T(8,128)(2,1)} %bitcast.43, bf16[8,224,2048]{2,1,0:T(8,128)(2,1)} %bitcast_dynamic-update-slice_fusion.1.weights), custom_call_target="tpu_custom_call" | custom-call | tf_op jit(solution)/shard_map/pallas_call | solution.py:221
  (21 shorter events, 0.4 us)
Async XLA Ops:
  6.5 58.7 %copy-start = (bf16[64,2048]{1,0:T(8,128)(2,1)S(1)}, bf16[64,2048]{1,0:T(8,128)(2,1)}, u32[]{:S(2)}) copy-start(bf16[64,2048]{1,0:T(8,128)(2,1)} %param.9) | copy-start | bytes 786436
  8.3 56.2 %all-to-all-start.2 = ((bf16[16,8,640]{2,1,0:T(8,128)(2,1)}), bf16[16,8,640]{2,1,0:T(8,128)(2,1)S(1)}, u32[]{:S(2)}, u32[]{:S(2)}) async-start(bf16[16,8,640]{2,1,0:T(8,128)(2,1)} %shard_map.91), calls=%async_computation.2 | async-start | bytes 327680 | tf_op jit(solution)/shard_map/all_to_all | solution.py:151
  52.5 52.4 %all-gather.3.cloned.1.call-start = ((), (), s32[]{:S(2)}) async-start(), calls=%async_computation.4 | async-start | bytes 1474560 | tf_op jit(solution)/shard_map/all_gather | solution.py:154
  64.5 0.7 copy-start.2
  67.1 44.5 %all-to-all-start = ((bf16[16,128,128]{2,1,0:T(8,128)(2,1)}), bf16[16,128,128]{2,1,0:T(8,128)(2,1)S(1)}, u32[]{:S(2)}, u32[]{:S(2)}) async-start(bf16[16,128,128]{2,1,0:T(8,128)(2,1)} %pad_maximum_fusion), calls=%async_computation | async-start | bytes 1048576 | tf_op jit(solution)/shard_map/all_to_all | solution.py:166
  74.9 158.3 %all-gather.5.cloned.1.call-start = ((), (), s32[]{:S(2)}) async-start(), calls=%async_computation.5 | async-start | bytes 8650752 | tf_op jit(solution)/shard_map/all_gather | solution.py:211
  105.0 14.5 %copy-start.1 = (bf16[1024,640]{1,0:T(8,128)(2,1)S(1)}, bf16[1024,640]{1,0:T(8,128)(2,1)}, u32[]{:S(2)}) copy-start(bf16[1024,640]{1,0:T(8,128)(2,1)} %all-gather.3.cloned.1.call-done.own_ref) | copy-start | bytes 3932164
  105.0 14.5 %collective-permute-start = (bf16[1024,640]{1,0:T(8,128)(2,1)}, bf16[1024,640]{1,0:T(8,128)(2,1)S(1)}, u32[]{:S(2)}, u32[]{:S(2)}) collective-permute-start(bf16[1024,640]{1,0:T(8,128)(2,1)} %all-gather.3.cloned.1.call-done.own_ref), channel_id=1, source_target_pairs={{0,8},{8,0},{16,24},{24,16},{32,40},{40,32},{48,56},{56,48},{64,72... | collective-permute-start | bytes 3932168 | tf_op jit(solution)/shard_map/ppermute | solution.py:156
  142.0 23.7 %collective-permute-start.1 = (bf16[224,2048]{1,0:T(8,128)(2,1)}, bf16[224,2048]{1,0:T(8,128)(2,1)S(1)}, u32[]{:S(2)}, u32[]{:S(2)}) collective-permute-start(bf16[224,2048]{1,0:T(8,128)(2,1)} %bitcast.48), channel_id=1, source_target_pairs={{0,1},{1,2},{2,3},{3,4},{4,5},{5,6},{6,7},{7,0},{8,9},{9,10},{10,1... | collective-permute-start | bytes 2752520 | tf_op jit(solution)/shard_map/ppermute | solution.py:193
  144.0 23.6 %collective-permute-start.3 = (bf16[224,2048]{1,0:T(8,128)(2,1)}, bf16[224,2048]{1,0:T(8,128)(2,1)S(1)}, u32[]{:S(2)}, u32[]{:S(2)}) collective-permute-start(bf16[224,2048]{1,0:T(8,128)(2,1)} %bitcast.49), channel_id=1, source_target_pairs={{0,7},{1,0},{2,1},{3,2},{4,3},{5,4},{6,5},{7,6},{8,15},{9,8},{10,9... | collective-permute-start | bytes 2752520 | tf_op jit(solution)/shard_map/ppermute | solution.py:215
  165.7 22.6 %collective-permute-start.2 = (bf16[224,2048]{1,0:T(8,128)(2,1)S(1)}, bf16[224,2048]{1,0:T(8,128)(2,1)S(1)}, u32[]{:S(2)}, u32[]{:S(2)}) collective-permute-start(bf16[224,2048]{1,0:T(8,128)(2,1)S(1)} %collective-permute-done.1), channel_id=1, source_target_pairs={{0,1},{1,2},{2,3},{3,4},{4,5},{5,6},{6,7},{7,0},{8,9},{9,10},{10,1... | collective-permute-start | bytes 2752520 | tf_op jit(solution)/shard_map/ppermute | solution.py:214
  167.6 22.6 %collective-permute-start.5 = (bf16[224,2048]{1,0:T(8,128)(2,1)S(1)}, bf16[224,2048]{1,0:T(8,128)(2,1)S(1)}, u32[]{:S(2)}, u32[]{:S(2)}) collective-permute-start(bf16[224,2048]{1,0:T(8,128)(2,1)S(1)} %collective-permute-done.3), channel_id=1, source_target_pairs={{0,7},{1,0},{2,1},{3,2},{4,3},{5,4},{6,5},{7,6},{8,15},{9,8},{10,9... | collective-permute-start | bytes 2752520 | tf_op jit(solution)/shard_map/ppermute | solution.py:215
  188.2 21.8 %collective-permute-start.4 = (bf16[224,2048]{1,0:T(8,128)(2,1)S(1)}, bf16[224,2048]{1,0:T(8,128)(2,1)S(1)}, u32[]{:S(2)}, u32[]{:S(2)}) collective-permute-start(bf16[224,2048]{1,0:T(8,128)(2,1)S(1)} %collective-permute-done.2), channel_id=1, source_target_pairs={{0,1},{1,2},{2,3},{3,4},{4,5},{5,6},{6,7},{7,0},{8,9},{9,10},{10,1... | collective-permute-start | bytes 2752520 | tf_op jit(solution)/shard_map/ppermute | solution.py:214
  190.2 41.9 %collective-permute-start.7 = (bf16[224,2048]{1,0:T(8,128)(2,1)S(1)}, bf16[224,2048]{1,0:T(8,128)(2,1)S(1)}, u32[]{:S(2)}, u32[]{:S(2)}) collective-permute-start(bf16[224,2048]{1,0:T(8,128)(2,1)S(1)} %collective-permute-done.5), channel_id=1, source_target_pairs={{0,7},{1,0},{2,1},{3,2},{4,3},{5,4},{6,5},{7,6},{8,15},{9,8},{10,9... | collective-permute-start | bytes 2752520 | tf_op jit(solution)/shard_map/ppermute | solution.py:215
  210.1 21.0 %collective-permute-start.6 = (bf16[224,2048]{1,0:T(8,128)(2,1)S(1)}, bf16[224,2048]{1,0:T(8,128)(2,1)S(1)}, u32[]{:S(2)}, u32[]{:S(2)}) collective-permute-start(bf16[224,2048]{1,0:T(8,128)(2,1)S(1)} %collective-permute-done.4), channel_id=1, source_target_pairs={{0,1},{1,2},{2,3},{3,4},{4,5},{5,6},{6,7},{7,0},{8,9},{9,10},{10,1... | collective-permute-start | bytes 2752520 | tf_op jit(solution)/shard_map/ppermute | solution.py:214
Sparse Core Ops, SparseCore 0:
  65.3 39.6 all-gather.2
  142.1 78.7 all-gather.4

commit v8 on v7

--- a/solution.py
+++ b/solution.py
@@ -41,16 +41,17 @@
         out_ref[z] = row
 
 
-def attend(chips, planes, toks, lat, scale, block, q_ref, wv_ref, own_ref, other_ref, out_ref, pos_buf):
+def attend(chips, planes, toks, lat, scale, block, core_ref, q_ref, wv_ref, keys_ref, out_ref, pos_buf):
     share = toks // planes
     half = LANES // 2
     lane = lax.broadcasted_iota(jnp.int32, (LANES, LANES), 1)
     pick = jnp.where(lane == half, float(DIGIT), jnp.where(lane == half + 1, 1.0, 0.0))
     pick = pick.astype(jnp.bfloat16)
     nt = (((1,), (1,)), ((), ()))
-    all_keys = jnp.concatenate([own_ref[...], other_ref[...]], axis=0)
+    all_keys = keys_ref[...].reshape(CORES * chips * toks, lat + LANES)
     key_pos = lax.dot_general(pick[0:8], all_keys[:, lat:], nt, preferred_element_type=jnp.float32)[0:1]
-    own_pos = lax.dot_general(own_ref[:, lat:], pick, nt, preferred_element_type=jnp.float32)
+    own = keys_ref[pl.ds(core_ref[0], 1), :, lat:].reshape(chips * toks, LANES)
+    own_pos = lax.dot_general(own, pick, nt, preferred_element_type=jnp.float32)
     own_pos = own_pos.reshape(planes, chips, share, LANES)
     for x in range(planes):
         pos_buf[:, x] = own_pos[x]
@@ -151,9 +152,14 @@
     own_keys = lax.all_to_all(
         own_keys, "ctx", split_axis=0, concat_axis=0, tiled=True, axis_index_groups=same_core
     )
-    own_keys = lax.all_gather(own_keys.reshape(chips * share, -1), "tp", axis=0, tiled=True)
-    swap = [(r, r // CORES * CORES + (r + 1) % CORES) for r in range(ranks)]
-    other_keys = lax.ppermute(own_keys, "ctx", swap)
+    one_row = [[r * planes + x for r in range(z * CORES, (z + 1) * CORES) for x in range(planes)] for z in range(chips)]
+    keys = lax.all_gather(
+        own_keys.reshape(chips * share, -1),
+        ("ctx", "tp"),
+        axis=0,
+        tiled=True,
+        axis_index_groups=one_row,
+    ).reshape(CORES, chips * toks, -1)
 
     angles = positions.astype(jnp.float32)[:, None] * freqs
     cosine, sine = jnp.cos(angles), jnp.sin(angles)
@@ -195,15 +201,16 @@
     upper = own_w
 
     hbm = pl.BlockSpec(memory_space=pl.ANY)
+    core = (lax.axis_index("ctx") % CORES).astype(jnp.int32).reshape(1)
     block = min(256, chips * toks)
     head_out = pl.pallas_call(
         functools.partial(attend, chips, planes, toks, lat, scale, block),
         out_shape=jax.ShapeDtypeStruct((chips * toks, v_dim), jnp.bfloat16),
-        in_specs=[vmem, vmem, vmem, vmem],
+        in_specs=[smem, vmem, vmem, vmem],
         out_specs=vmem,
         scratch_shapes=[pltpu.VMEM((chips, planes, share, LANES), jnp.float32)],
         compiler_params=pltpu.CompilerParams(vmem_limit_bytes=20 * 2**20),
-    )(queries, up_value, own_keys, other_keys)
+    )(core, queries, up_value, keys)
 
     by_plane = lax.all_to_all(
         head_out.reshape(planes, -1, v_dim), "tp", split_axis=0, concat_axis=0, tiled=True

time: 251 us -> 250 us (level)
  blocking collectives: 19 us -> 86.3 us
  starting transfers between devices: 80.5 us -> 29 us
  waiting for transfers between devices: 93.7 us -> 78.8 us
    all_to_all x0 -> x1, blocking collectives: none -> 56.2 us  [on_device(): lax.all_to_all(own_keys, 'ctx', split_axis=0, concat_axis=0, tiled=True,...]
    all_to_all x1 -> x0, starting transfers between devices: 44.2 us -> none  [on_device(): lax.all_to_all(own_keys, 'ctx', split_axis=0, concat_axis=0, tiled=True,...]
    all_gather x1, waiting for transfers between devices: 30 us -> 0.02 us  [on_device(): lax.all_gather(own_keys.reshape(chips * share, -1), ('ctx', 'tp'), axis=0...]
    all_to_all x1, waiting for transfers between devices: 0.01 us -> 22.2 us  [on_device(): lax.all_to_all(sent, 'ctx', split_axis=0, concat_axis=0, tiled=True, axis...]
    all_to_all x1 -> x0, waiting for transfers between devices: 7.85 us -> none  [on_device(): lax.all_to_all(own_keys, 'ctx', split_axis=0, concat_axis=0, tiled=True,...]
    all_to_all x1, blocking collectives: 3.62 us -> 10.3 us  [on_device(): lax.all_to_all(both, 'ctx', split_axis=0, concat_axis=0, tiled=True, axis...]
    ppermute x1 -> x0, starting transfers between devices: 6.54 us -> none  [on_device(): other_keys = lax.ppermute(own_keys, 'ctx', swap)]
    all_to_all x1, blocking collectives: 15.4 us -> 19.8 us  [on_device(): lax.all_to_all(head_out.reshape(planes, -1, v_dim), 'tp', split_axis=0, c...]
  transfers between devices with their start and end apart: 12 -> 10, of which waited for: 6 -> 5; matrix products, arithmetic and copies ran while one was open for 10% -> 8% of each run, Pallas kernels for 0% -> 0%
where the time goes in v8:
time: 250 us; the launch traced here: 245 us
  blocking collectives  86.3 us (35%)
  waiting for transfers between devices  78.8 us (32%)
  starting transfers between devices  29 us (12%)
  local copies, waits for them, and re-layouts  16.5 us (7%)
  Pallas kernels  16.3 us (7%)
  between operations  13.8 us (6%)
  other arithmetic  3.98 us (2%)
    all_to_all x1, blocking collectives, on_device(): lax.all_to_all(own_keys, 'ctx', split_axis=0, concat_axis=0, tiled=True,...  56.2 us
    ppermute x3, waiting for transfers between devices, on_device(): lower = lax.ppermute(lower, 'tp', right)  39.8 us
    all_to_all x1, waiting for transfers between devices, on_device(): lax.all_to_all(sent, 'ctx', split_axis=0, concat_axis=0, tiled=True, axis...  22.2 us
    all_to_all x1, blocking collectives, on_device(): lax.all_to_all(head_out.reshape(planes, -1, v_dim), 'tp', split_axis=0, c...  19.8 us
    ppermute x1, waiting for transfers between devices, on_device(): lower = lax.ppermute(own_w, 'tp', right)  16.7 us
    ppermute x3, starting transfers between devices, on_device(): upper = lax.ppermute(upper, 'tp', left)  14 us
    all_to_all x1, blocking collectives, on_device(): lax.all_to_all(both, 'ctx', split_axis=0, concat_axis=0, tiled=True, axis...  10.3 us
    dynamic_update_slice x8, local copies, waits for them, and re-layouts, placed(): lax.dynamic_update_slice(stack, block[None], ((plane + shift) % planes, 0...  8.28 us
  transfers between devices with their start and end apart: 10, of which 5 were waited for; matrix products, arithmetic and copies ran while one was open for 8% of the time, Pallas kernels for 0%

profile of v8, /device:TPU:65, one launch (start us, length us, event | category | flops | bytes accessed | tf_op | source)
XLA Modules:
  0.0 245.2 jit_solution(12161322862187199466)
XLA Ops:
  6.6 1.7 shard_map.91
  8.3 56.2 %all_to_all.20 = bf16[16,8,640]{2,1,0:T(8,128)(2,1)} all-to-all(bf16[16,8,640]{2,1,0:T(8,128)(2,1)} %shard_map.91), channel_id=1, replica_groups={{0,16,32,48,64,80,96,112,128,144,160,176,192,208,224,240},{8,24,40,56,7..., dimensions={0} | all-to-all | bytes 327680 | tf_op jit(solution)/shard_map/all_to_all | solution.py:152
  64.5 0.1 all-gather.3.cloned.1.call-update
  64.6 0.7 convert_element_type.14
  65.3 1.1 reshape.85
  66.4 0.9 reshape.86
  67.3 0.9 multiply_cosine_fusion
  68.1 0.1 fusion.7
  68.3 0.2 fusion.1
  68.5 0.2 maximum_bitcast_fusion
  68.7 0.1 bitcast_bitcast_fusion
  68.7 1.7 pad_maximum_fusion
  70.5 7.2 %all-to-all-start = ((bf16[16,128,128]{2,1,0:T(8,128)(2,1)}), bf16[16,128,128]{2,1,0:T(8,128)(2,1)S(1)}, u32[]{:S(2)}, u32[]{:S(2)}) async-start(bf16[16,128,128]{2,1,0:T(8,128)(2,1)} %pad_maximum_fusion), calls=%async_computation | async-start | bytes 1048576 | tf_op jit(solution)/shard_map/all_to_all | solution.py:172
  77.7 0.1 all-gather.5.cloned.1.call-start
  77.8 0.1 pad.2.clone
  77.8 22.2 %all-to-all-done = bf16[16,128,128]{2,1,0:T(8,128)(2,1)S(1)} async-done(((bf16[16,128,128]{2,1,0:T(8,128)(2,1)}), bf16[16,128,128]{2,1,0:T(8,128)(2,1)S(1)}, u32[]{:S(2)}, u32[]{:S(2)}) %all-to-all-start) | async-done | bytes 524320 | tf_op jit(solution)/shard_map/all_to_all | solution.py:172
  100.1 10.3 %all_to_all.21 = bf16[2,16,32,128]{3,2,1,0:T(8,128)(2,1)S(1)} all-to-all(bf16[2,16,32,128]{3,2,1,0:T(8,128)(2,1)S(1)} %broadcast_in_dim.42), channel_id=1, replica_groups={{0,8},{16,24},{32,40},{48,56},{64,72},{80,88},{96,104},{112,120},{128,1..., dimensions={0} | all-to-all | bytes 524288 | tf_op jit(solution)/shard_map/all_to_all | solution.py:180
  110.5 0.1 reshape.88
  110.6 0.1 fusion.4
  110.7 0.1 pad_maximum_fusion.1
  110.8 0.4 convolution_convert_fusion
  111.2 0.3 maximum_maximum_fusion.q_ref
  111.5 0.0 all-gather.3.cloned.1.call-done
  111.6 1.7 copy-done.1
  113.3 7.1 %shard_map.92 = bf16[1024,128]{1,0:T(8,128)(2,1)S(1)} custom-call(s32[1]{0:T(128)} %bitcast.core_ref, bf16[1024,640]{1,0:T(8,128)(2,1)S(1)} %maximum_maximum_fusion.q_ref, bf16[512,128]{1,0:T(8,128)(2,1)S(1)} %bitcast.45, bf16[2,1024,640]{2,1,0:T(8,128)(2,1)S(1)} %bitcast.43), custom_call_target="tpu_custom_call" | custom-call | tf_op jit(solution)/shard_map/pallas_call | solution.py:206
  120.3 19.8 %all_to_all.22 = bf16[8,128,128]{2,1,0:T(8,128)(2,1)} all-to-all(bf16[8,128,128]{2,1,0:T(8,128)(2,1)S(1)} %bitcast.44), channel_id=1, replica_groups=mesh['groups'=2,'ctx'=32,'tp'=8] {'tp'}, dimensions={0} | all-to-all | bytes 524288 | tf_op jit(solution)/shard_map/all_to_all | solution.py:215
  140.1 0.1 all-gather.5.cloned.1.call-update
  140.2 2.0 collective-permute-start
  142.2 4.6 %collective-permute-start.2 = (bf16[224,2048]{1,0:T(8,128)(2,1)S(1)}, bf16[224,2048]{1,0:T(8,128)(2,1)S(1)}, u32[]{:S(2)}, u32[]{:S(2)}) collective-permute-start(bf16[224,2048]{1,0:T(8,128)(2,1)S(1)} %bitcast.52), channel_id=1, source_target_pairs={{0,7},{1,0},{2,1},{3,2},{4,3},{5,4},{6,5},{7,6},{8,15},{9,8},{10,9... | collective-permute-start | bytes 2752520 | tf_op jit(solution)/shard_map/ppermute | solution.py:222
  146.9 16.7 %collective-permute-done = bf16[224,2048]{1,0:T(8,128)(2,1)S(1)} collective-permute-done((bf16[224,2048]{1,0:T(8,128)(2,1)S(1)}, bf16[224,2048]{1,0:T(8,128)(2,1)S(1)}, u32[]{:S(2)}, u32[]{:S(2)}) %collective-permute-start) | collective-permute-done | bytes 917536 | tf_op jit(solution)/shard_map/ppermute | solution.py:199
  163.6 1.9 collective-permute-start.1
  165.5 4.8 %collective-permute-start.4 = (bf16[224,2048]{1,0:T(8,128)(2,1)S(1)}, bf16[224,2048]{1,0:T(8,128)(2,1)S(1)}, u32[]{:S(2)}, u32[]{:S(2)}) collective-permute-start(bf16[224,2048]{1,0:T(8,128)(2,1)S(1)} %collective-permute-done.2), channel_id=1, source_target_pairs={{0,7},{1,0},{2,1},{3,2},{4,3},{5,4},{6,5},{7,6},{8,15},{9,8},{10,9... | collective-permute-start | bytes 2752520 | tf_op jit(solution)/shard_map/ppermute | solution.py:222
  170.3 3.9 %broadcast_in_dim.45 = bf16[8,224,2048]{2,1,0:T(8,128)(2,1)} broadcast(bf16[]{:T(256)} %constant.68.clone.1), dimensions={} | broadcast | bytes 7340034 | tf_op jit(solution)/shard_map/broadcast_in_dim | solution.py:194
  174.2 1.1 bitcast_dynamic-update-slice_fusion
  175.3 1.0 bitcast_dynamic-update-slice_fusion.7
  176.3 9.8 %collective-permute-done.1 = bf16[224,2048]{1,0:T(8,128)(2,1)S(1)} collective-permute-done((bf16[224,2048]{1,0:T(8,128)(2,1)S(1)}, bf16[224,2048]{1,0:T(8,128)(2,1)S(1)}, u32[]{:S(2)}, u32[]{:S(2)}) %collective-permute-start.1) | collective-permute-done | bytes 917536 | tf_op jit(solution)/shard_map/ppermute | solution.py:221
  186.1 1.9 collective-permute-start.3
  188.1 4.6 %collective-permute-start.6 = (bf16[224,2048]{1,0:T(8,128)(2,1)S(1)}, bf16[224,2048]{1,0:T(8,128)(2,1)S(1)}, u32[]{:S(2)}, u32[]{:S(2)}) collective-permute-start(bf16[224,2048]{1,0:T(8,128)(2,1)S(1)} %collective-permute-done.4), channel_id=1, source_target_pairs={{0,7},{1,0},{2,1},{3,2},{4,3},{5,4},{6,5},{7,6},{8,15},{9,8},{10,9... | collective-permute-start | bytes 2752520 | tf_op jit(solution)/shard_map/ppermute | solution.py:222
  192.7 1.0 bitcast_dynamic-update-slice_fusion.6
  193.7 1.0 bitcast_dynamic-update-slice_fusion.5
  194.8 13.1 %collective-permute-done.3 = bf16[224,2048]{1,0:T(8,128)(2,1)S(1)} collective-permute-done((bf16[224,2048]{1,0:T(8,128)(2,1)S(1)}, bf16[224,2048]{1,0:T(8,128)(2,1)S(1)}, u32[]{:S(2)}, u32[]{:S(2)}) %collective-permute-start.3) | collective-permute-done | bytes 917536 | tf_op jit(solution)/shard_map/ppermute | solution.py:221
  207.8 1.9 collective-permute-start.5
  209.8 1.0 bitcast_dynamic-update-slice_fusion.4
  210.8 1.0 bitcast_dynamic-update-slice_fusion.3
  211.8 16.9 %collective-permute-done.5 = bf16[224,2048]{1,0:T(8,128)(2,1)S(1)} collective-permute-done((bf16[224,2048]{1,0:T(8,128)(2,1)S(1)}, bf16[224,2048]{1,0:T(8,128)(2,1)S(1)}, u32[]{:S(2)}, u32[]{:S(2)}) %collective-permute-start.5) | collective-permute-done | bytes 917536 | tf_op jit(solution)/shard_map/ppermute | solution.py:221
  228.7 1.1 bitcast_dynamic-update-slice_fusion.2
  229.8 1.0 bitcast_dynamic-update-slice_fusion.1.weights
  230.8 7.5 %shard_map.93 = bf16[224,256]{1,0:T(8,128)(2,1)} custom-call(bf16[16,2,8,128,128]{4,3,2,1,0:T(8,128)(2,1)} %bitcast.46, bf16[8,224,2048]{2,1,0:T(8,128)(2,1)} %bitcast_dynamic-update-slice_fusion.1.weights), custom_call_target="tpu_custom_call" | custom-call | tf_op jit(solution)/shard_map/pallas_call | solution.py:228
  (18 shorter events, 0.1 us)
Async XLA Ops:
  6.5 62.1 %copy-start = (bf16[64,2048]{1,0:T(8,128)(2,1)S(1)}, bf16[64,2048]{1,0:T(8,128)(2,1)}, u32[]{:S(2)}) copy-start(bf16[64,2048]{1,0:T(8,128)(2,1)} %param.9) | copy-start | bytes 786436
  6.6 105.0 %all-gather.3.cloned.1.call-start = ((), (), s32[]{:S(2)}) async-start(), calls=%async_computation.4 | async-start | bytes 2785280 | tf_op jit(solution)/shard_map/all_gather | solution.py:156
  70.5 69.7 %copy-start.2 = (bf16[2048,224]{0,1:T(8,128)(2,1)S(1)}, bf16[2048,224]{0,1:T(8,128)(2,1)}, u32[]{:S(2)}) copy-start(bf16[2048,224]{0,1:T(8,128)(2,1)} %param.16) | copy-start | bytes 2752516
  70.5 29.6 %all-to-all-start = ((bf16[16,128,128]{2,1,0:T(8,128)(2,1)}), bf16[16,128,128]{2,1,0:T(8,128)(2,1)S(1)}, u32[]{:S(2)}, u32[]{:S(2)}) async-start(bf16[16,128,128]{2,1,0:T(8,128)(2,1)} %pad_maximum_fusion), calls=%async_computation | async-start | bytes 1048576 | tf_op jit(solution)/shard_map/all_to_all | solution.py:172
  77.7 153.1 %all-gather.5.cloned.1.call-start = ((), (), s32[]{:S(2)}) async-start(), calls=%async_computation.5 | async-start | bytes 8650752 | tf_op jit(solution)/shard_map/all_gather | solution.py:218
  111.5 1.7 copy-start.1
  140.2 23.3 %collective-permute-start = (bf16[224,2048]{1,0:T(8,128)(2,1)S(1)}, bf16[224,2048]{1,0:T(8,128)(2,1)S(1)}, u32[]{:S(2)}, u32[]{:S(2)}) collective-permute-start(bf16[224,2048]{1,0:T(8,128)(2,1)S(1)} %bitcast.51), channel_id=1, source_target_pairs={{0,1},{1,2},{2,3},{3,4},{4,5},{5,6},{6,7},{7,0},{8,9},{9,10},{10,1... | collective-permute-start | bytes 2752520 | tf_op jit(solution)/shard_map/ppermute | solution.py:199
  142.2 23.3 %collective-permute-start.2 = (bf16[224,2048]{1,0:T(8,128)(2,1)S(1)}, bf16[224,2048]{1,0:T(8,128)(2,1)S(1)}, u32[]{:S(2)}, u32[]{:S(2)}) collective-permute-start(bf16[224,2048]{1,0:T(8,128)(2,1)S(1)} %bitcast.52), channel_id=1, source_target_pairs={{0,7},{1,0},{2,1},{3,2},{4,3},{5,4},{6,5},{7,6},{8,15},{9,8},{10,9... | collective-permute-start | bytes 2752520 | tf_op jit(solution)/shard_map/ppermute | solution.py:222
  163.6 22.6 %collective-permute-start.1 = (bf16[224,2048]{1,0:T(8,128)(2,1)S(1)}, bf16[224,2048]{1,0:T(8,128)(2,1)S(1)}, u32[]{:S(2)}, u32[]{:S(2)}) collective-permute-start(bf16[224,2048]{1,0:T(8,128)(2,1)S(1)} %collective-permute-done), channel_id=1, source_target_pairs={{0,1},{1,2},{2,3},{3,4},{4,5},{5,6},{6,7},{7,0},{8,9},{9,10},{10,1... | collective-permute-start | bytes 2752520 | tf_op jit(solution)/shard_map/ppermute | solution.py:221
  165.5 22.6 %collective-permute-start.4 = (bf16[224,2048]{1,0:T(8,128)(2,1)S(1)}, bf16[224,2048]{1,0:T(8,128)(2,1)S(1)}, u32[]{:S(2)}, u32[]{:S(2)}) collective-permute-start(bf16[224,2048]{1,0:T(8,128)(2,1)S(1)} %collective-permute-done.2), channel_id=1, source_target_pairs={{0,7},{1,0},{2,1},{3,2},{4,3},{5,4},{6,5},{7,6},{8,15},{9,8},{10,9... | collective-permute-start | bytes 2752520 | tf_op jit(solution)/shard_map/ppermute | solution.py:222
  186.1 21.7 %collective-permute-start.3 = (bf16[224,2048]{1,0:T(8,128)(2,1)S(1)}, bf16[224,2048]{1,0:T(8,128)(2,1)S(1)}, u32[]{:S(2)}, u32[]{:S(2)}) collective-permute-start(bf16[224,2048]{1,0:T(8,128)(2,1)S(1)} %collective-permute-done.1), channel_id=1, source_target_pairs={{0,1},{1,2},{2,3},{3,4},{4,5},{5,6},{6,7},{7,0},{8,9},{9,10},{10,1... | collective-permute-start | bytes 2752520 | tf_op jit(solution)/shard_map/ppermute | solution.py:221
  188.1 41.7 %collective-permute-start.6 = (bf16[224,2048]{1,0:T(8,128)(2,1)S(1)}, bf16[224,2048]{1,0:T(8,128)(2,1)S(1)}, u32[]{:S(2)}, u32[]{:S(2)}) collective-permute-start(bf16[224,2048]{1,0:T(8,128)(2,1)S(1)} %collective-permute-done.4), channel_id=1, source_target_pairs={{0,7},{1,0},{2,1},{3,2},{4,3},{5,4},{6,5},{7,6},{8,15},{9,8},{10,9... | collective-permute-start | bytes 2752520 | tf_op jit(solution)/shard_map/ppermute | solution.py:222
  207.8 20.9 %collective-permute-start.5 = (bf16[224,2048]{1,0:T(8,128)(2,1)S(1)}, bf16[224,2048]{1,0:T(8,128)(2,1)S(1)}, u32[]{:S(2)}, u32[]{:S(2)}) collective-permute-start(bf16[224,2048]{1,0:T(8,128)(2,1)S(1)} %collective-permute-done.3), channel_id=1, source_target_pairs={{0,1},{1,2},{2,3},{3,4},{4,5},{5,6},{6,7},{7,0},{8,9},{9,10},{10,1... | collective-permute-start | bytes 2752520 | tf_op jit(solution)/shard_map/ppermute | solution.py:221
Sparse Core Ops, SparseCore 0:
  64.7 44.8 all-gather.2
  140.3 73.6 all-gather.4
